TPU v7x, 256 devices: a 4x2x16 block of a 4x16x16 slice. The times are simulated.
256 devices in a mesh: groups: 2 (over y), expert: 4 (over x), etp: 32 (over z, core).
Axes of the slice: x: 4, y: 2, z: 16, core: 2. Of those that a mesh axis runs over, the one named last changes fastest.
The devices are a block of a 4x16x16 slice.
Arguments:
- tokens: bfloat16 [1024, 4096], P(('groups', 'expert'), 'etp'), parts along dimension 0, may hold values from -6 to 6
- route_ids: int32 [1024, 2], P(('groups', 'expert')), parts along dimension 0, may hold values from 0 to 3, all different within a row; in each aligned block of 128 rows (0 to 127, 128 to 255, ...) at most 96 rows name the same one
- gate_weights: float32 [1024, 2], P(('groups', 'expert')), parts along dimension 0, may hold values from 0.2 to 1
- w_gate: bfloat16 [4, 4096, 14336], P('expert', None, 'etp'), may hold values from -0.09375 to 0.09375
- w_up: bfloat16 [4, 4096, 14336], P('expert', None, 'etp'), may hold values from -0.09375 to 0.09375
- w_down: bfloat16 [4, 14336, 4096], P('expert', 'etp'), may hold values from -0.09375 to 0.09375
Outputs:
- mixed: bfloat16 [1024, 4096], P(('groups', 'expert'), 'etp'), parts along dimension 0
There are 2 independent parts, one for each index of `groups`. A program takes and returns all parts, laid end to end along the dimension named above; an argument that names none is the same for every part. Nothing has to cross between parts.
Inputs may be any that keep to these rules, and one draw needn't show every extreme that they name: `route_ids`: each row names two different experts. In the rows of one index of expert (128 aligned rows), no expert is named by more than 96 rows, a bound that some block reaches.
All inputs are finite; a program needn't handle non-finite values.
Results may differ from a plain program's by a relative error of at most 0.024.
Values may be sent and summed in bfloat16 or wider, within the bound.
No kernel may reach another device: no remote copies, remote signals or barrier semaphores. Data moves between devices by JAX's collectives and lax.ppermute only.
A program may use at most 64 MiB of HBM per device.

v0:
```python
import jax
import jax.numpy as jnp
from jax import lax
from jax.sharding import Mesh
from jax.sharding import PartitionSpec as P

CAP = 96
ETP = ("etp_0", "etp_1")


def joined_along(tiles, dim):
    shape = list(tiles.shape[1:])
    shape[dim] *= tiles.shape[0]
    return jnp.moveaxis(tiles, 0, dim).reshape(shape)


def all_blocks(shard, axes, order):
    tiles = shard[None]
    for k in order:
        tiles = lax.all_gather(tiles, axes[k], axis=0, tiled=True)
    current = [lax.axis_size(axes[k]) for k in reversed(order)]
    tiles = tiles.reshape(*current, *shard.shape)
    turned = sorted(range(len(order)), key=lambda place: order[len(order) - 1 - place])
    return tiles.transpose(*turned, *range(len(order), tiles.ndim)).reshape(-1, *shard.shape)


def whole_of(shard, axes, order, dim):
    return joined_along(all_blocks(shard, axes, order), dim)


def cut_along(shard, dim, count):
    shape = shard.shape
    tiles = shard.reshape(*shape[:dim], count, shape[dim] // count, *shape[dim + 1 :])
    return jnp.moveaxis(tiles, dim, 0)


def sum_at_owner(shard, axis, dim):
    tiles = cut_along(shard, dim, lax.axis_size(axis))
    arrived = lax.all_to_all(tiles, axis, split_axis=0, concat_axis=0, tiled=True)
    return arrived.astype(jnp.float32).sum(axis=0)


def shards(tokens, route_ids, gate_weights, w_gate, w_up, w_down):
    cycle_size = lax.axis_size("expert")
    token_count, local_width = tokens.shape
    slot_total = cycle_size * CAP
    expert_iota = lax.broadcasted_iota(jnp.int32, (1, 1, cycle_size), 2)
    hit_mask = route_ids[:, :, None] == expert_iota
    routed = jnp.any(hit_mask, axis=1).astype(jnp.int32)
    weighting = jnp.sum(jnp.where(hit_mask, gate_weights[:, :, None], 0.0), axis=1)
    slot_index = jnp.cumsum(routed, axis=0) - 1
    expert_base = lax.broadcasted_iota(jnp.int32, (1, cycle_size), 1) * CAP
    target_slot = jnp.where(routed == 1, expert_base + slot_index, -1)
    slot_iota = lax.broadcasted_iota(jnp.int32, (1, 1, slot_total), 2)
    pick_table = target_slot[:, :, None] == slot_iota
    select_table = jnp.any(pick_table, axis=1).astype(jnp.bfloat16)
    combine_table = jnp.sum(jnp.where(pick_table, weighting[:, :, None], 0.0), axis=1)
    dispatched = jnp.dot(select_table.T, tokens, preferred_element_type=jnp.float32)
    dispatched = dispatched.astype(jnp.bfloat16).reshape(cycle_size, CAP, local_width)
    gate_local = w_gate[0]
    up_local = w_up[0]
    down_local = w_down[0]
    received = lax.all_to_all(dispatched, "expert", split_axis=0, concat_axis=0, tiled=True)
    columns_in = whole_of(received.reshape(slot_total, local_width), ETP, (0, 1), 1)
    gate_sum = jnp.dot(columns_in, gate_local, preferred_element_type=jnp.float32)
    up_sum = jnp.dot(columns_in, up_local, preferred_element_type=jnp.float32)
    hidden = (jax.nn.silu(gate_sum) * up_sum).astype(jnp.bfloat16)
    partial_out = jnp.dot(hidden, down_local, preferred_element_type=jnp.float32).astype(
        jnp.bfloat16
    )
    finished = sum_at_owner(partial_out, ETP, 1).astype(jnp.bfloat16)
    results = lax.all_to_all(
        finished.reshape(cycle_size, CAP, local_width),
        "expert",
        split_axis=0,
        concat_axis=0,
        tiled=True,
    )
    flat_results = results.reshape(slot_total, local_width).astype(jnp.float32)
    mixed = jnp.dot(combine_table, flat_results)
    return mixed.astype(jnp.bfloat16)


def solution(mesh):
    finer = Mesh(
        mesh.devices.reshape(mesh.shape["groups"], mesh.shape["expert"], 16, 2),
        ("groups", "expert", "etp_0", "etp_1"),
    )
    placed = (
        P(("groups", "expert"), ETP),
        P(("groups", "expert"), None),
        P(("groups", "expert"), None),
        P("expert", None, ETP),
        P("expert", None, ETP),
        P("expert", ETP, None),
    )
    return jax.shard_map(
        shards, mesh=finer, in_specs=placed, out_specs=P(("groups", "expert"), ETP), check_vma=False
    )
```

profile of v0, /device:TPU:40, one launch (start us, length us, event | category | flops | bytes accessed | tf_op | source)
XLA Modules:
  0.0 317.1 jit_solution(13523252470046150234)
XLA Ops:
  6.5 0.0 copy-start
  6.6 0.0 all-gather.3.cloned.1.call-start
  6.6 0.7 fusion.18
  7.3 0.1 copy.29
  7.4 0.2 reduce_window_sum.11
  7.6 0.1 copy.30
  7.6 0.1 add_select_fusion
  7.7 0.2 fusion.14
  7.9 0.0 copy-done
  7.9 0.3 convolution_convert_fusion.1
  8.1 10.3 %all_to_all.15 = bf16[4,96,128]{2,1,0:T(8,128)(2,1)} all-to-all(bf16[4,96,128]{2,1,0:T(8,128)(2,1)S(1)} %bitcast.49), channel_id=1, replica_groups=mesh['groups'=2,'expert'=4,'etp_0'=16,'etp_1'=2] {'expert'}, dimensions={0} | all-to-all | bytes 196608 | tf_op jit(solution)/shard_map/all_to_all | solution.py:63
  18.4 0.1 all-gather.3.cloned.1.call-update
  18.5 0.1 all-gather.5.cloned.1.call-start
  18.6 81.5 %all-gather.3.cloned.1.call-done = bf16[16,384,128]{2,1,0:T(8,128)(2,1)} async-done(((bf16[1,384,128]{2,1,0:T(8,128)(2,1)}), bf16[16,384,128]{2,1,0:T(8,128)(2,1)}) %all-gather.3.cloned.1.call-update) | async-done | bytes 1572880 | tf_op jit(solution)/shard_map/all_gather | solution.py:20
  100.0 0.1 all-gather.5.cloned.1.call-update
  100.1 19.5 %all-gather.5.cloned.1.call-done = bf16[32,384,128]{2,1,0:T(8,128)(2,1)} async-done(((bf16[16,384,128]{2,1,0:T(8,128)(2,1)}), bf16[32,384,128]{2,1,0:T(8,128)(2,1)}) %all-gather.5.cloned.1.call-update) | async-done | bytes 3145744 | tf_op jit(solution)/shard_map/all_gather | solution.py:20
  119.6 2.1 copy.31
  121.7 2.8 copy.32
  124.5 0.0 copy-start.1
  124.5 6.0 %fusion.3 = f32[384,448]{0,1:T(8,128)} fusion(bf16[384,4096]{0,1:T(8,128)(2,1)} %bitcast.45, bf16[1,4096,448]{1,2,0:T(8,128)(2,1)} %param.9), kind=kOutput, calls=%fused_computation.4 | convolution fusion | flops 1409286144 | bytes 7503872 | tf_op jit(solution)/shard_map/dot_general | solution.py:65
  130.6 0.0 copy-done.1
  130.6 8.9 %fusion.5 = bf16[48,32,8,128]{3,2,1,0:T(8,128)(2,1)} fusion(bf16[1,448,4096]{2,1,0:T(8,128)(2,1)} %param.11, bf16[384,4096]{0,1:T(8,128)(2,1)S(1)} %bitcast.46, bf16[1,4096,448]{1,2,0:T(8,128)(2,1)} %param.10, f32[384,448]{0,1:T(8,128)} %fusion.3), kind=kOutput, calls=%fused_computation.7 | convolution fusion | flops 2821177344 | bytes 14319616 | tf_op jit(solution)/shard_map/dot_general | solution.py:68
  139.5 4.5 %copy.36 = bf16[48,32,8,128]{3,2,0,1:T(8,128)(2,1)} copy(bf16[48,32,8,128]{3,2,1,0:T(8,128)(2,1)} %fusion.5) | data formatting | bytes 6291456 | tf_op jit(solution)/shard_map/reshape | solution.py:33
  143.9 0.0 copy-start.2
  143.9 0.0 copy-start.3
  143.9 13.3 %all-to-all-start.1 = ((bf16[32,384,128]{2,1,0:T(8,128)(2,1)}), bf16[32,384,128]{2,1,0:T(8,128)(2,1)S(1)}, u32[]{:S(2)}, u32[]{:S(2)}) async-start(bf16[32,384,128]{2,1,0:T(8,128)(2,1)} %bitcast.42), calls=%async_computation.1 | async-start | bytes 6291456 | tf_op jit(solution)/shard_map/all_to_all | solution.py:39
  157.2 0.0 copy-done.2
  157.2 0.0 copy-done.3
  157.2 141.1 %all-to-all-done.1 = bf16[32,384,128]{2,1,0:T(8,128)(2,1)S(1)} async-done(((bf16[32,384,128]{2,1,0:T(8,128)(2,1)}), bf16[32,384,128]{2,1,0:T(8,128)(2,1)S(1)}, u32[]{:S(2)}, u32[]{:S(2)}) %all-to-all-start.1) | async-done | bytes 3145760 | tf_op jit(solution)/shard_map/all_to_all | solution.py:39
  298.4 1.1 reduce_sum.32
  299.4 4.3 %all-to-all-start.2 = ((bf16[4,96,128]{2,1,0:T(8,128)(2,1)}), bf16[4,96,128]{2,1,0:T(8,128)(2,1)S(1)}, u32[]{:S(2)}, u32[]{:S(2)}) async-start(bf16[4,96,128]{2,1,0:T(8,128)(2,1)} %bitcast.11), calls=%async_computation.2 | async-start | bytes 196608 | tf_op jit(solution)/shard_map/all_to_all | solution.py:72
  303.7 0.2 select_reduce_fusion
  303.9 5.6 %all-to-all-done.2 = bf16[4,96,128]{2,1,0:T(8,128)(2,1)S(1)} async-done(((bf16[4,96,128]{2,1,0:T(8,128)(2,1)}), bf16[4,96,128]{2,1,0:T(8,128)(2,1)S(1)}, u32[]{:S(2)}, u32[]{:S(2)}) %all-to-all-start.2) | async-done | bytes 98336 | tf_op jit(solution)/shard_map/all_to_all | solution.py:72
  309.5 0.8 fusion.20
  (3 shorter events, 0.0 us)
Async XLA Ops:
  6.5 1.3 copy-start
  6.6 93.5 %all-gather.3.cloned.1.call-start = ((), (), s32[]{:S(2)}) async-start(), calls=%async_computation.3 | async-start | bytes 1671168 | tf_op jit(solution)/shard_map/all_gather | solution.py:20
  18.5 101.1 %all-gather.5.cloned.1.call-start = ((), (), s32[]{:S(2)}) async-start(), calls=%async_computation.4 | async-start | bytes 4718592 | tf_op jit(solution)/shard_map/all_gather | solution.py:20
  124.5 6.0 %copy-start.1 = (bf16[384,32,128]{0,2,1:T(8,128)(2,1)S(1)}, bf16[384,32,128]{0,2,1:T(8,128)(2,1)}, u32[]{:S(2)}) copy-start(bf16[384,32,128]{0,2,1:T(8,128)(2,1)} %copy.32) | copy-start | bytes 9437188
  143.9 13.3 %copy-start.2 = (f32[128,2]{0,1:T(2,128)S(1)}, f32[128,2]{0,1:T(2,128)}, u32[]{:S(2)}) copy-start(f32[128,2]{0,1:T(2,128)} %param.8) | copy-start | bytes 3076
  143.9 13.3 %copy-start.3 = (s32[128,2]{0,1:T(2,128)S(1)}, s32[128,2]{0,1:T(2,128)}, u32[]{:S(2)}) copy-start(s32[128,2]{0,1:T(2,128)} %param.7) | copy-start | bytes 3076
  143.9 154.4 %all-to-all-start.1 = ((bf16[32,384,128]{2,1,0:T(8,128)(2,1)}), bf16[32,384,128]{2,1,0:T(8,128)(2,1)S(1)}, u32[]{:S(2)}, u32[]{:S(2)}) async-start(bf16[32,384,128]{2,1,0:T(8,128)(2,1)} %bitcast.42), calls=%async_computation.1 | async-start | bytes 6291456 | tf_op jit(solution)/shard_map/all_to_all | solution.py:39
  299.4 10.1 %all-to-all-start.2 = ((bf16[4,96,128]{2,1,0:T(8,128)(2,1)}), bf16[4,96,128]{2,1,0:T(8,128)(2,1)S(1)}, u32[]{:S(2)}, u32[]{:S(2)}) async-start(bf16[4,96,128]{2,1,0:T(8,128)(2,1)} %bitcast.11), calls=%async_computation.2 | async-start | bytes 196608 | tf_op jit(solution)/shard_map/all_to_all | solution.py:72
Sparse Core Ops, SparseCore 0:
  18.6 81.3 all-gather.2
  101.8 17.7 all-gather.4
where the time goes:
time: 321 us; the launch traced here: 317 us
  waiting for transfers between devices  248 us (77%)
  starting transfers between devices  17.6 us (5%)
  matrix products  16 us (5%)
  between operations  13.5 us (4%)
  blocking collectives  10.3 us (3%)
  local copies, waits for them, and re-layouts  9.57 us (3%)
    all_to_all x1, waiting for transfers between devices, sum_at_owner(): lax.all_to_all(tiles, axis, split_axis=0, concat_axis=0, tiled=True)  141 us
    all_gather x2, waiting for transfers between devices, all_blocks(): tiles = lax.all_gather(tiles, axes[k], axis=0, tiled=True)  101 us
    all_to_all x1, starting transfers between devices, sum_at_owner(): lax.all_to_all(tiles, axis, split_axis=0, concat_axis=0, tiled=True)  13.3 us
    all_to_all x1, blocking collectives, shards(): lax.all_to_all(dispatched, 'expert', split_axis=0, concat_axis=0, tiled=T...  10.3 us
    dot_general x1, matrix products, shards(): jnp.dot(hidden, down_local, preferred_element_type=jnp.float32)  8.87 us
  transfers between devices with their start and end apart: 4, of which 4 were waited for; matrix products, arithmetic and copies ran while one was open for 0% of the time, Pallas kernels for 0%

commit v1 on v0

v1 whole, which is shorter than its diff:
```python
import functools

import jax
import jax.numpy as jnp
from jax import lax
from jax.experimental import pallas as pl
from jax.experimental.pallas import tpu as pltpu
from jax.sharding import Mesh
from jax.sharding import PartitionSpec as P

CAP = 96
CORES = 2
ETP = ("etp_0", "etp_1")
LANES = 128
CHUNKS = 4

VMEM = pl.BlockSpec(memory_space=pltpu.VMEM)
SMEM = pl.BlockSpec(memory_space=pltpu.SMEM)
ANY = pl.BlockSpec(memory_space=pl.ANY)


def dot32(a, b):
    return jnp.dot(a, b, preferred_element_type=jnp.float32)


def columns_of(ref, start, count):
    groups, _, rows, lanes = ref.shape
    parts = [ref[:, z].reshape(groups * rows, lanes) for z in range(start, start + count)]
    return jnp.concatenate(parts, axis=1)


def dispatch_body(table_ref, tokens_ref, out_ref):
    experts, chips, cap, lanes = out_ref.shape
    table = table_ref[...]
    for z in range(0, chips, 2):
        pair = jnp.concatenate([tokens_ref[z], tokens_ref[z + 1]], axis=1)
        rows = dot32(table, pair).astype(out_ref.dtype)
        for k in range(2):
            out_ref[:, z + k] = rows[:, k * lanes : (k + 1) * lanes].reshape(experts, cap, lanes)


def weight_copies(core, w_refs, bufs, sems):
    chips = bufs[0].shape[0]
    step = chips // CHUNKS
    return [
        [
            pltpu.make_async_copy(
                w.at[pl.ds(k * step, step), core], buf.at[pl.ds(k * step, step)], sems.at[i, k]
            )
            for i, (w, buf) in enumerate(zip(w_refs, bufs))
        ]
        for k in range(CHUNKS)
    ]


def up_partial(copies, x_ref, bufs, emit):
    chips, lanes, width = bufs[0].shape
    step = chips // CHUNKS
    for k in range(CHUNKS):
        for copy in copies[k]:
            copy.wait()
        x = columns_of(x_ref, k * step, step)
        emit(k, [dot32(x, buf[k * step : (k + 1) * step].reshape(step * lanes, width)) for buf in bufs])


def first_half_body(core_ref, x_ref, wg_ref, wu_ref, gate_ref, up_ref, g_buf, u_buf, sems):
    copies = weight_copies(core_ref[0], (wg_ref, wu_ref), (g_buf, u_buf), sems)
    for chunk in copies:
        for copy in chunk:
            copy.start()

    def emit(k, sums):
        for ref, value in zip((gate_ref, up_ref), sums):
            ref[...] = value if k == 0 else ref[...] + value

    up_partial(copies, x_ref, (g_buf, u_buf), emit)


def down_copies(core, wd_ref, d_buf, sem):
    chips = d_buf.shape[1] // LANES
    return [
        pltpu.make_async_copy(
            wd_ref.at[:, pl.ds(pl.multiple_of((z * CORES + core) * LANES, LANES), LANES)],
            d_buf.at[:, pl.ds(z * LANES, LANES)],
            sem.at[z],
        )
        for z in range(chips)
    ]


def down_into(copies, hidden, d_buf, out_ref):
    blocks, chips, cap, lanes = out_ref.shape
    step = chips // CHUNKS
    for k in range(CHUNKS):
        for copy in copies[k * step : (k + 1) * step]:
            copy.wait()
        part = dot32(hidden, d_buf[:, k * step * lanes : (k + 1) * step * lanes]).astype(out_ref.dtype)
        for z in range(step):
            out_ref[:, k * step + z] = part[:, z * lanes : (z + 1) * lanes].reshape(blocks, cap, lanes)


def second_half_body(
    core_ref, x_ref, gate_ref, up_ref, wg_ref, wu_ref, wd_ref, hidden_ref, out_ref, g_buf, u_buf, d_buf, g_acc, u_acc, sems, d_sem
):
    other = 1 - core_ref[0]
    copies = weight_copies(other, (wg_ref, wu_ref), (g_buf, u_buf), sems)
    downs = down_copies(other, wd_ref, d_buf, d_sem)
    for chunk in copies:
        for copy in chunk:
            copy.start()
    for copy in downs:
        copy.start()

    def emit(k, sums):
        for ref, base, value in zip((g_acc, u_acc), (gate_ref, up_ref), sums):
            ref[...] = (base if k == 0 else ref)[...] + value

    up_partial(copies, x_ref, (g_buf, u_buf), emit)
    gate = g_acc[...]
    hidden = (gate / (1.0 + jnp.exp(-gate)) * u_acc[...]).astype(jnp.bfloat16)
    hidden_ref[...] = hidden
    down_into(downs, hidden, d_buf, out_ref)


def own_down_body(core_ref, hidden_ref, wd_ref, out_ref, d_buf, d_sem):
    downs = down_copies(core_ref[0], wd_ref, d_buf, d_sem)
    for copy in downs:
        copy.start()
    down_into(downs, hidden_ref[...], d_buf, out_ref)


def combine_body(table_ref, results_ref, out_ref):
    chips, _, lanes = out_ref.shape
    table = table_ref[...]
    for z in range(0, chips, 2):
        rows = dot32(table, columns_of(results_ref, z, 2)).astype(out_ref.dtype)
        for k in range(2):
            out_ref[z + k] = rows[:, k * lanes : (k + 1) * lanes]


def call(body, out_shape, in_specs, scratch=(), flops=0):
    outs = jax.tree.map(lambda _: VMEM, out_shape)
    return pl.pallas_call(
        body,
        out_shape=out_shape,
        in_specs=list(in_specs),
        out_specs=outs,
        scratch_shapes=list(scratch),
        cost_estimate=pl.CostEstimate(flops=flops, transcendentals=0, bytes_accessed=flops // 400),
        compiler_params=pltpu.CompilerParams(vmem_limit_bytes=40 * 1024 * 1024),
    )


def shards(tokens, route_ids, gate_weights, w_gate, w_up, w_down):
    experts = lax.axis_size("expert")
    chips = lax.axis_size("etp_0")
    token_count, lanes = tokens.shape
    slots = experts * CAP
    _, width_in, width = w_gate.shape
    bf16, f32 = jnp.bfloat16, jnp.float32
    shape = jax.ShapeDtypeStruct

    expert_iota = lax.broadcasted_iota(jnp.int32, (1, 1, experts), 2)
    hit_mask = route_ids[:, :, None] == expert_iota
    routed = jnp.any(hit_mask, axis=1).astype(jnp.int32)
    weighting = jnp.sum(jnp.where(hit_mask, gate_weights[:, :, None], 0.0), axis=1)
    slot_index = jnp.cumsum(routed, axis=0) - 1
    expert_base = lax.broadcasted_iota(jnp.int32, (1, experts), 1) * CAP
    target_slot = jnp.where(routed == 1, expert_base + slot_index, -1)
    slot_iota = lax.broadcasted_iota(jnp.int32, (1, 1, slots), 2)
    pick_table = target_slot[:, :, None] == slot_iota
    select_table = jnp.any(pick_table, axis=1).astype(bf16).T
    combine_table = jnp.sum(jnp.where(pick_table, weighting[:, :, None], 0.0), axis=1).astype(bf16)

    core = lax.axis_index("etp_1").astype(jnp.int32).reshape(1)
    swap = functools.partial(lax.ppermute, axis_name="etp_1", perm=[(0, 1), (1, 0)])
    exchange = functools.partial(lax.all_to_all, split_axis=0, concat_axis=0, tiled=True)

    gathered = lax.all_gather(tokens, "etp_0", axis=0, tiled=False)
    sent = call(
        dispatch_body, shape((experts, chips, CAP, lanes), bf16), (VMEM, VMEM), flops=2 * slots * token_count * chips * lanes
    )(select_table, gathered)
    own = exchange(sent, "expert")
    other = swap(own)

    gate_rows = w_gate.reshape(chips, CORES, lanes, width)
    up_rows = w_up.reshape(chips, CORES, lanes, width)
    down_rows = w_down[0]
    up_flops = 2 * slots * width * width_in
    w_bufs = [pltpu.VMEM((chips, lanes, width), bf16)] * 2
    w_sems = pltpu.SemaphoreType.DMA((2, CHUNKS))
    d_buf = pltpu.VMEM((width, chips * lanes), bf16)
    d_sem = pltpu.SemaphoreType.DMA((chips,))
    acc = shape((slots, width), f32)
    gate_half, up_half = call(
        first_half_body, (acc, acc), (SMEM, VMEM, ANY, ANY), [*w_bufs, w_sems], flops=up_flops
    )(core, own, gate_rows, up_rows)
    hidden, theirs = call(
        second_half_body,
        (shape((slots, width), bf16), shape((experts, chips, CAP, lanes), bf16)),
        (SMEM, VMEM, VMEM, VMEM, ANY, ANY, ANY),
        [*w_bufs, d_buf, pltpu.VMEM((slots, width), f32), pltpu.VMEM((slots, width), f32), w_sems, d_sem],
        flops=up_flops * 3 // 2,
    )(core, other, gate_half, up_half, gate_rows, up_rows, down_rows)
    arrived = swap(theirs)
    mine = call(
        own_down_body, shape((experts, chips, CAP, lanes), f32), (SMEM, VMEM, ANY), [d_buf, d_sem], flops=up_flops // 2
    )(core, hidden, down_rows)
    chip_sum = (mine + arrived.astype(f32)).astype(bf16)
    results = exchange(chip_sum, "expert")
    blended = call(
        combine_body, shape((chips, token_count, lanes), bf16), (VMEM, VMEM), flops=2 * slots * token_count * chips * lanes
    )(combine_table, results)
    pieces = exchange(blended, "etp_0")
    return pieces.astype(f32).sum(axis=0).astype(bf16)


def solution(mesh):
    groups, experts, etp = (mesh.shape[name] for name in ("groups", "expert", "etp"))
    finer = Mesh(
        mesh.devices.reshape(groups, experts, etp // CORES, CORES),
        ("groups", "expert", "etp_0", "etp_1"),
    )
    placed = (
        P(("groups", "expert"), ETP),
        P(("groups", "expert"), None),
        P(("groups", "expert"), None),
        P("expert", None, ETP),
        P("expert", None, ETP),
        P("expert", ETP, None),
    )
    return jax.shard_map(
        shards, mesh=finer, in_specs=placed, out_specs=P(("groups", "expert"), ETP), check_vma=False
    )
```

time: 321 us -> 162 us (0.50)
  waiting for transfers between devices: 248 us -> 22 us
  blocking collectives: 10.3 us -> 102 us
  matrix products: 16 us -> 0 us
  between operations: 13.5 us -> 0.12 us
  starting transfers between devices: 17.6 us -> 4.41 us
  Pallas kernels: 0 us -> 11 us
  local copies, waits for them, and re-layouts: 9.57 us -> 18.2 us
    all_to_all x2 -> x1, waiting for transfers between devices: 147 us -> 21.2 us  [shards(): results = exchange(chip_sum, 'expert')]
    all_gather x2 -> x0, waiting for transfers between devices: 101 us -> none  [all_blocks(): tiles = lax.all_gather(tiles, axes[k], axis=0, tiled=True)]
    all_gather x0 -> x1, blocking collectives: none -> 51.6 us  [shards(): gathered = lax.all_gather(tokens, 'etp_0', axis=0, tiled=False)]
    all_to_all x1 -> x2, blocking collectives: 10.3 us -> 50.1 us  [the longest x1 31.9 us: shards(): pieces = exchange(blended, 'etp_0')]
    unnamed x8 -> x14, local copies, waits for them, and re-layouts: 0.02 us -> 17.9 us
    dot_general x4 -> x0, matrix products: 16 us -> none  [the longest x1 8.87 us: shards(): jnp.dot(hidden, down_local, preferred_element_type=jnp.float32)]
    all_to_all x2 -> x1, starting transfers between devices: 17.5 us -> 3.78 us  [shards(): results = exchange(chip_sum, 'expert')]
    pallas_call x0 -> x5, Pallas kernels: none -> 11 us  [the longest x1 5.19 us: shards(): call(second_half_body, (shape((slots, width), bf16), shape((experts, chip...]
  transfers between devices with their start and end apart: 4 -> 3, of which waited for: 4 -> 2; matrix products, arithmetic and copies ran while one was open for 0% -> 8% of each run, Pallas kernels for 0% -> 3%
where the time goes in v1:
time: 162 us; the launch traced here: 161 us
  blocking collectives  102 us (63%)
  waiting for transfers between devices  22 us (14%)
  local copies, waits for them, and re-layouts  18.2 us (11%)
  Pallas kernels  11 us (7%)
  starting transfers between devices  4.41 us (3%)
  other arithmetic  3.64 us (2%)
    all_gather x1, blocking collectives, shards(): gathered = lax.all_gather(tokens, 'etp_0', axis=0, tiled=False)  51.6 us
    all_to_all x1, blocking collectives, shards(): pieces = exchange(blended, 'etp_0')  31.9 us
    all_to_all x1, waiting for transfers between devices, shards(): results = exchange(chip_sum, 'expert')  21.2 us
    all_to_all x1, blocking collectives, shards(): own = exchange(sent, 'expert')  18.2 us
    unnamed x14, local copies, waits for them, and re-layouts  17.9 us
    pallas_call x1, Pallas kernels, shards(): call(second_half_body, (shape((slots, width), bf16), shape((experts, chip...  5.19 us
    all_to_all x1, starting transfers between devices, shards(): results = exchange(chip_sum, 'expert')  3.78 us
  transfers between devices with their start and end apart: 3, of which 2 were waited for; matrix products, arithmetic and copies ran while one was open for 8% of the time, Pallas kernels for 3%

profile of v1, /device:TPU:40, one launch (start us, length us, event | category | flops | bytes accessed | tf_op | source)
XLA Modules:
  0.0 161.1 jit_solution(9914284270718780827)
XLA Ops:
  0.0 0.7 fusion.1
  0.7 0.1 copy.19
  0.8 0.2 reduce_window_sum.11
  1.0 0.1 copy.20
  1.1 0.1 add_select_fusion
  1.1 0.2 fusion
  1.3 0.2 copy.21
  1.5 51.6 %all-gather = bf16[2048,128]{1,0:T(8,128)(2,1)S(1)} all-gather(bf16[128,128]{1,0:T(8,128)(2,1)} %param.6), channel_id=2, replica_groups=mesh['groups'=2,'expert'=4,'etp_0'=16,'etp_1'=2] {'etp_0'}, dimensions={0}, use_global_device_ids=true | all-gather | bytes 557056 | tf_op jit(solution)/shard_map/all_gather | solution.py:179
  53.1 0.6 shard_map.64
  53.7 18.2 %all_to_all.15.x_ref = bf16[4,16,96,128]{3,2,1,0:T(8,128)(2,1)S(1)} all-to-all(bf16[4,16,96,128]{3,2,1,0:T(8,128)(2,1)S(1)} %shard_map.64), channel_id=1, replica_groups=mesh['groups'=2,'expert'=4,'etp_0'=16,'etp_1'=2] {'expert'}, dimensions={0} | all-to-all | bytes 3145728 | tf_op jit(solution)/shard_map/all_to_all | solution.py:183
  71.8 0.0 collective-permute-start
  71.8 6.4 %copy.22 = bf16[1,4096,448]{2,1,0:T(8,128)(2,1)} copy(bf16[1,4096,448]{1,2,0:T(8,128)(2,1)} %param.9) | data formatting | bytes 7340032 | tf_op args[3]
  78.2 6.5 %copy.23 = bf16[1,4096,448]{2,1,0:T(8,128)(2,1)} copy(bf16[1,4096,448]{1,2,0:T(8,128)(2,1)} %param.10) | data formatting | bytes 7340032 | tf_op args[4]
  84.7 0.0 copy-start
  84.7 2.2 %copy-done = bf16[1,4096,448]{2,1,0:T(8,128)(2,1)S(1)} copy-done((bf16[1,4096,448]{2,1,0:T(8,128)(2,1)S(1)}, bf16[1,4096,448]{2,1,0:T(8,128)(2,1)}, u32[]{:S(2)}) %copy-start) | copy-done | bytes 3670040
  86.9 0.0 copy-start.2
  86.9 2.2 %copy-done.2 = bf16[1,4096,448]{2,1,0:T(8,128)(2,1)S(1)} copy-done((bf16[1,4096,448]{2,1,0:T(8,128)(2,1)S(1)}, bf16[1,4096,448]{2,1,0:T(8,128)(2,1)}, u32[]{:S(2)}) %copy-start.2) | copy-done | bytes 3670040
  89.1 0.0 copy-start.1
  89.1 0.0 copy-start.3
  89.1 2.7 %shard_map.65 = (f32[384,448]{1,0:T(8,128)S(1)}, f32[384,448]{1,0:T(8,128)S(1)}) custom-call(s32[1]{0:T(128)} %bitcast.core_ref, bf16[4,16,96,128]{3,2,1,0:T(8,128)(2,1)S(1)} %all_to_all.15.x_ref, bf16[16,2,128,448]{3,2,1,0:T(8,128)(2,1)S(1)} %bitcast.7, bf16[16,2,128,448]{3,2,1,0:T(8,128)(2,1)S(1)} %bitcast.10), custom_call_target="tpu_custom_call" | custom-call | flops 1409286144 | bytes 3523215 | tf_op jit(solution)/shard_map/pallas_call | solution.py:195
  91.8 0.0 collective-permute-done.x_ref
  91.8 0.0 copy-done.1
  91.8 0.6 copy-done.3
  92.4 5.2 %shard_map.66 = (bf16[384,448]{1,0:T(8,128)(2,1)S(1)}, bf16[4,16,96,128]{3,2,1,0:T(8,128)(2,1)S(1)}) custom-call(s32[1]{0:T(128)} %bitcast.core_ref, bf16[4,16,96,128]{3,2,1,0:T(8,128)(2,1)S(1)} %collective-permute-done.x_ref, f32[384,448]{1,0:T(8,128)S(1)} %get-tuple-element.9.gate_ref, f32[384,448]{1,0:T(8,128)S(1)} %get-tuple-element.10.up_ref, ...), custom_call_target="tpu_custom_call" | custom-call | flops 2113929216 | bytes 5284823 | tf_op jit(solution)/shard_map/pallas_call | solution.py:198
  97.6 0.6 collective-permute-start.1
  98.2 2.2 %shard_map.67 = f32[4,16,96,128]{3,2,1,0:T(8,128)S(1)} custom-call(s32[1]{0:T(128)} %bitcast.core_ref, bf16[384,448]{1,0:T(8,128)(2,1)S(1)} %get-tuple-element.11.hidden_ref, bf16[448,4096]{1,0:T(8,128)(2,1)S(1)} %bitcast.12), custom_call_target="tpu_custom_call" | custom-call | flops 704643072 | bytes 1761607 | tf_op jit(solution)/shard_map/pallas_call | solution.py:206
  100.4 0.8 collective-permute-done.1
  101.3 1.6 add_convert_fusion
  102.9 0.0 copy-start.4
  102.9 0.0 copy-start.5
  102.9 3.8 %all-to-all-start.1 = ((bf16[4,16,96,128]{3,2,1,0:T(8,128)(2,1)}), bf16[4,16,96,128]{3,2,1,0:T(8,128)(2,1)S(1)}, u32[]{:S(2)}, u32[]{:S(2)}) async-start(bf16[4,16,96,128]{3,2,1,0:T(8,128)(2,1)} %add_convert_fusion), calls=%async_computation.1 | async-start | bytes 3145728 | tf_op jit(solution)/shard_map/all_to_all | solution.py:210
  106.6 0.0 copy-done.4
  106.7 0.0 copy-done.5
  106.7 0.2 select_reduce_fusion.table_ref
  106.9 21.2 %all-to-all-done.1.results_ref = bf16[4,16,96,128]{3,2,1,0:T(8,128)(2,1)S(1)} async-done(((bf16[4,16,96,128]{3,2,1,0:T(8,128)(2,1)}), bf16[4,16,96,128]{3,2,1,0:T(8,128)(2,1)S(1)}, u32[]{:S(2)}, u32[]{:S(2)}) %all-to-all-start.1) | async-done | bytes 1572896 | tf_op jit(solution)/shard_map/all_to_all | solution.py:210
  128.1 0.4 shard_map.68
  128.5 31.9 %all_to_all.16 = bf16[16,128,128]{2,1,0:T(8,128)(2,1)S(1)} all-to-all(bf16[16,128,128]{2,1,0:T(8,128)(2,1)S(1)} %shard_map.68), channel_id=1, replica_groups=mesh['groups'=2,'expert'=4,'etp_0'=16,'etp_1'=2] {'etp_0'}, dimensions={0} | all-to-all | bytes 1048576 | tf_op jit(solution)/shard_map/all_to_all | solution.py:214
  160.4 0.7 reduce_sum.32
  (4 shorter events, 0.0 us)
Async XLA Ops:
  71.8 19.9 %collective-permute-start = (bf16[4,16,96,128]{3,2,1,0:T(8,128)(2,1)S(1)}, bf16[4,16,96,128]{3,2,1,0:T(8,128)(2,1)S(1)}, u32[]{:S(2)}, u32[]{:S(2)}) collective-permute-start(bf16[4,16,96,128]{3,2,1,0:T(8,128)(2,1)S(1)} %all_to_all.15.x_ref), channel_id=1, source_target_pairs={{0,1},{1,0},{2,3},{3,2},{4,5},{5,4},{6,7},{7,6},{8,9},{9,8},{10,11... | collective-permute-start | bytes 4718600 | tf_op jit(solution)/shard_map/ppermute | solution.py:184
  84.7 2.2 %copy-start = (bf16[1,4096,448]{2,1,0:T(8,128)(2,1)S(1)}, bf16[1,4096,448]{2,1,0:T(8,128)(2,1)}, u32[]{:S(2)}) copy-start(bf16[1,4096,448]{2,1,0:T(8,128)(2,1)} %copy.22) | copy-start | bytes 11010052
  86.9 2.2 %copy-start.2 = (bf16[1,4096,448]{2,1,0:T(8,128)(2,1)S(1)}, bf16[1,4096,448]{2,1,0:T(8,128)(2,1)}, u32[]{:S(2)}) copy-start(bf16[1,4096,448]{2,1,0:T(8,128)(2,1)} %copy.23) | copy-start | bytes 11010052
  89.1 2.7 %copy-start.1 = (bf16[1,4096,448]{2,1,0:T(8,128)(2,1)S(1)}, bf16[1,4096,448]{2,1,0:T(8,128)(2,1)}, u32[]{:S(2)}) copy-start(bf16[1,4096,448]{2,1,0:T(8,128)(2,1)} %copy.22) | copy-start | bytes 11010052
  89.1 3.3 %copy-start.3 = (bf16[1,448,4096]{2,1,0:T(8,128)(2,1)S(1)}, bf16[1,448,4096]{2,1,0:T(8,128)(2,1)}, u32[]{:S(2)}) copy-start(bf16[1,448,4096]{2,1,0:T(8,128)(2,1)} %param.11) | copy-start | bytes 11010052
  97.6 3.7 %collective-permute-start.1 = (bf16[4,16,96,128]{3,2,1,0:T(8,128)(2,1)S(1)}, bf16[4,16,96,128]{3,2,1,0:T(8,128)(2,1)S(1)}, u32[]{:S(2)}, u32[]{:S(2)}) collective-permute-start(bf16[4,16,96,128]{3,2,1,0:T(8,128)(2,1)S(1)} %get-tuple-element.12), channel_id=1, source_target_pairs={{0,1},{1,0},{2,3},{3,2},{4,5},{5,4},{6,7},{7,6},{8,9},{9,8},{10,11... | collective-permute-start | bytes 4718600 | tf_op jit(solution)/shard_map/ppermute | solution.py:205
  102.9 3.8 %copy-start.4 = (f32[128,2]{0,1:T(2,128)S(1)}, f32[128,2]{0,1:T(2,128)}, u32[]{:S(2)}) copy-start(f32[128,2]{0,1:T(2,128)} %param.8) | copy-start | bytes 3076
  102.9 3.8 %copy-start.5 = (s32[128,2]{0,1:T(2,128)S(1)}, s32[128,2]{0,1:T(2,128)}, u32[]{:S(2)}) copy-start(s32[128,2]{0,1:T(2,128)} %param.7) | copy-start | bytes 3076
  102.9 25.2 %all-to-all-start.1 = ((bf16[4,16,96,128]{3,2,1,0:T(8,128)(2,1)}), bf16[4,16,96,128]{3,2,1,0:T(8,128)(2,1)S(1)}, u32[]{:S(2)}, u32[]{:S(2)}) async-start(bf16[4,16,96,128]{3,2,1,0:T(8,128)(2,1)} %add_convert_fusion), calls=%async_computation.1 | async-start | bytes 3145728 | tf_op jit(solution)/shard_map/all_to_all | solution.py:210

commit v2 on v1

v2 whole, which is shorter than its diff:
```python
import functools

import jax
import jax.numpy as jnp
from jax import lax
from jax.experimental import pallas as pl
from jax.experimental.pallas import tpu as pltpu
from jax.sharding import Mesh
from jax.sharding import PartitionSpec as P

CAP = 96
CORES = 2
ETP = ("etp_0", "etp_1")
LANES = 128
CHUNKS = 4

VMEM = pl.BlockSpec(memory_space=pltpu.VMEM)
SMEM = pl.BlockSpec(memory_space=pltpu.SMEM)


def dot32(a, b):
    return jnp.dot(a, b, preferred_element_type=jnp.float32)


def columns_of(ref, start, count):
    groups, _, rows, lanes = ref.shape
    parts = [ref[:, z].reshape(groups * rows, lanes) for z in range(start, start + count)]
    return jnp.concatenate(parts, axis=1)


def dispatch_body(table_ref, tokens_ref, out_ref):
    experts, chips, cap, lanes = out_ref.shape
    table = table_ref[...]
    for z in range(0, chips, 2):
        pair = jnp.concatenate([tokens_ref[z], tokens_ref[z + 1]], axis=1)
        rows = dot32(table, pair).astype(out_ref.dtype)
        for k in range(2):
            out_ref[:, z + k] = rows[:, k * lanes : (k + 1) * lanes].reshape(experts, cap, lanes)


def core_columns(ref, core, start, count):
    parts = [
        ref[:, pl.ds(pl.multiple_of((z * CORES + core) * LANES, LANES), LANES)] for z in range(start, start + count)
    ]
    return jnp.concatenate(parts, axis=1)


def up_partial(core, x_ref, w_refs):
    chips = x_ref.shape[1]
    step = chips // CHUNKS
    sums = [None] * len(w_refs)
    for k in range(CHUNKS):
        x = columns_of(x_ref, k * step, step)
        for i, w in enumerate(w_refs):
            part = lax.dot_general(
                x, core_columns(w, core, k * step, step), (((1,), (1,)), ((), ())), preferred_element_type=jnp.float32
            )
            sums[i] = part if k == 0 else sums[i] + part
    return sums


def down_into(core, hidden, wd_ref, out_ref):
    blocks, chips, cap, lanes = out_ref.shape
    step = chips // CHUNKS
    for k in range(CHUNKS):
        part = dot32(hidden, core_columns(wd_ref, core, k * step, step)).astype(out_ref.dtype)
        for z in range(step):
            out_ref[:, k * step + z] = part[:, z * lanes : (z + 1) * lanes].reshape(blocks, cap, lanes)


def first_half_body(core_ref, x_ref, wg_ref, wu_ref, gate_ref, up_ref):
    gate_ref[...], up_ref[...] = up_partial(core_ref[0], x_ref, (wg_ref, wu_ref))


def second_half_body(core_ref, x_ref, gate_ref, up_ref, wg_ref, wu_ref, wd_ref, hidden_ref, out_ref):
    other = 1 - core_ref[0]
    gate, up = up_partial(other, x_ref, (wg_ref, wu_ref))
    gate = gate + gate_ref[...]
    up = up + up_ref[...]
    hidden = (gate / (1.0 + jnp.exp(-gate)) * up).astype(jnp.bfloat16)
    hidden_ref[...] = hidden
    down_into(other, hidden, wd_ref, out_ref)


def own_down_body(core_ref, hidden_ref, wd_ref, out_ref):
    down_into(core_ref[0], hidden_ref[...], wd_ref, out_ref)


def combine_body(table_ref, results_ref, out_ref):
    chips, _, lanes = out_ref.shape
    table = table_ref[...]
    for z in range(0, chips, 2):
        rows = dot32(table, columns_of(results_ref, z, 2)).astype(out_ref.dtype)
        for k in range(2):
            out_ref[z + k] = rows[:, k * lanes : (k + 1) * lanes]


def call(body, out_shape, in_specs, flops=0):
    outs = jax.tree.map(lambda _: VMEM, out_shape)
    return pl.pallas_call(
        body,
        out_shape=out_shape,
        in_specs=list(in_specs),
        out_specs=outs,
        cost_estimate=pl.CostEstimate(flops=flops, transcendentals=0, bytes_accessed=flops // 400),
        compiler_params=pltpu.CompilerParams(vmem_limit_bytes=24 * 1024 * 1024),
    )


def shards(tokens, route_ids, gate_weights, w_gate, w_up, w_down):
    experts = lax.axis_size("expert")
    chips = lax.axis_size("etp_0")
    token_count, lanes = tokens.shape
    slots = experts * CAP
    _, width_in, width = w_gate.shape
    bf16, f32 = jnp.bfloat16, jnp.float32
    shape = jax.ShapeDtypeStruct

    expert_iota = lax.broadcasted_iota(jnp.int32, (1, 1, experts), 2)
    hit_mask = route_ids[:, :, None] == expert_iota
    routed = jnp.any(hit_mask, axis=1).astype(jnp.int32)
    weighting = jnp.sum(jnp.where(hit_mask, gate_weights[:, :, None], 0.0), axis=1)
    slot_index = jnp.cumsum(routed, axis=0) - 1
    expert_base = lax.broadcasted_iota(jnp.int32, (1, experts), 1) * CAP
    target_slot = jnp.where(routed == 1, expert_base + slot_index, -1)
    slot_iota = lax.broadcasted_iota(jnp.int32, (1, 1, slots), 2)
    pick_table = target_slot[:, :, None] == slot_iota
    select_table = jnp.any(pick_table, axis=1).astype(bf16).T
    combine_table = jnp.sum(jnp.where(pick_table, weighting[:, :, None], 0.0), axis=1).astype(bf16)

    select_table, combine_table = lax.optimization_barrier((select_table, combine_table))

    core = lax.axis_index("etp_1").astype(jnp.int32).reshape(1)
    swap = functools.partial(lax.ppermute, axis_name="etp_1", perm=[(0, 1), (1, 0)])
    exchange = functools.partial(lax.all_to_all, split_axis=0, concat_axis=0, tiled=True)

    gathered = lax.all_gather(tokens, "etp_0", axis=0, tiled=False)
    sent = call(
        dispatch_body, shape((experts, chips, CAP, lanes), bf16), (VMEM, VMEM), flops=2 * slots * token_count * chips * lanes
    )(select_table, gathered)
    own = exchange(sent, "expert")
    other = swap(own)

    gate_rows = jnp.swapaxes(w_gate[0], 0, 1)
    up_rows = jnp.swapaxes(w_up[0], 0, 1)
    down_rows = w_down[0]
    up_flops = 2 * slots * width * width_in
    acc = shape((slots, width), f32)
    gate_half, up_half = call(first_half_body, (acc, acc), (SMEM, VMEM, VMEM, VMEM), flops=up_flops)(
        core, own, gate_rows, up_rows
    )
    hidden, theirs = call(
        second_half_body,
        (shape((slots, width), bf16), shape((experts, chips, CAP, lanes), bf16)),
        (SMEM, VMEM, VMEM, VMEM, VMEM, VMEM, VMEM),
        flops=up_flops * 3 // 2,
    )(core, other, gate_half, up_half, gate_rows, up_rows, down_rows)
    arrived = swap(theirs)
    mine = call(
        own_down_body, shape((experts, chips, CAP, lanes), f32), (SMEM, VMEM, VMEM), flops=up_flops // 2
    )(core, hidden, down_rows)
    chip_sum = (mine + arrived.astype(f32)).astype(bf16)
    results = exchange(chip_sum, "expert")
    blended = call(
        combine_body, shape((chips, token_count, lanes), bf16), (VMEM, VMEM), flops=2 * slots * token_count * chips * lanes
    )(combine_table, results)
    pieces = exchange(blended, "etp_0")
    return pieces.astype(f32).sum(axis=0).astype(bf16)


def solution(mesh):
    groups, experts, etp = (mesh.shape[name] for name in ("groups", "expert", "etp"))
    finer = Mesh(
        mesh.devices.reshape(groups, experts, etp // CORES, CORES),
        ("groups", "expert", "etp_0", "etp_1"),
    )
    placed = (
        P(("groups", "expert"), ETP),
        P(("groups", "expert"), None),
        P(("groups", "expert"), None),
        P("expert", None, ETP),
        P("expert", None, ETP),
        P("expert", ETP, None),
    )
    return jax.shard_map(
        shards, mesh=finer, in_specs=placed, out_specs=P(("groups", "expert"), ETP), check_vma=False
    )
```

time: 162 us -> 146 us (0.901)
  blocking collectives: 102 us -> 125 us
  waiting for transfers between devices: 22 us -> 1.98 us
  local copies, waits for them, and re-layouts: 18.2 us -> 7.74 us
  Pallas kernels: 11 us -> 6.82 us
  starting transfers between devices: 4.41 us -> 0.63 us
    all_to_all x0 -> x1, blocking collectives: none -> 24 us  [shards(): results = exchange(chip_sum, 'expert')]
    all_to_all x1 -> x0, waiting for transfers between devices: 21.2 us -> none  [shards(): results = exchange(chip_sum, 'expert')]
    unnamed x14 -> x10, local copies, waits for them, and re-layouts: 17.9 us -> 7.4 us
    all_to_all x1 -> x0, starting transfers between devices: 3.78 us -> none  [shards(): results = exchange(chip_sum, 'expert')]
    pallas_call x1, Pallas kernels: 5.19 us -> 2.92 us  [shards(): call(second_half_body, (shape((slots, width), bf16), shape((experts, chip...]
  transfers between devices with their start and end apart: 3 -> 2, of which waited for: 2 -> 1; matrix products, arithmetic and copies ran while one was open for 8% -> 0% of each run, Pallas kernels for 3% -> 2%
where the time goes in v2:
time: 146 us
  blocking collectives  125 us (86%)
  local copies, waits for them, and re-layouts  7.74 us (5%)
  Pallas kernels  6.82 us (5%)
  other arithmetic  3.18 us (2%)
  waiting for transfers between devices  1.98 us (1%)
    all_gather x1, blocking collectives, shards(): gathered = lax.all_gather(tokens, 'etp_0', axis=0, tiled=False)  51.6 us
    all_to_all x1, blocking collectives, shards(): pieces = exchange(blended, 'etp_0')  31.6 us
    all_to_all x1, blocking collectives, shards(): results = exchange(chip_sum, 'expert')  24 us
    all_to_all x1, blocking collectives, shards(): own = exchange(sent, 'expert')  18.2 us
    unnamed x10, local copies, waits for them, and re-layouts  7.4 us
    pallas_call x1, Pallas kernels, shards(): call(second_half_body, (shape((slots, width), bf16), shape((experts, chip...  2.92 us
  transfers between devices with their start and end apart: 2, of which 1 were waited for; matrix products, arithmetic and copies ran while one was open for 0% of the time, Pallas kernels for 2%

profile of v2, /device:TPU:40, one launch (start us, length us, event | category | flops | bytes accessed | tf_op | source)
XLA Modules:
  0.0 145.8 jit_solution(14867180310006371431)
XLA Ops:
  0.0 0.7 fusion.1
  0.7 0.7 select_reduce_fusion.1
  1.4 0.1 copy.15
  1.5 0.2 reduce_window_sum.11
  1.7 0.1 copy.16
  1.8 0.1 add_select_fusion
  1.8 0.2 fusion
  2.0 0.2 copy.17
  2.2 0.2 select_reduce_fusion.table_ref
  2.4 51.6 %all-gather = bf16[2048,128]{1,0:T(8,128)(2,1)S(1)} all-gather(bf16[128,128]{1,0:T(8,128)(2,1)} %param.6), channel_id=2, replica_groups=mesh['groups'=2,'expert'=4,'etp_0'=16,'etp_1'=2] {'etp_0'}, dimensions={0}, use_global_device_ids=true | all-gather | bytes 557056 | tf_op jit(solution)/shard_map/all_gather | solution.py:137
  54.0 0.6 shard_map.64
  54.6 18.2 %all_to_all.15.x_ref = bf16[4,16,96,128]{3,2,1,0:T(8,128)(2,1)S(1)} all-to-all(bf16[4,16,96,128]{3,2,1,0:T(8,128)(2,1)S(1)} %shard_map.64), channel_id=1, replica_groups=mesh['groups'=2,'expert'=4,'etp_0'=16,'etp_1'=2] {'expert'}, dimensions={0} | all-to-all | bytes 3145728 | tf_op jit(solution)/shard_map/all_to_all | solution.py:141
  72.7 0.0 collective-permute-start
  72.7 0.0 copy-start.1
  72.7 2.0 %copy-done.1 = bf16[1,4096,448]{1,2,0:T(8,128)(2,1)S(1)} copy-done((bf16[1,4096,448]{1,2,0:T(8,128)(2,1)S(1)}, bf16[1,4096,448]{1,2,0:T(8,128)(2,1)}, u32[]{:S(2)}) %copy-start.1) | copy-done | bytes 3670040
  74.8 0.0 copy-start.3
  74.8 2.0 %copy-done.3 = bf16[1,4096,448]{1,2,0:T(8,128)(2,1)S(1)} copy-done((bf16[1,4096,448]{1,2,0:T(8,128)(2,1)S(1)}, bf16[1,4096,448]{1,2,0:T(8,128)(2,1)}, u32[]{:S(2)}) %copy-start.3) | copy-done | bytes 3670040
  76.8 0.0 copy-start
  76.8 0.0 copy-start.2
  76.8 1.9 %shard_map.65 = (f32[384,448]{1,0:T(8,128)S(1)}, f32[384,448]{1,0:T(8,128)S(1)}) custom-call(s32[1]{0:T(128)} %bitcast.1.core_ref, bf16[4,16,96,128]{3,2,1,0:T(8,128)(2,1)S(1)} %all_to_all.15.x_ref, bf16[448,4096]{1,0:T(8,128)(2,1)S(1)} %bitcast.13, bf16[448,4096]{1,0:T(8,128)(2,1)S(1)} %bitcast.15), custom_call_target="tpu_custom_call" | custom-call | flops 1409286144 | bytes 3523215 | tf_op jit(solution)/shard_map/pallas_call | solution.py:149
  78.7 0.0 collective-permute-done.x_ref
  78.7 0.2 copy-done
  78.8 1.1 copy-done.2
  80.0 0.0 copy-start.4
  80.0 2.0 %copy-done.4 = bf16[1,4096,448]{1,2,0:T(8,128)(2,1)S(1)} copy-done((bf16[1,4096,448]{1,2,0:T(8,128)(2,1)S(1)}, bf16[1,4096,448]{1,2,0:T(8,128)(2,1)}, u32[]{:S(2)}) %copy-start.4) | copy-done | bytes 3670040
  82.0 2.9 %shard_map.66 = (bf16[384,448]{1,0:T(8,128)(2,1)S(1)}, bf16[4,16,96,128]{3,2,1,0:T(8,128)(2,1)S(1)}) custom-call(s32[1]{0:T(128)} %bitcast.1.core_ref, bf16[4,16,96,128]{3,2,1,0:T(8,128)(2,1)S(1)} %collective-permute-done.x_ref, f32[384,448]{1,0:T(8,128)S(1)} %get-tuple-element.13.gate_ref, f32[384,448]{1,0:T(8,128)S(1)} %get-tuple-element.14.up_ref, ...), custom_call_target="tpu_custom_call" | custom-call | flops 2113929216 | bytes 5284823 | tf_op jit(solution)/shard_map/pallas_call | solution.py:152
  84.9 0.6 collective-permute-start.1
  85.6 1.1 shard_map.67
  86.6 2.0 %collective-permute-done.1 = bf16[4,16,96,128]{3,2,1,0:T(8,128)(2,1)S(1)} collective-permute-done((bf16[4,16,96,128]{3,2,1,0:T(8,128)(2,1)S(1)}, bf16[4,16,96,128]{3,2,1,0:T(8,128)(2,1)S(1)}, u32[]{:S(2)}, u32[]{:S(2)}) %collective-permute-start.1) | collective-permute-done | bytes 1572896 | tf_op jit(solution)/shard_map/ppermute | solution.py:158
  88.6 0.4 add_convert_fusion
  89.0 24.0 %all_to_all.16.results_ref = bf16[4,16,96,128]{3,2,1,0:T(8,128)(2,1)S(1)} all-to-all(bf16[4,16,96,128]{3,2,1,0:T(8,128)(2,1)S(1)} %add_convert_fusion), channel_id=1, replica_groups=mesh['groups'=2,'expert'=4,'etp_0'=16,'etp_1'=2] {'expert'}, dimensions={0} | all-to-all | bytes 3145728 | tf_op jit(solution)/shard_map/all_to_all | solution.py:163
  113.0 0.4 shard_map.68
  113.5 31.6 %all_to_all.17 = bf16[16,128,128]{2,1,0:T(8,128)(2,1)S(1)} all-to-all(bf16[16,128,128]{2,1,0:T(8,128)(2,1)S(1)} %shard_map.68), channel_id=1, replica_groups=mesh['groups'=2,'expert'=4,'etp_0'=16,'etp_1'=2] {'etp_0'}, dimensions={0} | all-to-all | bytes 1048576 | tf_op jit(solution)/shard_map/all_to_all | solution.py:167
  145.1 0.7 reduce_sum.32
  (3 shorter events, 0.0 us)
Async XLA Ops:
  72.7 5.9 %collective-permute-start = (bf16[4,16,96,128]{3,2,1,0:T(8,128)(2,1)S(1)}, bf16[4,16,96,128]{3,2,1,0:T(8,128)(2,1)S(1)}, u32[]{:S(2)}, u32[]{:S(2)}) collective-permute-start(bf16[4,16,96,128]{3,2,1,0:T(8,128)(2,1)S(1)} %all_to_all.15.x_ref), channel_id=1, source_target_pairs={{0,1},{1,0},{2,3},{3,2},{4,5},{5,4},{6,7},{7,6},{8,9},{9,8},{10,11... | collective-permute-start | bytes 4718600 | tf_op jit(solution)/shard_map/ppermute | solution.py:142
  72.7 2.0 %copy-start.1 = (bf16[1,4096,448]{1,2,0:T(8,128)(2,1)S(1)}, bf16[1,4096,448]{1,2,0:T(8,128)(2,1)}, u32[]{:S(2)}) copy-start(bf16[1,4096,448]{1,2,0:T(8,128)(2,1)} %param.9) | copy-start | bytes 11010052
  74.8 2.0 %copy-start.3 = (bf16[1,4096,448]{1,2,0:T(8,128)(2,1)S(1)}, bf16[1,4096,448]{1,2,0:T(8,128)(2,1)}, u32[]{:S(2)}) copy-start(bf16[1,4096,448]{1,2,0:T(8,128)(2,1)} %param.10) | copy-start | bytes 11010052
  76.8 2.0 %copy-start = (bf16[1,448,4096]{2,1,0:T(8,128)(2,1)S(1)}, bf16[1,448,4096]{2,1,0:T(8,128)(2,1)}, u32[]{:S(2)}) copy-start(bf16[1,448,4096]{2,1,0:T(8,128)(2,1)} %param.11) | copy-start | bytes 11010052
  76.8 3.2 %copy-start.2 = (bf16[1,4096,448]{1,2,0:T(8,128)(2,1)S(1)}, bf16[1,4096,448]{1,2,0:T(8,128)(2,1)}, u32[]{:S(2)}) copy-start(bf16[1,4096,448]{1,2,0:T(8,128)(2,1)} %param.9) | copy-start | bytes 11010052
  80.0 2.0 %copy-start.4 = (bf16[1,4096,448]{1,2,0:T(8,128)(2,1)S(1)}, bf16[1,4096,448]{1,2,0:T(8,128)(2,1)}, u32[]{:S(2)}) copy-start(bf16[1,4096,448]{1,2,0:T(8,128)(2,1)} %param.10) | copy-start | bytes 11010052
  84.9 3.7 %collective-permute-start.1 = (bf16[4,16,96,128]{3,2,1,0:T(8,128)(2,1)S(1)}, bf16[4,16,96,128]{3,2,1,0:T(8,128)(2,1)S(1)}, u32[]{:S(2)}, u32[]{:S(2)}) collective-permute-start(bf16[4,16,96,128]{3,2,1,0:T(8,128)(2,1)S(1)} %get-tuple-element.16), channel_id=1, source_target_pairs={{0,1},{1,0},{2,3},{3,2},{4,5},{5,4},{6,7},{7,6},{8,9},{9,8},{10,11... | collective-permute-start | bytes 4718600 | tf_op jit(solution)/shard_map/ppermute | solution.py:158

commit v3 on v2

v3 whole, which is shorter than its diff:
```python
import functools

import jax
import jax.numpy as jnp
from jax import lax
from jax.experimental import pallas as pl
from jax.experimental.pallas import tpu as pltpu
from jax.sharding import Mesh
from jax.sharding import PartitionSpec as P

CAP = 96
CORES = 2
Z = ("z_0", "z_1")
ETP = (*Z, "core")
LANES = 128
CHUNKS = 4
AHEAD = 2
PARITIES = 2

HBM = pl.BlockSpec(memory_space=pltpu.HBM)
VMEM = pl.BlockSpec(memory_space=pltpu.VMEM)
SMEM = pl.BlockSpec(memory_space=pltpu.SMEM)


def dot32(a, b):
    return jnp.dot(a, b, preferred_element_type=jnp.float32)


def columns_of(ref, start, count):
    groups, _, rows, lanes = ref.shape
    parts = [ref[:, z].reshape(groups * rows, lanes) for z in range(start, start + count)]
    return jnp.concatenate(parts, axis=1)


def dispatch_body(table_ref, tokens_ref, out_ref):
    experts, chips, cap, lanes = out_ref.shape
    table = table_ref[...]
    for z in range(0, chips, 2):
        pair = jnp.concatenate([tokens_ref[z], tokens_ref[z + 1]], axis=1)
        rows = dot32(table, pair).astype(out_ref.dtype)
        for k in range(2):
            out_ref[:, z + k] = rows[:, k * lanes : (k + 1) * lanes].reshape(experts, cap, lanes)


def core_copies(w_ref, core, buf, sems, first=0):
    return [
        pltpu.make_async_copy(
            w_ref.at[:, pl.ds(pl.multiple_of(((first + k) * CORES + core) * LANES, LANES), LANES)],
            buf.at[:, pl.ds(k * LANES, LANES)],
            sems.at[k],
        )
        for k in range(buf.shape[1] // LANES)
    ]


def start_all(copies):
    for copy in copies:
        copy.start()


def wait_all(copies):
    for copy in copies:
        if copy is not None:
            copy.wait()


def chunk_of(bufs, k, size):
    for buf in bufs:
        if k * size < buf.shape[1]:
            return buf[:, k * size : (k + 1) * size]
        k -= buf.shape[1] // size


def up_partial(x_ref, weights):
    chips = x_ref.shape[1]
    step = chips // CHUNKS
    sums = [None] * len(weights)
    for k in range(CHUNKS):
        x = columns_of(x_ref, k * step, step)
        for i, (copies, bufs) in enumerate(weights):
            wait_all(copies[k * step : (k + 1) * step])
            part = lax.dot_general(
                x, chunk_of(bufs, k, step * LANES), (((1,), (1,)), ((), ())), preferred_element_type=jnp.float32
            )
            sums[i] = part if k == 0 else sums[i] + part
    return sums


def down_into(hidden, copies, wd_ref, out_ref):
    blocks, chips, cap, lanes = out_ref.shape
    step = chips // CHUNKS
    for k in range(CHUNKS):
        wait_all(copies[k * step : (k + 1) * step])
        part = dot32(hidden, wd_ref[:, k * step * lanes : (k + 1) * step * lanes]).astype(out_ref.dtype)
        for z in range(step):
            out_ref[:, k * step + z] = part[:, z * lanes : (z + 1) * lanes].reshape(blocks, cap, lanes)


def first_half_body(core_ref, x_ref, wg_ref, wu_ref, gate_ref, up_ref, g_ahead, u_ahead, g_buf, u_buf, sems, ahead_sems):
    core = core_ref[0]
    gates = core_copies(wg_ref, core, g_buf, sems.at[0])
    ups = core_copies(wu_ref, core, u_buf, sems.at[1])
    ahead = core_copies(wg_ref, 1 - core, g_ahead, ahead_sems.at[0])
    ahead += core_copies(wu_ref, 1 - core, u_ahead, ahead_sems.at[1])
    for pair in zip(gates, ups):
        start_all(pair)
    start_all(ahead)
    gate_ref[...], up_ref[...] = up_partial(x_ref, [(gates, [g_buf]), (ups, [u_buf])])
    wait_all(ahead)


def second_half_body(
    core_ref, x_ref, gate_ref, up_ref, g_ahead, u_ahead, wg_ref, wu_ref, wd_ref,
    hidden_ref, out_ref, down_own, g_buf, u_buf, d_buf, sems,
):
    core = core_ref[0]
    here = g_ahead.shape[1] // LANES
    gates = core_copies(wg_ref, 1 - core, g_buf, sems.at[0], here)
    ups = core_copies(wu_ref, 1 - core, u_buf, sems.at[1], here)
    downs = core_copies(wd_ref, 1 - core, d_buf, sems.at[2])
    owns = core_copies(wd_ref, core, down_own, sems.at[3])
    for pair in zip(gates, ups):
        start_all(pair)
    start_all(downs)
    start_all(owns)
    held = [None] * here
    gate, up = up_partial(x_ref, [(held + gates, [g_ahead, g_buf]), (held + ups, [u_ahead, u_buf])])
    gate = gate + gate_ref[...]
    up = up + up_ref[...]
    hidden = (gate / (1.0 + jnp.exp(-gate)) * up).astype(jnp.bfloat16)
    hidden_ref[...] = hidden
    down_into(hidden, downs, d_buf, out_ref)
    wait_all(owns)


def own_down_body(hidden_ref, down_own, out_ref):
    down_into(hidden_ref[...], [], down_own, out_ref)


def combine_body(parity_ref, table_ref, results_ref, own_ref, right_ref, left_ref):
    parity = parity_ref[0]
    table = table_ref[...]
    half = right_ref.shape[0]

    def rows_of(chip):
        return results_ref[:, chip].reshape(-1, LANES)

    for k in range(2 * half):
        mine, other = rows_of(PARITIES * k + parity), rows_of(PARITIES * k + 1 - parity)
        rows = dot32(table, jnp.concatenate([mine, other], axis=1)).astype(own_ref.dtype)
        own_ref[k] = rows[:, :LANES]
        (right_ref if k < half else left_ref)[k % half] = rows[:, LANES:]


def chip_pair_body(own_ref, low_ref, high_ref, out_ref):
    half = low_ref.shape[0]
    for part, ref in enumerate((low_ref, high_ref)):
        rows = pl.ds(part * half, half)
        out_ref[rows] = (own_ref[rows].astype(jnp.float32) + ref[...].astype(jnp.float32)).astype(out_ref.dtype)


def call(body, out_shape, in_specs, scratch=(), flops=0):
    outs = jax.tree.map(lambda _: VMEM, out_shape)
    return pl.pallas_call(
        body,
        out_shape=out_shape,
        in_specs=list(in_specs),
        out_specs=outs,
        scratch_shapes=list(scratch),
        cost_estimate=pl.CostEstimate(flops=flops, transcendentals=0, bytes_accessed=flops // 400),
        compiler_params=pltpu.CompilerParams(vmem_limit_bytes=24 * 1024 * 1024),
    )


def shards(tokens, route_ids, gate_weights, w_gate, w_up, w_down):
    experts = lax.axis_size("expert")
    chips = lax.axis_size(Z)
    token_count, lanes = tokens.shape
    slots = experts * CAP
    _, width_in, width = w_gate.shape
    bf16, f32 = jnp.bfloat16, jnp.float32
    shape = jax.ShapeDtypeStruct

    expert_iota = lax.broadcasted_iota(jnp.int32, (1, 1, experts), 2)
    hit_mask = route_ids[:, :, None] == expert_iota
    routed = jnp.any(hit_mask, axis=1).astype(jnp.int32)
    weighting = jnp.sum(jnp.where(hit_mask, gate_weights[:, :, None], 0.0), axis=1)
    slot_index = jnp.cumsum(routed, axis=0) - 1
    expert_base = lax.broadcasted_iota(jnp.int32, (1, experts), 1) * CAP
    target_slot = jnp.where(routed == 1, expert_base + slot_index, -1)
    slot_iota = lax.broadcasted_iota(jnp.int32, (1, 1, slots), 2)
    pick_table = target_slot[:, :, None] == slot_iota
    select_table = jnp.any(pick_table, axis=1).astype(bf16).T
    combine_table = jnp.sum(jnp.where(pick_table, weighting[:, :, None], 0.0), axis=1).astype(bf16)

    core = lax.axis_index("core").astype(jnp.int32).reshape(1)
    parity = lax.axis_index("z_1").astype(jnp.int32).reshape(1)
    select_table, combine_table, core, parity = lax.optimization_barrier((select_table, combine_table, core, parity))

    swap = functools.partial(lax.ppermute, axis_name="core", perm=[(0, 1), (1, 0)])
    exchange = functools.partial(lax.all_to_all, split_axis=0, concat_axis=0, tiled=True)

    gathered = lax.all_gather(tokens, Z, axis=0, tiled=False)
    sent = call(
        dispatch_body, shape((experts, chips, CAP, lanes), bf16), (VMEM, VMEM), flops=2 * slots * token_count * chips * lanes
    )(select_table, gathered)
    own = exchange(sent, "expert")
    other = swap(own)

    gate_rows, up_rows, down_rows = (
        pltpu.with_memory_space_constraint(w, pltpu.HBM)
        for w in (jnp.swapaxes(w_gate[0], 0, 1), jnp.swapaxes(w_up[0], 0, 1), w_down[0])
    )
    up_flops = 2 * slots * width * width_in
    acc = shape((slots, width), f32)
    ahead = shape((width, AHEAD * (chips // CHUNKS) * lanes), bf16)
    half_width = chips * lanes
    gate_half, up_half, gate_ahead, up_ahead = call(
        first_half_body,
        (acc, acc, ahead, ahead),
        (SMEM, VMEM, HBM, HBM),
        [pltpu.VMEM((width, half_width), bf16)] * 2 + [pltpu.SemaphoreType.DMA((2, chips)), pltpu.SemaphoreType.DMA((2, chips))],
        flops=up_flops,
    )(core, own, gate_rows, up_rows)
    rest = pltpu.VMEM((width, half_width - ahead.shape[1]), bf16)
    hidden, theirs, down_own = call(
        second_half_body,
        (
            shape((slots, width), bf16),
            shape((experts, chips, CAP, lanes), bf16),
            shape((width, half_width), bf16),
        ),
        (SMEM, VMEM, VMEM, VMEM, VMEM, VMEM, HBM, HBM, HBM),
        [rest, rest, pltpu.VMEM((width, half_width), bf16), pltpu.SemaphoreType.DMA((4, chips))],
        flops=up_flops * 3 // 2,
    )(core, other, gate_half, up_half, gate_ahead, up_ahead, gate_rows, up_rows, down_rows)
    arrived = swap(theirs)
    mine = call(own_down_body, shape((experts, chips, CAP, lanes), f32), (VMEM, VMEM), flops=up_flops // 2)(
        hidden, down_own
    )
    chip_sum = (mine + arrived.astype(f32)).astype(bf16)
    results = exchange(chip_sum, "expert")

    of_parity = chips // PARITIES

    def block(count):
        return shape((count, token_count, lanes), bf16)

    blended, right, left = call(
        combine_body,
        (block(of_parity), block(of_parity // 2), block(of_parity // 2)),
        (SMEM, VMEM, VMEM),
        flops=2 * slots * token_count * chips * lanes,
    )(parity, combine_table, results)
    low = lax.ppermute(right, Z, [(z, (z + 1) % chips) for z in range(chips)])
    high = lax.ppermute(left, Z, [(z, (z - 1) % chips) for z in range(chips)])
    paired = call(chip_pair_body, block(of_parity), (VMEM, VMEM, VMEM))(blended, low, high)
    pieces = exchange(paired, "z_0")
    return pieces.astype(f32).sum(axis=0).astype(bf16)


def solution(mesh):
    groups, experts, etp = (mesh.shape[name] for name in ("groups", "expert", "etp"))
    finer = Mesh(
        mesh.devices.reshape(groups, experts, etp // (CORES * PARITIES), PARITIES, CORES),
        ("groups", "expert", *ETP),
    )
    placed = (
        P(("groups", "expert"), ETP),
        P(("groups", "expert"), None),
        P(("groups", "expert"), None),
        P("expert", None, ETP),
        P("expert", None, ETP),
        P("expert", ETP, None),
    )
    return jax.shard_map(
        shards, mesh=finer, in_specs=placed, out_specs=P(("groups", "expert"), ETP), check_vma=False
    )
```

time: 146 us -> 142 us (0.973)
  blocking collectives: 125 us -> 117 us
  local copies, waits for them, and re-layouts: 7.74 us -> 0.34 us
  Pallas kernels: 6.82 us -> 12.3 us
  starting transfers between devices: 0.63 us -> 3.97 us
  waiting for transfers between devices: 1.98 us -> 5.01 us
    all_to_all x1, blocking collectives: 31.6 us -> 23.4 us  [shards(): pieces = exchange(paired, 'z_0')]
    unnamed x10 -> x0, local copies, waits for them, and re-layouts: 7.4 us -> none
    ppermute x0 -> x2, starting transfers between devices: none -> 3.34 us  [the longest x1 3.21 us: shards(): high = lax.ppermute(left, Z, [(z, (z - 1) % chips) for z in range(chips)])]
    ppermute x0 -> x2, waiting for transfers between devices: none -> 2.94 us  [the longest x1 2.94 us: shards(): low = lax.ppermute(right, Z, [(z, (z + 1) % chips) for z in range(chips)])]
    pallas_call x3 -> x4, Pallas kernels: 3.34 us -> 6.17 us  [the longest x1 4.7 us: shards(): call(first_half_body, (acc, acc, ahead, ahead), (SMEM, VMEM, HBM, HBM), [...]
    pallas_call x1, Pallas kernels: 2.92 us -> 5.56 us  [shards(): call(second_half_body, (shape((slots, width), bf16), shape((experts, chip...]
  transfers between devices with their start and end apart: 2 -> 4, of which waited for: 1 -> 2; matrix products, arithmetic and copies ran while one was open for 0% -> 0% of each run, Pallas kernels for 2% -> 4%
where the time goes in v3:
time: 142 us
  blocking collectives  117 us (82%)
  Pallas kernels  12.3 us (9%)
  waiting for transfers between devices  5.01 us (4%)
  starting transfers between devices  3.97 us (3%)
  other arithmetic  3.25 us (2%)
    all_gather x1, blocking collectives, shards(): gathered = lax.all_gather(tokens, Z, axis=0, tiled=False)  51.6 us
    all_to_all x1, blocking collectives, shards(): results = exchange(chip_sum, 'expert')  24 us
    all_to_all x1, blocking collectives, shards(): pieces = exchange(paired, 'z_0')  23.4 us
    all_to_all x1, blocking collectives, shards(): own = exchange(sent, 'expert')  18.2 us
    pallas_call x1, Pallas kernels, shards(): call(second_half_body, (shape((slots, width), bf16), shape((experts, chip...  5.56 us
    pallas_call x1, Pallas kernels, shards(): call(first_half_body, (acc, acc, ahead, ahead), (SMEM, VMEM, HBM, HBM), [...  4.7 us
    ppermute x1, starting transfers between devices, shards(): high = lax.ppermute(left, Z, [(z, (z - 1) % chips) for z in range(chips)])  3.21 us
    ppermute x1, waiting for transfers between devices, shards(): low = lax.ppermute(right, Z, [(z, (z + 1) % chips) for z in range(chips)])  2.94 us
  transfers between devices with their start and end apart: 4, of which 2 were waited for; matrix products, arithmetic and copies ran while one was open for 0% of the time, Pallas kernels for 4%

profile of v3, /device:TPU:40, one launch (start us, length us, event | category | flops | bytes accessed | tf_op | source)
XLA Modules:
  0.0 142.1 jit_solution(15668130145284315479)
XLA Ops:
  0.0 0.7 fusion.1
  0.7 0.7 select_reduce_fusion.1
  1.4 0.1 copy.15
  1.5 0.2 reduce_window_sum.11
  1.7 0.1 copy.16
  1.8 0.1 add_select_fusion
  1.8 0.2 fusion
  2.0 0.2 copy.17
  2.2 0.2 select_reduce_fusion.table_ref
  2.4 51.6 %all-gather = bf16[2048,128]{1,0:T(8,128)(2,1)S(1)} all-gather(bf16[128,128]{1,0:T(8,128)(2,1)} %param.6), channel_id=2, replica_groups=mesh['groups'=2,'expert'=4,'z_0'=8,'z_1'=2,'core'=2] {'z_0','z_1'}, dimensions={0}, use_global_device_ids=true | all-gather | bytes 557056 | tf_op jit(solution)/shard_map/all_gather | solution.py:203
  54.0 0.6 shard_map.64
  54.6 18.2 %all_to_all.15.x_ref = bf16[4,16,96,128]{3,2,1,0:T(8,128)(2,1)S(1)} all-to-all(bf16[4,16,96,128]{3,2,1,0:T(8,128)(2,1)S(1)} %shard_map.64), channel_id=1, replica_groups=mesh['groups'=2,'expert'=4,'z_0'=8,'z_1'=2,'core'=2] {'expert'}, dimensions={0} | all-to-all | bytes 3145728 | tf_op jit(solution)/shard_map/all_to_all | solution.py:207
  72.7 0.0 collective-permute-start
  72.7 4.7 %shard_map.65 = (f32[384,448]{1,0:T(8,128)S(1)}, f32[384,448]{1,0:T(8,128)S(1)}, bf16[448,1024]{1,0:T(8,128)(2,1)S(1)}, bf16[448,1024]{1,0:T(8,128)(2,1)S(1)}) custom-call(s32[1]{0:T(128)} %bitcast.1.core_ref, bf16[4,16,96,128]{3,2,1,0:T(8,128)(2,1)S(1)} %all_to_all.15.x_ref, bf16[448,4096]{1,0:T(8,128)(2,1)} %bitcast.13, bf16[448,4096]{1,0:T(8,128)(2,1)} %bitcast.15), custom_call_target="tpu_custom_call" | custom-call | flops 1409286144 | bytes 3523215 | tf_op jit(solution)/shard_map/pallas_call | solution.py:218
  77.4 0.0 collective-permute-done.x_ref
  77.4 5.6 %shard_map.66 = (bf16[384,448]{1,0:T(8,128)(2,1)S(1)}, bf16[4,16,96,128]{3,2,1,0:T(8,128)(2,1)S(1)}, bf16[448,2048]{1,0:T(8,128)(2,1)S(1)}) custom-call(s32[1]{0:T(128)} %bitcast.1.core_ref, bf16[4,16,96,128]{3,2,1,0:T(8,128)(2,1)S(1)} %collective-permute-done.x_ref, f32[384,448]{1,0:T(8,128)S(1)} %get-tuple-element.23.gate_ref, ...), custom_call_target="tpu_custom_call" | custom-call | flops 2113929216 | bytes 5284823 | tf_op jit(solution)/shard_map/pallas_call | solution.py:226
  83.0 0.6 collective-permute-start.1
  83.6 1.0 shard_map.67
  84.6 2.1 %collective-permute-done.1 = bf16[4,16,96,128]{3,2,1,0:T(8,128)(2,1)S(1)} collective-permute-done((bf16[4,16,96,128]{3,2,1,0:T(8,128)(2,1)S(1)}, bf16[4,16,96,128]{3,2,1,0:T(8,128)(2,1)S(1)}, u32[]{:S(2)}, u32[]{:S(2)}) %collective-permute-start.1) | collective-permute-done | bytes 1572896 | tf_op jit(solution)/shard_map/ppermute | solution.py:237
  86.7 0.5 add_convert_fusion
  87.2 24.0 %all_to_all.16.results_ref = bf16[4,16,96,128]{3,2,1,0:T(8,128)(2,1)S(1)} all-to-all(bf16[4,16,96,128]{3,2,1,0:T(8,128)(2,1)S(1)} %add_convert_fusion), channel_id=1, replica_groups=mesh['groups'=2,'expert'=4,'z_0'=8,'z_1'=2,'core'=2] {'expert'}, dimensions={0} | all-to-all | bytes 3145728 | tf_op jit(solution)/shard_map/all_to_all | solution.py:242
  111.2 0.4 shard_map.68
  111.7 0.1 collective-permute-start.2
  111.8 3.2 %collective-permute-start.3 = (bf16[4,128,128]{2,1,0:T(8,128)(2,1)S(1)}, bf16[4,128,128]{2,1,0:T(8,128)(2,1)S(1)}, u32[]{:S(2)}, u32[]{:S(2)}) collective-permute-start(bf16[4,128,128]{2,1,0:T(8,128)(2,1)S(1)} %get-tuple-element.32), channel_id=1, source_target_pairs={{0,30},{2,0},{4,2},{6,4},{8,6},{10,8},{12,10},{14,12},{16,14},{18,... | collective-permute-start | bytes 393224 | tf_op jit(solution)/shard_map/ppermute | solution.py:256
  115.0 2.9 %collective-permute-done.2.low_ref = bf16[4,128,128]{2,1,0:T(8,128)(2,1)S(1)} collective-permute-done((bf16[4,128,128]{2,1,0:T(8,128)(2,1)S(1)}, bf16[4,128,128]{2,1,0:T(8,128)(2,1)S(1)}, u32[]{:S(2)}, u32[]{:S(2)}) %collective-permute-start.2) | collective-permute-done | bytes 131104 | tf_op jit(solution)/shard_map/ppermute | solution.py:255
  118.0 0.0 collective-permute-done.3.high_ref
  118.0 0.1 shard_map.69
  118.0 23.4 %all_to_all.17 = bf16[8,128,128]{2,1,0:T(8,128)(2,1)S(1)} all-to-all(bf16[8,128,128]{2,1,0:T(8,128)(2,1)S(1)} %shard_map.69), channel_id=1, replica_groups=mesh['groups'=2,'expert'=4,'z_0'=8,'z_1'=2,'core'=2] {'z_0'}, dimensions={0} | all-to-all | bytes 524288 | tf_op jit(solution)/shard_map/all_to_all | solution.py:258
  141.4 0.7 reduce_sum.32
  (3 shorter events, 0.0 us)
Async XLA Ops:
  72.7 4.7 %collective-permute-start = (bf16[4,16,96,128]{3,2,1,0:T(8,128)(2,1)S(1)}, bf16[4,16,96,128]{3,2,1,0:T(8,128)(2,1)S(1)}, u32[]{:S(2)}, u32[]{:S(2)}) collective-permute-start(bf16[4,16,96,128]{3,2,1,0:T(8,128)(2,1)S(1)} %all_to_all.15.x_ref), channel_id=1, source_target_pairs={{0,1},{1,0},{2,3},{3,2},{4,5},{5,4},{6,7},{7,6},{8,9},{9,8},{10,11... | collective-permute-start | bytes 4718600 | tf_op jit(solution)/shard_map/ppermute | solution.py:208
  83.0 3.7 %collective-permute-start.1 = (bf16[4,16,96,128]{3,2,1,0:T(8,128)(2,1)S(1)}, bf16[4,16,96,128]{3,2,1,0:T(8,128)(2,1)S(1)}, u32[]{:S(2)}, u32[]{:S(2)}) collective-permute-start(bf16[4,16,96,128]{3,2,1,0:T(8,128)(2,1)S(1)} %get-tuple-element.29), channel_id=1, source_target_pairs={{0,1},{1,0},{2,3},{3,2},{4,5},{5,4},{6,7},{7,6},{8,9},{9,8},{10,11... | collective-permute-start | bytes 4718600 | tf_op jit(solution)/shard_map/ppermute | solution.py:237
  111.7 6.3 %collective-permute-start.2 = (bf16[4,128,128]{2,1,0:T(8,128)(2,1)S(1)}, bf16[4,128,128]{2,1,0:T(8,128)(2,1)S(1)}, u32[]{:S(2)}, u32[]{:S(2)}) collective-permute-start(bf16[4,128,128]{2,1,0:T(8,128)(2,1)S(1)} %get-tuple-element.31), channel_id=1, source_target_pairs={{0,2},{2,4},{4,6},{6,8},{8,10},{10,12},{12,14},{14,16},{16,18},{18... | collective-permute-start | bytes 393224 | tf_op jit(solution)/shard_map/ppermute | solution.py:255
  111.8 6.2 %collective-permute-start.3 = (bf16[4,128,128]{2,1,0:T(8,128)(2,1)S(1)}, bf16[4,128,128]{2,1,0:T(8,128)(2,1)S(1)}, u32[]{:S(2)}, u32[]{:S(2)}) collective-permute-start(bf16[4,128,128]{2,1,0:T(8,128)(2,1)S(1)} %get-tuple-element.32), channel_id=1, source_target_pairs={{0,30},{2,0},{4,2},{6,4},{8,6},{10,8},{12,10},{14,12},{16,14},{18,... | collective-permute-start | bytes 393224 | tf_op jit(solution)/shard_map/ppermute | solution.py:256

commit v4 on v3

v4 whole, which is shorter than its diff:
```python
import functools

import jax
import jax.numpy as jnp
from jax import lax
from jax.experimental import pallas as pl
from jax.experimental.pallas import tpu as pltpu
from jax.sharding import Mesh
from jax.sharding import PartitionSpec as P

CAP = 96
CORES = 2
Z = ("z_0", "z_1")
ETP = (*Z, "core")
LANES = 128
CHUNKS = 4
UNITS = 128
PARITIES = 2

HBM = pl.BlockSpec(memory_space=pltpu.HBM)
VMEM = pl.BlockSpec(memory_space=pltpu.VMEM)
SMEM = pl.BlockSpec(memory_space=pltpu.SMEM)


def dot32(a, b):
    return jnp.dot(a, b, preferred_element_type=jnp.float32)


def side_by_side(tiles):
    return jnp.concatenate([tile.reshape(-1, LANES) for tile in tiles], axis=1)


def slot_table(routes_ref, cap, experts, weight_of):
    tokens = routes_ref.shape[1]
    rows = -(-experts // 8) * 8
    expert = lax.broadcasted_iota(jnp.int32, (rows, tokens), 0)
    hit = (routes_ref[0:1, :] == expert) | (routes_ref[1:2, :] == expert)
    square = (tokens, tokens)
    earlier = lax.broadcasted_iota(jnp.int32, square, 0) < lax.broadcasted_iota(jnp.int32, square, 1)
    ones = [jnp.where(mask, 1.0, 0.0).astype(jnp.bfloat16) for mask in (hit, earlier)]
    slot = jnp.where(hit, dot32(*ones), -1.0).astype(jnp.int32)
    number = lax.broadcasted_iota(jnp.int32, (cap, tokens), 0)
    parts = [jnp.where(slot[e : e + 1, :] == number, weight_of(e), 0.0) for e in range(experts)]
    return jnp.concatenate(parts, axis=0).astype(jnp.bfloat16)


def dispatch_body(routes_ref, tokens_ref, out_ref):
    experts, chips, cap, lanes = out_ref.shape
    table = slot_table(routes_ref, cap, experts, lambda e: 1.0)
    for z in range(0, chips, 2):
        rows = dot32(table, side_by_side([tokens_ref[z], tokens_ref[z + 1]])).astype(out_ref.dtype)
        for k in range(2):
            out_ref[:, z + k] = rows[:, k * lanes : (k + 1) * lanes].reshape(experts, cap, lanes)


def row_copies(w_ref, buf, sems):
    width = w_ref.shape[0]
    spans = [pl.ds(k, min(UNITS, width - k)) for k in range(0, width, UNITS)]
    return [pltpu.make_async_copy(w_ref.at[span], buf.at[span], sems.at[i]) for i, span in enumerate(spans)]


def start_all(copies):
    for copy in copies:
        copy.start()


def wait_all(copies):
    for copy in copies:
        copy.wait()


def core_columns(ref, rows, core, start, count):
    return side_by_side(
        [ref[rows, pl.ds(pl.multiple_of((z * CORES + core) * LANES, LANES), LANES)] for z in range(start, start + count)]
    )


def up_partial(core, x_ref, gate_w, up_w, ready, emit):
    chips = x_ref.shape[1]
    width = gate_w.shape[0]
    x = side_by_side([x_ref[:, z] for z in range(chips)])
    for i, k in enumerate(range(0, width, UNITS)):
        rows = slice(k, min(k + UNITS, width))
        size = rows.stop - rows.start
        ready(i)
        both = jnp.concatenate([core_columns(w, rows, core, 0, chips) for w in (gate_w, up_w)], axis=0)
        part = lax.dot_general(x, both, (((1,), (1,)), ((), ())), preferred_element_type=jnp.float32)
        emit(rows, part[:, :size], part[:, size:])


def down_into(hidden, core, wd_ref, out_ref):
    blocks, chips, cap, lanes = out_ref.shape
    step = chips // CHUNKS
    for k in range(0, chips, step):
        part = dot32(hidden, core_columns(wd_ref, slice(None), core, k, step)).astype(out_ref.dtype)
        for z in range(step):
            out_ref[:, k + z] = part[:, z * lanes : (z + 1) * lanes].reshape(blocks, cap, lanes)


def first_half_body(
    core_ref, x_ref, routes_ref, weights_ref, wg_ref, wu_ref, gate_ref, up_ref, g_here, u_here, table_ref, sems
):
    gates = row_copies(wg_ref, g_here, sems.at[0])
    ups = row_copies(wu_ref, u_here, sems.at[1])
    for pair in zip(gates, ups):
        start_all(pair)

    def weight_of(e):
        return sum(jnp.where(routes_ref[k : k + 1, :] == e, weights_ref[k : k + 1, :], 0.0) for k in range(2))

    table_ref[...] = slot_table(routes_ref, x_ref.shape[2], x_ref.shape[0], weight_of).T

    def ready(i):
        wait_all((gates[i], ups[i]))

    def emit(rows, gate, up):
        gate_ref[:, rows], up_ref[:, rows] = gate, up

    up_partial(core_ref[0], x_ref, g_here, u_here, ready, emit)


def second_half_body(
    core_ref, x_ref, gate_ref, up_ref, g_here, u_here, wd_ref, hidden_ref, out_ref, d_here, sems
):
    other = 1 - core_ref[0]
    downs = row_copies(wd_ref, d_here, sems)
    start_all(downs)

    def emit(rows, gate, up):
        gate = gate + gate_ref[:, rows]
        up = up + up_ref[:, rows]
        hidden_ref[:, rows] = (gate / (1.0 + jnp.exp(-gate)) * up).astype(hidden_ref.dtype)

    up_partial(other, x_ref, g_here, u_here, lambda i: None, emit)
    wait_all(downs)
    down_into(hidden_ref[...], other, d_here, out_ref)


def own_down_body(core_ref, hidden_ref, d_here, out_ref):
    down_into(hidden_ref[...], core_ref[0], d_here, out_ref)


def combine_body(parity_ref, table_ref, results_ref, own_ref, right_ref, left_ref):
    parity = parity_ref[0]
    table = table_ref[...]
    half = right_ref.shape[0]

    def rows_of(chip):
        return results_ref[:, chip].reshape(-1, LANES)

    for k in range(2 * half):
        mine, other = rows_of(PARITIES * k + parity), rows_of(PARITIES * k + 1 - parity)
        rows = dot32(table, jnp.concatenate([mine, other], axis=1)).astype(own_ref.dtype)
        own_ref[k] = rows[:, :LANES]
        (right_ref if k < half else left_ref)[k % half] = rows[:, LANES:]


def chip_pair_body(own_ref, low_ref, high_ref, out_ref):
    half = low_ref.shape[0]
    for part, ref in enumerate((low_ref, high_ref)):
        rows = pl.ds(part * half, half)
        out_ref[rows] = (own_ref[rows].astype(jnp.float32) + ref[...].astype(jnp.float32)).astype(out_ref.dtype)


def call(body, out_shape, in_specs, scratch=(), flops=0):
    outs = jax.tree.map(lambda _: VMEM, out_shape)
    return pl.pallas_call(
        body,
        out_shape=out_shape,
        in_specs=list(in_specs),
        out_specs=outs,
        scratch_shapes=list(scratch),
        cost_estimate=pl.CostEstimate(flops=flops, transcendentals=0, bytes_accessed=flops // 400),
        compiler_params=pltpu.CompilerParams(vmem_limit_bytes=24 * 1024 * 1024),
    )


def shards(tokens, route_ids, gate_weights, w_gate, w_up, w_down):
    experts = lax.axis_size("expert")
    chips = lax.axis_size(Z)
    token_count, lanes = tokens.shape
    slots = experts * CAP
    _, width_in, width = w_gate.shape
    bf16, f32 = jnp.bfloat16, jnp.float32
    shape = jax.ShapeDtypeStruct

    routes, weights = route_ids.T, gate_weights.T
    core = lax.axis_index("core").astype(jnp.int32).reshape(1)
    parity = lax.axis_index("z_1").astype(jnp.int32).reshape(1)
    tokens, core, parity = lax.optimization_barrier((tokens, core, parity))

    swap = functools.partial(lax.ppermute, axis_name="core", perm=[(0, 1), (1, 0)])
    exchange = functools.partial(lax.all_to_all, split_axis=0, concat_axis=0, tiled=True)

    gathered = lax.all_gather(tokens, Z, axis=0, tiled=False)
    sent = call(
        dispatch_body, shape((experts, chips, CAP, lanes), bf16), (VMEM, VMEM), flops=2 * slots * token_count * chips * lanes
    )(routes, gathered)
    own = exchange(sent, "expert")
    other = swap(own)

    gate_rows, up_rows, down_rows = (
        pltpu.with_memory_space_constraint(w, pltpu.HBM)
        for w in (jnp.swapaxes(w_gate[0], 0, 1), jnp.swapaxes(w_up[0], 0, 1), w_down[0])
    )
    up_flops = 2 * slots * width * width_in
    acc = shape((slots, width), f32)
    held = shape((width, width_in), bf16)
    copies = len(range(0, width, UNITS))
    gate_half, up_half, gate_here, up_here, combine_table = call(
        first_half_body,
        (acc, acc, held, held, shape((token_count, slots), bf16)),
        (SMEM, VMEM, VMEM, VMEM, HBM, HBM),
        [pltpu.SemaphoreType.DMA((2, copies))],
        flops=up_flops,
    )(core, own, routes, weights, gate_rows, up_rows)
    hidden, theirs, down_here = call(
        second_half_body,
        (shape((slots, width), bf16), shape((experts, chips, CAP, lanes), bf16), held),
        (SMEM, VMEM, VMEM, VMEM, VMEM, VMEM, HBM),
        [pltpu.SemaphoreType.DMA((copies,))],
        flops=up_flops * 3 // 2,
    )(core, other, gate_half, up_half, gate_here, up_here, down_rows)
    arrived = swap(theirs)
    mine = call(own_down_body, shape((experts, chips, CAP, lanes), f32), (SMEM, VMEM, VMEM), flops=up_flops // 2)(
        core, hidden, down_here
    )
    chip_sum = (mine + arrived.astype(f32)).astype(bf16)
    results = exchange(chip_sum, "expert")

    of_parity = chips // PARITIES

    def block(count):
        return shape((count, token_count, lanes), bf16)

    blended, right, left = call(
        combine_body,
        (block(of_parity), block(of_parity // 2), block(of_parity // 2)),
        (SMEM, VMEM, VMEM),
        flops=2 * slots * token_count * chips * lanes,
    )(parity, combine_table, results)
    low = lax.ppermute(right, Z, [(z, (z + 1) % chips) for z in range(chips)])
    high = lax.ppermute(left, Z, [(z, (z - 1) % chips) for z in range(chips)])
    paired = call(chip_pair_body, block(of_parity), (VMEM, VMEM, VMEM))(blended, low, high)
    pieces = exchange(paired, "z_0")
    return pieces.astype(f32).sum(axis=0).astype(bf16)


def solution(mesh):
    groups, experts, etp = (mesh.shape[name] for name in ("groups", "expert", "etp"))
    finer = Mesh(
        mesh.devices.reshape(groups, experts, etp // (CORES * PARITIES), PARITIES, CORES),
        ("groups", "expert", *ETP),
    )
    placed = (
        P(("groups", "expert"), ETP),
        P(("groups", "expert"), None),
        P(("groups", "expert"), None),
        P("expert", None, ETP),
        P("expert", None, ETP),
        P("expert", ETP, None),
    )
    return jax.shard_map(
        shards, mesh=finer, in_specs=placed, out_specs=P(("groups", "expert"), ETP), check_vma=False
    )
```

time: 142 us -> 141 us (level)
  other arithmetic: 3.25 us -> 1.09 us
  transfers between devices with their start and end apart: 4 -> 4, of which waited for: 2 -> 2; matrix products, arithmetic and copies ran while one was open for 0% -> 0% of each run, Pallas kernels for 4% -> 5%
where the time goes in v4:
time: 141 us
  blocking collectives  117 us (83%)
  Pallas kernels  12.6 us (9%)
  waiting for transfers between devices  4.93 us (3%)
  starting transfers between devices  3.96 us (3%)
    all_gather x1, blocking collectives, shards(): gathered = lax.all_gather(tokens, Z, axis=0, tiled=False)  51.7 us
    all_to_all x1, blocking collectives, shards(): results = exchange(chip_sum, 'expert')  24 us
    all_to_all x1, blocking collectives, shards(): pieces = exchange(paired, 'z_0')  23.4 us
    all_to_all x1, blocking collectives, shards(): own = exchange(sent, 'expert')  18.2 us
    pallas_call x1, Pallas kernels, shards(): call(first_half_body, (acc, acc, held, held, shape((token_count, slots),...  5.63 us
    pallas_call x1, Pallas kernels, shards(): call(second_half_body, (shape((slots, width), bf16), shape((experts, chip...  4.77 us
    ppermute x1, starting transfers between devices, shards(): high = lax.ppermute(left, Z, [(z, (z - 1) % chips) for z in range(chips)])  3.21 us
    ppermute x1, waiting for transfers between devices, shards(): low = lax.ppermute(right, Z, [(z, (z + 1) % chips) for z in range(chips)])  2.94 us
  transfers between devices with their start and end apart: 4, of which 2 were waited for; matrix products, arithmetic and copies ran while one was open for 0% of the time, Pallas kernels for 5%

profile of v4, /device:TPU:40, one launch (start us, length us, event | category | flops | bytes accessed | tf_op | source)
XLA Modules:
  0.0 140.6 jit_solution(14393688105380491939)
XLA Ops:
  0.0 0.0 copy-start.1
  0.0 51.7 %all-gather = bf16[2048,128]{1,0:T(8,128)(2,1)S(1)} all-gather(bf16[128,128]{1,0:T(8,128)(2,1)} %param.6), channel_id=2, replica_groups=mesh['groups'=2,'expert'=4,'z_0'=8,'z_1'=2,'core'=2] {'z_0','z_1'}, dimensions={0}, use_global_device_ids=true | all-gather | bytes 557056 | tf_op jit(solution)/shard_map/all_gather | solution.py:195
  51.7 0.0 copy-start
  51.7 0.7 copy-done
  52.4 0.7 shard_map.64
  53.0 18.2 %all_to_all.15.x_ref = bf16[4,16,96,128]{3,2,1,0:T(8,128)(2,1)S(1)} all-to-all(bf16[4,16,96,128]{3,2,1,0:T(8,128)(2,1)S(1)} %shard_map.64), channel_id=1, replica_groups=mesh['groups'=2,'expert'=4,'z_0'=8,'z_1'=2,'core'=2] {'expert'}, dimensions={0} | all-to-all | bytes 3145728 | tf_op jit(solution)/shard_map/all_to_all | solution.py:199
  71.2 0.0 collective-permute-start
  71.2 0.0 copy-done.1
  71.2 5.6 %shard_map.65 = (f32[384,448]{1,0:T(8,128)S(1)}, f32[384,448]{1,0:T(8,128)S(1)}, bf16[448,4096]{1,0:T(8,128)(2,1)S(1)}, bf16[448,4096]{1,0:T(8,128)(2,1)S(1)}, bf16[128,384]{1,0:T(8,128)(2,1)S(1)}) custom-call(s32[1]{0:T(128)} %bitcast.core_ref, bf16[4,16,96,128]{3,2,1,0:T(8,128)(2,1)S(1)} %all_to_all.15.x_ref, s32[2,128]{1,0:T(2,128)S(1)} %bitcast.14, ...), custom_call_target="tpu_custom_call" | custom-call | flops 1409286144 | bytes 3523215 | tf_op jit(solution)/shard_map/pallas_call | solution.py:210
  76.8 0.0 collective-permute-done.x_ref
  76.9 4.8 %shard_map.66 = (bf16[384,448]{1,0:T(8,128)(2,1)S(1)}, bf16[4,16,96,128]{3,2,1,0:T(8,128)(2,1)S(1)}, bf16[448,4096]{1,0:T(8,128)(2,1)S(1)}) custom-call(s32[1]{0:T(128)} %bitcast.core_ref, bf16[4,16,96,128]{3,2,1,0:T(8,128)(2,1)S(1)} %collective-permute-done.x_ref, f32[384,448]{1,0:T(8,128)S(1)} %get-tuple-element.23.gate_ref, ...), custom_call_target="tpu_custom_call" | custom-call | flops 2113929216 | bytes 5284823 | tf_op jit(solution)/shard_map/pallas_call | solution.py:217
  81.6 0.6 collective-permute-start.1
  82.2 1.1 shard_map.67
  83.3 2.0 %collective-permute-done.1 = bf16[4,16,96,128]{3,2,1,0:T(8,128)(2,1)S(1)} collective-permute-done((bf16[4,16,96,128]{3,2,1,0:T(8,128)(2,1)S(1)}, bf16[4,16,96,128]{3,2,1,0:T(8,128)(2,1)S(1)}, u32[]{:S(2)}, u32[]{:S(2)}) %collective-permute-start.1) | collective-permute-done | bytes 1572896 | tf_op jit(solution)/shard_map/ppermute | solution.py:224
  85.3 0.4 add_convert_fusion
  85.7 24.0 %all_to_all.16.results_ref = bf16[4,16,96,128]{3,2,1,0:T(8,128)(2,1)S(1)} all-to-all(bf16[4,16,96,128]{3,2,1,0:T(8,128)(2,1)S(1)} %add_convert_fusion), channel_id=1, replica_groups=mesh['groups'=2,'expert'=4,'z_0'=8,'z_1'=2,'core'=2] {'expert'}, dimensions={0} | all-to-all | bytes 3145728 | tf_op jit(solution)/shard_map/all_to_all | solution.py:229
  109.7 0.4 shard_map.68
  110.2 0.1 collective-permute-start.2
  110.3 3.2 %collective-permute-start.3 = (bf16[4,128,128]{2,1,0:T(8,128)(2,1)S(1)}, bf16[4,128,128]{2,1,0:T(8,128)(2,1)S(1)}, u32[]{:S(2)}, u32[]{:S(2)}) collective-permute-start(bf16[4,128,128]{2,1,0:T(8,128)(2,1)S(1)} %get-tuple-element.32), channel_id=1, source_target_pairs={{0,30},{2,0},{4,2},{6,4},{8,6},{10,8},{12,10},{14,12},{16,14},{18,... | collective-permute-start | bytes 393224 | tf_op jit(solution)/shard_map/ppermute | solution.py:243
  113.5 2.9 %collective-permute-done.2.low_ref = bf16[4,128,128]{2,1,0:T(8,128)(2,1)S(1)} collective-permute-done((bf16[4,128,128]{2,1,0:T(8,128)(2,1)S(1)}, bf16[4,128,128]{2,1,0:T(8,128)(2,1)S(1)}, u32[]{:S(2)}, u32[]{:S(2)}) %collective-permute-start.2) | collective-permute-done | bytes 131104 | tf_op jit(solution)/shard_map/ppermute | solution.py:242
  116.5 0.0 collective-permute-done.3.high_ref
  116.5 0.1 shard_map.69
  116.5 23.4 %all_to_all.17 = bf16[8,128,128]{2,1,0:T(8,128)(2,1)S(1)} all-to-all(bf16[8,128,128]{2,1,0:T(8,128)(2,1)S(1)} %shard_map.69), channel_id=1, replica_groups=mesh['groups'=2,'expert'=4,'z_0'=8,'z_1'=2,'core'=2] {'z_0'}, dimensions={0} | all-to-all | bytes 524288 | tf_op jit(solution)/shard_map/all_to_all | solution.py:245
  139.9 0.7 reduce_sum.12
Async XLA Ops:
  0.0 71.2 %copy-start.1 = (f32[128,2]{0,1:T(2,128)S(1)}, f32[128,2]{0,1:T(2,128)}, u32[]{:S(2)}) copy-start(f32[128,2]{0,1:T(2,128)} %param.8) | copy-start | bytes 3076
  51.7 0.7 copy-start
  71.2 5.6 %collective-permute-start = (bf16[4,16,96,128]{3,2,1,0:T(8,128)(2,1)S(1)}, bf16[4,16,96,128]{3,2,1,0:T(8,128)(2,1)S(1)}, u32[]{:S(2)}, u32[]{:S(2)}) collective-permute-start(bf16[4,16,96,128]{3,2,1,0:T(8,128)(2,1)S(1)} %all_to_all.15.x_ref), channel_id=1, source_target_pairs={{0,1},{1,0},{2,3},{3,2},{4,5},{5,4},{6,7},{7,6},{8,9},{9,8},{10,11... | collective-permute-start | bytes 4718600 | tf_op jit(solution)/shard_map/ppermute | solution.py:200
  81.6 3.7 %collective-permute-start.1 = (bf16[4,16,96,128]{3,2,1,0:T(8,128)(2,1)S(1)}, bf16[4,16,96,128]{3,2,1,0:T(8,128)(2,1)S(1)}, u32[]{:S(2)}, u32[]{:S(2)}) collective-permute-start(bf16[4,16,96,128]{3,2,1,0:T(8,128)(2,1)S(1)} %get-tuple-element.29), channel_id=1, source_target_pairs={{0,1},{1,0},{2,3},{3,2},{4,5},{5,4},{6,7},{7,6},{8,9},{9,8},{10,11... | collective-permute-start | bytes 4718600 | tf_op jit(solution)/shard_map/ppermute | solution.py:224
  110.2 6.3 %collective-permute-start.2 = (bf16[4,128,128]{2,1,0:T(8,128)(2,1)S(1)}, bf16[4,128,128]{2,1,0:T(8,128)(2,1)S(1)}, u32[]{:S(2)}, u32[]{:S(2)}) collective-permute-start(bf16[4,128,128]{2,1,0:T(8,128)(2,1)S(1)} %get-tuple-element.31), channel_id=1, source_target_pairs={{0,2},{2,4},{4,6},{6,8},{8,10},{10,12},{12,14},{14,16},{16,18},{18... | collective-permute-start | bytes 393224 | tf_op jit(solution)/shard_map/ppermute | solution.py:242
  110.3 6.2 %collective-permute-start.3 = (bf16[4,128,128]{2,1,0:T(8,128)(2,1)S(1)}, bf16[4,128,128]{2,1,0:T(8,128)(2,1)S(1)}, u32[]{:S(2)}, u32[]{:S(2)}) collective-permute-start(bf16[4,128,128]{2,1,0:T(8,128)(2,1)S(1)} %get-tuple-element.32), channel_id=1, source_target_pairs={{0,30},{2,0},{4,2},{6,4},{8,6},{10,8},{12,10},{14,12},{16,14},{18,... | collective-permute-start | bytes 393224 | tf_op jit(solution)/shard_map/ppermute | solution.py:243

commit v5 on v4

--- a/solution.py
+++ b/solution.py
@@ -14,7 +14,6 @@
 ETP = (*Z, "core")
 LANES = 128
 CHUNKS = 4
-UNITS = 128
 PARITIES = 2
 
 HBM = pl.BlockSpec(memory_space=pltpu.HBM)
@@ -53,10 +52,10 @@
             out_ref[:, z + k] = rows[:, k * lanes : (k + 1) * lanes].reshape(experts, cap, lanes)
 
 
-def row_copies(w_ref, buf, sems):
-    width = w_ref.shape[0]
-    spans = [pl.ds(k, min(UNITS, width - k)) for k in range(0, width, UNITS)]
-    return [pltpu.make_async_copy(w_ref.at[span], buf.at[span], sems.at[i]) for i, span in enumerate(spans)]
+def column_copies(w_ref, buf, sems):
+    step = w_ref.shape[1] // CHUNKS
+    spans = [pl.ds(k * step, step) for k in range(CHUNKS)]
+    return [pltpu.make_async_copy(w_ref.at[:, span], buf.at[:, span], sems.at[i]) for i, span in enumerate(spans)]
 
 
 def start_all(copies):
@@ -69,39 +68,42 @@
         copy.wait()
 
 
-def core_columns(ref, rows, core, start, count):
+def core_columns(ref, core, start, count):
     return side_by_side(
-        [ref[rows, pl.ds(pl.multiple_of((z * CORES + core) * LANES, LANES), LANES)] for z in range(start, start + count)]
-    )
-
-
-def up_partial(core, x_ref, gate_w, up_w, ready, emit):
-    chips = x_ref.shape[1]
-    width = gate_w.shape[0]
-    x = side_by_side([x_ref[:, z] for z in range(chips)])
-    for i, k in enumerate(range(0, width, UNITS)):
-        rows = slice(k, min(k + UNITS, width))
-        size = rows.stop - rows.start
-        ready(i)
-        both = jnp.concatenate([core_columns(w, rows, core, 0, chips) for w in (gate_w, up_w)], axis=0)
-        part = lax.dot_general(x, both, (((1,), (1,)), ((), ())), preferred_element_type=jnp.float32)
-        emit(rows, part[:, :size], part[:, size:])
-
-
-def down_into(hidden, core, wd_ref, out_ref):
+        [ref[:, pl.ds(pl.multiple_of((z * CORES + core) * LANES, LANES), LANES)] for z in range(start, start + count)]
+    )
+
+
+def up_partial(core, x_ref, w_refs, ready):
+    step = x_ref.shape[1] // CHUNKS
+    sums = [None] * len(w_refs)
+    for k in range(CHUNKS):
+        ready(k)
+        x = side_by_side([x_ref[:, z] for z in range(k * step, (k + 1) * step)])
+        for i, w in enumerate(w_refs):
+            part = lax.dot_general(
+                x, core_columns(w, core, k * step, step), (((1,), (1,)), ((), ())), preferred_element_type=jnp.float32
+            )
+            sums[i] = part if k == 0 else sums[i] + part
+    return sums
+
+
+def down_into(hidden, core, wd_ref, out_ref, ready=None):
     blocks, chips, cap, lanes = out_ref.shape
     step = chips // CHUNKS
-    for k in range(0, chips, step):
-        part = dot32(hidden, core_columns(wd_ref, slice(None), core, k, step)).astype(out_ref.dtype)
+    for k in range(CHUNKS):
+        if ready is not None:
+            ready(k)
+        part = dot32(hidden, core_columns(wd_ref, core, k * step, step)).astype(out_ref.dtype)
         for z in range(step):
-            out_ref[:, k + z] = part[:, z * lanes : (z + 1) * lanes].reshape(blocks, cap, lanes)
+            out_ref[:, k * step + z] = part[:, z * lanes : (z + 1) * lanes].reshape(blocks, cap, lanes)
 
 
 def first_half_body(
     core_ref, x_ref, routes_ref, weights_ref, wg_ref, wu_ref, gate_ref, up_ref, g_here, u_here, table_ref, sems
 ):
-    gates = row_copies(wg_ref, g_here, sems.at[0])
-    ups = row_copies(wu_ref, u_here, sems.at[1])
+    gates = column_copies(wg_ref, g_here, sems.at[0])
+    ups = column_copies(wu_ref, u_here, sems.at[1])
     for pair in zip(gates, ups):
         start_all(pair)
 
@@ -110,30 +112,23 @@
 
     table_ref[...] = slot_table(routes_ref, x_ref.shape[2], x_ref.shape[0], weight_of).T
 
-    def ready(i):
-        wait_all((gates[i], ups[i]))
-
-    def emit(rows, gate, up):
-        gate_ref[:, rows], up_ref[:, rows] = gate, up
-
-    up_partial(core_ref[0], x_ref, g_here, u_here, ready, emit)
+    gate_ref[...], up_ref[...] = up_partial(
+        core_ref[0], x_ref, (g_here, u_here), lambda k: wait_all((gates[k], ups[k]))
+    )
 
 
 def second_half_body(
     core_ref, x_ref, gate_ref, up_ref, g_here, u_here, wd_ref, hidden_ref, out_ref, d_here, sems
 ):
     other = 1 - core_ref[0]
-    downs = row_copies(wd_ref, d_here, sems)
+    downs = column_copies(wd_ref, d_here, sems)
     start_all(downs)
-
-    def emit(rows, gate, up):
-        gate = gate + gate_ref[:, rows]
-        up = up + up_ref[:, rows]
-        hidden_ref[:, rows] = (gate / (1.0 + jnp.exp(-gate)) * up).astype(hidden_ref.dtype)
-
-    up_partial(other, x_ref, g_here, u_here, lambda i: None, emit)
-    wait_all(downs)
-    down_into(hidden_ref[...], other, d_here, out_ref)
+    gate, up = up_partial(other, x_ref, (g_here, u_here), lambda k: None)
+    gate = gate + gate_ref[...]
+    up = up + up_ref[...]
+    hidden = (gate / (1.0 + jnp.exp(-gate)) * up).astype(hidden_ref.dtype)
+    hidden_ref[...] = hidden
+    down_into(hidden, other, d_here, out_ref, lambda k: downs[k].wait())
 
 
 def own_down_body(core_ref, hidden_ref, d_here, out_ref):
@@ -206,19 +201,18 @@
     up_flops = 2 * slots * width * width_in
     acc = shape((slots, width), f32)
     held = shape((width, width_in), bf16)
-    copies = len(range(0, width, UNITS))
     gate_half, up_half, gate_here, up_here, combine_table = call(
         first_half_body,
         (acc, acc, held, held, shape((token_count, slots), bf16)),
         (SMEM, VMEM, VMEM, VMEM, HBM, HBM),
-        [pltpu.SemaphoreType.DMA((2, copies))],
+        [pltpu.SemaphoreType.DMA((2, CHUNKS))],
         flops=up_flops,
     )(core, own, routes, weights, gate_rows, up_rows)
     hidden, theirs, down_here = call(
         second_half_body,
         (shape((slots, width), bf16), shape((experts, chips, CAP, lanes), bf16), held),
         (SMEM, VMEM, VMEM, VMEM, VMEM, VMEM, HBM),
-        [pltpu.SemaphoreType.DMA((copies,))],
+        [pltpu.SemaphoreType.DMA((CHUNKS,))],
         flops=up_flops * 3 // 2,
     )(core, other, gate_half, up_half, gate_here, up_here, down_rows)
     arrived = swap(theirs)

time: 141 us -> 139 us (0.986)
  Pallas kernels: 12.6 us -> 11 us
    pallas_call x1, Pallas kernels: 5.63 us -> 4.09 us  [shards(): call(first_half_body, (acc, acc, held, held, shape((token_count, slots),...]
  transfers between devices with their start and end apart: 4 -> 4, of which waited for: 2 -> 2; matrix products, arithmetic and copies ran while one was open for 0% -> 0% of each run, Pallas kernels for 5% -> 4%
where the time goes in v5:
time: 139 us
  blocking collectives  117 us (84%)
  Pallas kernels  11 us (8%)
  waiting for transfers between devices  4.93 us (4%)
  starting transfers between devices  3.97 us (3%)
    all_gather x1, blocking collectives, shards(): gathered = lax.all_gather(tokens, Z, axis=0, tiled=False)  51.7 us
    all_to_all x1, blocking collectives, shards(): results = exchange(chip_sum, 'expert')  24 us
    all_to_all x1, blocking collectives, shards(): pieces = exchange(paired, 'z_0')  23.4 us
    all_to_all x1, blocking collectives, shards(): own = exchange(sent, 'expert')  18.2 us
    pallas_call x1, Pallas kernels, shards(): call(second_half_body, (shape((slots, width), bf16), shape((experts, chip...  4.64 us
    pallas_call x1, Pallas kernels, shards(): call(first_half_body, (acc, acc, held, held, shape((token_count, slots),...  4.09 us
    ppermute x1, starting transfers between devices, shards(): high = lax.ppermute(left, Z, [(z, (z - 1) % chips) for z in range(chips)])  3.21 us
    ppermute x1, waiting for transfers between devices, shards(): low = lax.ppermute(right, Z, [(z, (z + 1) % chips) for z in range(chips)])  2.94 us
  transfers between devices with their start and end apart: 4, of which 2 were waited for; matrix products, arithmetic and copies ran while one was open for 0% of the time, Pallas kernels for 4%

profile of v5, /device:TPU:40, one launch (start us, length us, event | category | flops | bytes accessed | tf_op | source)
XLA Modules:
  0.0 138.9 jit_solution(2838457542968475986)
XLA Ops:
  0.0 0.0 copy-start.1
  0.0 51.7 %all-gather = bf16[2048,128]{1,0:T(8,128)(2,1)S(1)} all-gather(bf16[128,128]{1,0:T(8,128)(2,1)} %param.6), channel_id=2, replica_groups=mesh['groups'=2,'expert'=4,'z_0'=8,'z_1'=2,'core'=2] {'z_0','z_1'}, dimensions={0}, use_global_device_ids=true | all-gather | bytes 557056 | tf_op jit(solution)/shard_map/all_gather | solution.py:190
  51.7 0.0 copy-start
  51.7 0.7 copy-done
  52.4 0.7 shard_map.64
  53.0 18.2 %all_to_all.15.x_ref = bf16[4,16,96,128]{3,2,1,0:T(8,128)(2,1)S(1)} all-to-all(bf16[4,16,96,128]{3,2,1,0:T(8,128)(2,1)S(1)} %shard_map.64), channel_id=1, replica_groups=mesh['groups'=2,'expert'=4,'z_0'=8,'z_1'=2,'core'=2] {'expert'}, dimensions={0} | all-to-all | bytes 3145728 | tf_op jit(solution)/shard_map/all_to_all | solution.py:194
  71.2 0.0 collective-permute-start
  71.2 0.0 copy-done.1
  71.2 4.1 %shard_map.65 = (f32[384,448]{1,0:T(8,128)S(1)}, f32[384,448]{1,0:T(8,128)S(1)}, bf16[448,4096]{1,0:T(8,128)(2,1)S(1)}, bf16[448,4096]{1,0:T(8,128)(2,1)S(1)}, bf16[128,384]{1,0:T(8,128)(2,1)S(1)}) custom-call(s32[1]{0:T(128)} %bitcast.core_ref, bf16[4,16,96,128]{3,2,1,0:T(8,128)(2,1)S(1)} %all_to_all.15.x_ref, s32[2,128]{1,0:T(2,128)S(1)} %bitcast.14, ...), custom_call_target="tpu_custom_call" | custom-call | flops 1409286144 | bytes 3523215 | tf_op jit(solution)/shard_map/pallas_call | solution.py:204
  75.3 0.0 collective-permute-done.x_ref
  75.3 4.6 %shard_map.66 = (bf16[384,448]{1,0:T(8,128)(2,1)S(1)}, bf16[4,16,96,128]{3,2,1,0:T(8,128)(2,1)S(1)}, bf16[448,4096]{1,0:T(8,128)(2,1)S(1)}) custom-call(s32[1]{0:T(128)} %bitcast.core_ref, bf16[4,16,96,128]{3,2,1,0:T(8,128)(2,1)S(1)} %collective-permute-done.x_ref, f32[384,448]{1,0:T(8,128)S(1)} %get-tuple-element.23.gate_ref, ...), custom_call_target="tpu_custom_call" | custom-call | flops 2113929216 | bytes 5284823 | tf_op jit(solution)/shard_map/pallas_call | solution.py:211
  80.0 0.6 collective-permute-start.1
  80.6 1.0 shard_map.67
  81.6 2.0 %collective-permute-done.1 = bf16[4,16,96,128]{3,2,1,0:T(8,128)(2,1)S(1)} collective-permute-done((bf16[4,16,96,128]{3,2,1,0:T(8,128)(2,1)S(1)}, bf16[4,16,96,128]{3,2,1,0:T(8,128)(2,1)S(1)}, u32[]{:S(2)}, u32[]{:S(2)}) %collective-permute-start.1) | collective-permute-done | bytes 1572896 | tf_op jit(solution)/shard_map/ppermute | solution.py:218
  83.6 0.4 add_convert_fusion
  84.1 24.0 %all_to_all.16.results_ref = bf16[4,16,96,128]{3,2,1,0:T(8,128)(2,1)S(1)} all-to-all(bf16[4,16,96,128]{3,2,1,0:T(8,128)(2,1)S(1)} %add_convert_fusion), channel_id=1, replica_groups=mesh['groups'=2,'expert'=4,'z_0'=8,'z_1'=2,'core'=2] {'expert'}, dimensions={0} | all-to-all | bytes 3145728 | tf_op jit(solution)/shard_map/all_to_all | solution.py:223
  108.1 0.4 shard_map.68
  108.5 0.1 collective-permute-start.2
  108.7 3.2 %collective-permute-start.3 = (bf16[4,128,128]{2,1,0:T(8,128)(2,1)S(1)}, bf16[4,128,128]{2,1,0:T(8,128)(2,1)S(1)}, u32[]{:S(2)}, u32[]{:S(2)}) collective-permute-start(bf16[4,128,128]{2,1,0:T(8,128)(2,1)S(1)} %get-tuple-element.32), channel_id=1, source_target_pairs={{0,30},{2,0},{4,2},{6,4},{8,6},{10,8},{12,10},{14,12},{16,14},{18,... | collective-permute-start | bytes 393224 | tf_op jit(solution)/shard_map/ppermute | solution.py:237
  111.9 2.9 %collective-permute-done.2.low_ref = bf16[4,128,128]{2,1,0:T(8,128)(2,1)S(1)} collective-permute-done((bf16[4,128,128]{2,1,0:T(8,128)(2,1)S(1)}, bf16[4,128,128]{2,1,0:T(8,128)(2,1)S(1)}, u32[]{:S(2)}, u32[]{:S(2)}) %collective-permute-start.2) | collective-permute-done | bytes 131104 | tf_op jit(solution)/shard_map/ppermute | solution.py:236
  114.8 0.0 collective-permute-done.3.high_ref
  114.8 0.1 shard_map.69
  114.9 23.4 %all_to_all.17 = bf16[8,128,128]{2,1,0:T(8,128)(2,1)S(1)} all-to-all(bf16[8,128,128]{2,1,0:T(8,128)(2,1)S(1)} %shard_map.69), channel_id=1, replica_groups=mesh['groups'=2,'expert'=4,'z_0'=8,'z_1'=2,'core'=2] {'z_0'}, dimensions={0} | all-to-all | bytes 524288 | tf_op jit(solution)/shard_map/all_to_all | solution.py:239
  138.3 0.7 reduce_sum.12
Async XLA Ops:
  0.0 71.2 %copy-start.1 = (f32[128,2]{0,1:T(2,128)S(1)}, f32[128,2]{0,1:T(2,128)}, u32[]{:S(2)}) copy-start(f32[128,2]{0,1:T(2,128)} %param.8) | copy-start | bytes 3076
  51.7 0.7 copy-start
  71.2 4.1 %collective-permute-start = (bf16[4,16,96,128]{3,2,1,0:T(8,128)(2,1)S(1)}, bf16[4,16,96,128]{3,2,1,0:T(8,128)(2,1)S(1)}, u32[]{:S(2)}, u32[]{:S(2)}) collective-permute-start(bf16[4,16,96,128]{3,2,1,0:T(8,128)(2,1)S(1)} %all_to_all.15.x_ref), channel_id=1, source_target_pairs={{0,1},{1,0},{2,3},{3,2},{4,5},{5,4},{6,7},{7,6},{8,9},{9,8},{10,11... | collective-permute-start | bytes 4718600 | tf_op jit(solution)/shard_map/ppermute | solution.py:195
  80.0 3.7 %collective-permute-start.1 = (bf16[4,16,96,128]{3,2,1,0:T(8,128)(2,1)S(1)}, bf16[4,16,96,128]{3,2,1,0:T(8,128)(2,1)S(1)}, u32[]{:S(2)}, u32[]{:S(2)}) collective-permute-start(bf16[4,16,96,128]{3,2,1,0:T(8,128)(2,1)S(1)} %get-tuple-element.29), channel_id=1, source_target_pairs={{0,1},{1,0},{2,3},{3,2},{4,5},{5,4},{6,7},{7,6},{8,9},{9,8},{10,11... | collective-permute-start | bytes 4718600 | tf_op jit(solution)/shard_map/ppermute | solution.py:218
  108.5 6.3 %collective-permute-start.2 = (bf16[4,128,128]{2,1,0:T(8,128)(2,1)S(1)}, bf16[4,128,128]{2,1,0:T(8,128)(2,1)S(1)}, u32[]{:S(2)}, u32[]{:S(2)}) collective-permute-start(bf16[4,128,128]{2,1,0:T(8,128)(2,1)S(1)} %get-tuple-element.31), channel_id=1, source_target_pairs={{0,2},{2,4},{4,6},{6,8},{8,10},{10,12},{12,14},{14,16},{16,18},{18... | collective-permute-start | bytes 393224 | tf_op jit(solution)/shard_map/ppermute | solution.py:236
  108.7 6.2 %collective-permute-start.3 = (bf16[4,128,128]{2,1,0:T(8,128)(2,1)S(1)}, bf16[4,128,128]{2,1,0:T(8,128)(2,1)S(1)}, u32[]{:S(2)}, u32[]{:S(2)}) collective-permute-start(bf16[4,128,128]{2,1,0:T(8,128)(2,1)S(1)} %get-tuple-element.32), channel_id=1, source_target_pairs={{0,30},{2,0},{4,2},{6,4},{8,6},{10,8},{12,10},{14,12},{16,14},{18,... | collective-permute-start | bytes 393224 | tf_op jit(solution)/shard_map/ppermute | solution.py:237

commit v6 on v5

--- a/solution.py
+++ b/solution.py
@@ -14,6 +14,9 @@
 ETP = (*Z, "core")
 LANES = 128
 CHUNKS = 4
+TOP = 12
+LEVELS = 14
+MARK_ROWS = 8
 PARITIES = 2
 
 HBM = pl.BlockSpec(memory_space=pltpu.HBM)
@@ -44,12 +47,24 @@
 
 
 def dispatch_body(routes_ref, tokens_ref, out_ref):
-    experts, chips, cap, lanes = out_ref.shape
-    table = slot_table(routes_ref, cap, experts, lambda e: 1.0)
-    for z in range(0, chips, 2):
-        rows = dot32(table, side_by_side([tokens_ref[z], tokens_ref[z + 1]])).astype(out_ref.dtype)
-        for k in range(2):
-            out_ref[:, z + k] = rows[:, k * lanes : (k + 1) * lanes].reshape(experts, cap, lanes)
+    experts, rows, lanes = out_ref.shape
+    tokens = tokens_ref[...]
+    largest = jnp.max(jnp.abs(tokens.astype(jnp.float32)))
+    scale, mark = jnp.float32(2.0**TOP), jnp.float32(1.0)
+    for level in range(1, LEVELS):
+        lower = largest < 2.0 ** (15 - TOP - 8 * level)
+        scale = jnp.where(lower, 2.0 ** (TOP + 8 * level), scale)
+        mark = jnp.where(lower, 2.0**-level, mark)
+    picked = dot32(slot_table(routes_ref, CAP, experts, lambda e: 1.0), tokens) * scale
+    out_ref[:, :CAP] = picked.astype(out_ref.dtype).reshape(experts, CAP, lanes)
+    out_ref[:, CAP:] = jnp.full((experts, rows - CAP, lanes), mark, jnp.float32).astype(out_ref.dtype)
+
+
+def unscaled(tile_ref, z):
+    mark = tile_ref[z, :, CAP : CAP + 1].astype(jnp.float32)
+    for _ in range(3):
+        mark = mark * mark
+    return tile_ref[z, :, :CAP] * (mark * 2.0**-TOP).astype(tile_ref.dtype)
 
 
 def column_copies(w_ref, buf, sems):
@@ -58,77 +73,57 @@
     return [pltpu.make_async_copy(w_ref.at[:, span], buf.at[:, span], sems.at[i]) for i, span in enumerate(spans)]
 
 
-def start_all(copies):
-    for copy in copies:
-        copy.start()
-
-
-def wait_all(copies):
-    for copy in copies:
-        copy.wait()
-
-
 def core_columns(ref, core, start, count):
     return side_by_side(
         [ref[:, pl.ds(pl.multiple_of((z * CORES + core) * LANES, LANES), LANES)] for z in range(start, start + count)]
     )
 
 
-def up_partial(core, x_ref, w_refs, ready):
-    step = x_ref.shape[1] // CHUNKS
-    sums = [None] * len(w_refs)
+def up_partial(core, x_ref, w_ref, copies=None):
+    step = x_ref.shape[0] // CHUNKS
+    total = None
     for k in range(CHUNKS):
-        ready(k)
-        x = side_by_side([x_ref[:, z] for z in range(k * step, (k + 1) * step)])
-        for i, w in enumerate(w_refs):
-            part = lax.dot_general(
-                x, core_columns(w, core, k * step, step), (((1,), (1,)), ((), ())), preferred_element_type=jnp.float32
-            )
-            sums[i] = part if k == 0 else sums[i] + part
-    return sums
-
-
-def down_into(hidden, core, wd_ref, out_ref, ready=None):
+        x = side_by_side([unscaled(x_ref, z) for z in range(k * step, (k + 1) * step)])
+        if copies is not None:
+            copies[k].wait()
+        part = lax.dot_general(
+            x, core_columns(w_ref, core, k * step, step), (((1,), (1,)), ((), ())), preferred_element_type=jnp.float32
+        )
+        total = part if k == 0 else total + part
+    return total
+
+
+def down_into(hidden, core, wd_ref, out_ref):
     blocks, chips, cap, lanes = out_ref.shape
     step = chips // CHUNKS
     for k in range(CHUNKS):
-        if ready is not None:
-            ready(k)
         part = dot32(hidden, core_columns(wd_ref, core, k * step, step)).astype(out_ref.dtype)
         for z in range(step):
             out_ref[:, k * step + z] = part[:, z * lanes : (z + 1) * lanes].reshape(blocks, cap, lanes)
 
 
 def first_half_body(
-    core_ref, x_ref, routes_ref, weights_ref, wg_ref, wu_ref, gate_ref, up_ref, g_here, u_here, table_ref, sems
+    core_ref, x_ref, routes_ref, weights_ref, wg_ref, wu_ref, gate_ref, up_ref, u_here, table_ref, sems
 ):
-    gates = column_copies(wg_ref, g_here, sems.at[0])
-    ups = column_copies(wu_ref, u_here, sems.at[1])
-    for pair in zip(gates, ups):
-        start_all(pair)
+    copies = column_copies(wu_ref, u_here, sems)
+    for copy in copies:
+        copy.start()
 
     def weight_of(e):
         return sum(jnp.where(routes_ref[k : k + 1, :] == e, weights_ref[k : k + 1, :], 0.0) for k in range(2))
 
-    table_ref[...] = slot_table(routes_ref, x_ref.shape[2], x_ref.shape[0], weight_of).T
-
-    gate_ref[...], up_ref[...] = up_partial(
-        core_ref[0], x_ref, (g_here, u_here), lambda k: wait_all((gates[k], ups[k]))
-    )
-
-
-def second_half_body(
-    core_ref, x_ref, gate_ref, up_ref, g_here, u_here, wd_ref, hidden_ref, out_ref, d_here, sems
-):
+    table_ref[...] = slot_table(routes_ref, CAP, x_ref.shape[1], weight_of).T
+    gate_ref[...] = up_partial(core_ref[0], x_ref, wg_ref)
+    up_ref[...] = up_partial(core_ref[0], x_ref, u_here, copies)
+
+
+def second_half_body(core_ref, x_ref, gate_ref, up_ref, wg_ref, wu_ref, wd_ref, hidden_ref, out_ref):
     other = 1 - core_ref[0]
-    downs = column_copies(wd_ref, d_here, sems)
-    start_all(downs)
-    gate, up = up_partial(other, x_ref, (g_here, u_here), lambda k: None)
-    gate = gate + gate_ref[...]
-    up = up + up_ref[...]
+    gate = up_partial(other, x_ref, wg_ref) + gate_ref[...]
+    up = up_partial(other, x_ref, wu_ref) + up_ref[...]
     hidden = (gate / (1.0 + jnp.exp(-gate)) * up).astype(hidden_ref.dtype)
     hidden_ref[...] = hidden
-    down_into(hidden, other, d_here, out_ref, lambda k: downs[k].wait())
+    down_into(hidden, other, wd_ref, out_ref)
 
 
 def own_down_body(core_ref, hidden_ref, d_here, out_ref):
@@ -166,7 +161,7 @@
         out_specs=outs,
         scratch_shapes=list(scratch),
         cost_estimate=pl.CostEstimate(flops=flops, transcendentals=0, bytes_accessed=flops // 400),
-        compiler_params=pltpu.CompilerParams(vmem_limit_bytes=24 * 1024 * 1024),
+        compiler_params=pltpu.CompilerParams(vmem_limit_bytes=16 * 1024 * 1024),
     )
 
 
@@ -187,37 +182,31 @@
     swap = functools.partial(lax.ppermute, axis_name="core", perm=[(0, 1), (1, 0)])
     exchange = functools.partial(lax.all_to_all, split_axis=0, concat_axis=0, tiled=True)
 
-    gathered = lax.all_gather(tokens, Z, axis=0, tiled=False)
-    sent = call(
-        dispatch_body, shape((experts, chips, CAP, lanes), bf16), (VMEM, VMEM), flops=2 * slots * token_count * chips * lanes
-    )(routes, gathered)
-    own = exchange(sent, "expert")
+    picked = call(dispatch_body, shape((experts, CAP + MARK_ROWS, lanes), bf16), (VMEM, VMEM))(routes, tokens)
+    slices = exchange(picked.astype(jnp.float16), "expert")
+    own = lax.all_gather(slices, Z, axis=0, tiled=False).astype(bf16)
     other = swap(own)
 
-    gate_rows, up_rows, down_rows = (
-        pltpu.with_memory_space_constraint(w, pltpu.HBM)
-        for w in (jnp.swapaxes(w_gate[0], 0, 1), jnp.swapaxes(w_up[0], 0, 1), w_down[0])
-    )
+    gate_rows, up_rows, down_rows = w_gate[0].T, w_up[0].T, w_down[0]
+    up_rows = pltpu.with_memory_space_constraint(up_rows, pltpu.HBM)
     up_flops = 2 * slots * width * width_in
     acc = shape((slots, width), f32)
-    held = shape((width, width_in), bf16)
-    gate_half, up_half, gate_here, up_here, combine_table = call(
+    gate_half, up_half, up_here, combine_table = call(
         first_half_body,
-        (acc, acc, held, held, shape((token_count, slots), bf16)),
-        (SMEM, VMEM, VMEM, VMEM, HBM, HBM),
-        [pltpu.SemaphoreType.DMA((2, CHUNKS))],
+        (acc, acc, shape((width, width_in), bf16), shape((token_count, slots), bf16)),
+        (SMEM, VMEM, VMEM, VMEM, VMEM, HBM),
+        [pltpu.SemaphoreType.DMA((CHUNKS,))],
         flops=up_flops,
     )(core, own, routes, weights, gate_rows, up_rows)
-    hidden, theirs, down_here = call(
+    hidden, theirs = call(
         second_half_body,
-        (shape((slots, width), bf16), shape((experts, chips, CAP, lanes), bf16), held),
-        (SMEM, VMEM, VMEM, VMEM, VMEM, VMEM, HBM),
-        [pltpu.SemaphoreType.DMA((CHUNKS,))],
+        (shape((slots, width), bf16), shape((experts, chips, CAP, lanes), bf16)),
+        (SMEM, VMEM, VMEM, VMEM, VMEM, VMEM, VMEM),
         flops=up_flops * 3 // 2,
-    )(core, other, gate_half, up_half, gate_here, up_here, down_rows)
+    )(core, other, gate_half, up_half, gate_rows, up_here, down_rows)
     arrived = swap(theirs)
     mine = call(own_down_body, shape((experts, chips, CAP, lanes), f32), (SMEM, VMEM, VMEM), flops=up_flops // 2)(
-        core, hidden, down_here
+        core, hidden, down_rows
     )
     chip_sum = (mine + arrived.astype(f32)).astype(bf16)
     results = exchange(chip_sum, "expert")

time: 139 us -> 138 us (level)
  Pallas kernels: 11 us -> 8.55 us
    all_to_all x1, blocking collectives: 18.2 us -> 10.2 us  [shards(): slices = exchange(picked.astype(jnp.float16), 'expert')]
    all_gather x1, blocking collectives: 51.7 us -> 58.6 us  [shards(): own = lax.all_gather(slices, Z, axis=0, tiled=False).astype(bf16)]
    pallas_call x1, Pallas kernels: 4.64 us -> 2.88 us  [shards(): call(second_half_body, (shape((slots, width), bf16), shape((experts, chip...]
where the time goes in v6:
time: 138 us; the launch traced here: 137 us
  blocking collectives  117 us (85%)
  Pallas kernels  8.55 us (6%)
  waiting for transfers between devices  5.02 us (4%)
  starting transfers between devices  3.88 us (3%)
  local copies, waits for them, and re-layouts  1.68 us (1%)
  other arithmetic  1.41 us (1%)
    all_gather x1, blocking collectives, shards(): own = lax.all_gather(slices, Z, axis=0, tiled=False).astype(bf16)  58.6 us
    all_to_all x1, blocking collectives, shards(): pieces = exchange(paired, 'z_0')  24.1 us
    all_to_all x1, blocking collectives, shards(): results = exchange(chip_sum, 'expert')  23.9 us
    all_to_all x1, blocking collectives, shards(): slices = exchange(picked.astype(jnp.float16), 'expert')  10.2 us
    pallas_call x1, Pallas kernels, shards(): call(first_half_body, (acc, acc, shape((width, width_in), bf16), shape((t...  3.82 us
    ppermute x1, starting transfers between devices, shards(): high = lax.ppermute(left, Z, [(z, (z - 1) % chips) for z in range(chips)])  3.21 us
    ppermute x1, waiting for transfers between devices, shards(): low = lax.ppermute(right, Z, [(z, (z + 1) % chips) for z in range(chips)])  2.94 us
    pallas_call x1, Pallas kernels, shards(): call(second_half_body, (shape((slots, width), bf16), shape((experts, chip...  2.88 us
  transfers between devices with their start and end apart: 4, of which 2 were waited for; matrix products, arithmetic and copies ran while one was open for 0% of the time, Pallas kernels for 4%

profile of v6, /device:TPU:40, one launch (start us, length us, event | category | flops | bytes accessed | tf_op | source)
XLA Modules:
  0.0 137.5 jit_solution(5834968412600313517)
XLA Ops:
  0.0 0.0 copy-start.2
  0.0 0.8 copy-done.2
  0.8 0.0 copy-start.3
  0.8 0.7 copy-done.3
  1.4 0.3 shard_map.64
  1.8 10.2 %all_to_all.15 = f16[4,104,128]{2,1,0:T(8,128)(2,1)S(1)} all-to-all(f16[4,104,128]{2,1,0:T(8,128)(2,1)S(1)} %convert_element_type.14), channel_id=1, replica_groups=mesh['groups'=2,'expert'=4,'z_0'=8,'z_1'=2,'core'=2] {'expert'}, dimensions={0} | all-to-all | bytes 212992 | tf_op jit(solution)/shard_map/all_to_all | solution.py:186
  12.0 0.0 copy-start.1
  12.0 58.6 %all-gather.2 = f16[64,104,128]{2,1,0:T(8,128)(2,1)S(1)} all-gather(f16[4,104,128]{2,1,0:T(8,128)(2,1)S(1)} %all_to_all.15), channel_id=2, replica_groups=mesh['groups'=2,'expert'=4,'z_0'=8,'z_1'=2,'core'=2] {'z_0','z_1'}, dimensions={0}, use_global_device_ids=true | all-gather | bytes 1810432 | tf_op jit(solution)/shard_map/all_gather | solution.py:187
  70.6 0.0 copy-start.4
  70.6 0.0 copy-start.5
  70.6 0.3 convert_element_type.18
  70.9 0.1 collective-permute-start
  71.0 0.0 copy-done.1
  71.0 0.2 copy-done.4
  71.2 0.0 copy-done.5
  71.3 0.0 copy-start
  71.3 3.8 %shard_map.65 = (f32[384,448]{1,0:T(8,128)S(1)}, f32[384,448]{1,0:T(8,128)S(1)}, bf16[448,4096]{1,0:T(8,128)(2,1)S(1)}, bf16[128,384]{1,0:T(8,128)(2,1)S(1)}) custom-call(s32[1]{0:T(128)} %bitcast.core_ref, bf16[16,4,104,128]{3,2,1,0:T(8,128)(2,1)S(1)} %bitcast.17, s32[2,128]{1,0:T(2,128)S(1)} %bitcast.19, f32[2,128]{1,0:T(2,128)S(1)} %bitcast.20, ...), custom_call_target="tpu_custom_call" | custom-call | flops 1409286144 | bytes 3523215 | tf_op jit(solution)/shard_map/pallas_call | solution.py:194
  75.1 0.0 collective-permute-done.x_ref
  75.1 0.0 copy-done
  75.1 2.9 %shard_map.66 = (bf16[384,448]{1,0:T(8,128)(2,1)S(1)}, bf16[4,16,96,128]{3,2,1,0:T(8,128)(2,1)S(1)}) custom-call(s32[1]{0:T(128)} %bitcast.core_ref, bf16[16,4,104,128]{3,2,1,0:T(8,128)(2,1)S(1)} %collective-permute-done.x_ref, f32[384,448]{1,0:T(8,128)S(1)} %get-tuple-element.21.gate_ref, f32[384,448]{1,0:T(8,128)S(1)} %get-tuple-element.22.up_ref, ...), custom_call_target="tpu_custom_call" | custom-call | flops 2113929216 | bytes 5284823 | tf_op jit(solution)/shard_map/pallas_call | solution.py:201
  78.0 0.4 collective-permute-start.1
  78.4 1.1 shard_map.67
  79.4 2.1 %collective-permute-done.1 = bf16[4,16,96,128]{3,2,1,0:T(8,128)(2,1)S(1)} collective-permute-done((bf16[4,16,96,128]{3,2,1,0:T(8,128)(2,1)S(1)}, bf16[4,16,96,128]{3,2,1,0:T(8,128)(2,1)S(1)}, u32[]{:S(2)}, u32[]{:S(2)}) %collective-permute-start.1) | collective-permute-done | bytes 1572896 | tf_op jit(solution)/shard_map/ppermute | solution.py:207
  81.5 0.4 add_convert_fusion
  82.0 23.9 %all_to_all.16.results_ref = bf16[4,16,96,128]{3,2,1,0:T(8,128)(2,1)S(1)} all-to-all(bf16[4,16,96,128]{3,2,1,0:T(8,128)(2,1)S(1)} %add_convert_fusion), channel_id=1, replica_groups=mesh['groups'=2,'expert'=4,'z_0'=8,'z_1'=2,'core'=2] {'expert'}, dimensions={0} | all-to-all | bytes 3145728 | tf_op jit(solution)/shard_map/all_to_all | solution.py:212
  105.9 0.4 shard_map.68
  106.3 0.1 collective-permute-start.2
  106.5 3.2 %collective-permute-start.3 = (bf16[4,128,128]{2,1,0:T(8,128)(2,1)S(1)}, bf16[4,128,128]{2,1,0:T(8,128)(2,1)S(1)}, u32[]{:S(2)}, u32[]{:S(2)}) collective-permute-start(bf16[4,128,128]{2,1,0:T(8,128)(2,1)S(1)} %get-tuple-element.28), channel_id=1, source_target_pairs={{0,30},{2,0},{4,2},{6,4},{8,6},{10,8},{12,10},{14,12},{16,14},{18,... | collective-permute-start | bytes 393224 | tf_op jit(solution)/shard_map/ppermute | solution.py:226
  109.7 2.9 %collective-permute-done.2.low_ref = bf16[4,128,128]{2,1,0:T(8,128)(2,1)S(1)} collective-permute-done((bf16[4,128,128]{2,1,0:T(8,128)(2,1)S(1)}, bf16[4,128,128]{2,1,0:T(8,128)(2,1)S(1)}, u32[]{:S(2)}, u32[]{:S(2)}) %collective-permute-start.2) | collective-permute-done | bytes 131104 | tf_op jit(solution)/shard_map/ppermute | solution.py:225
  112.6 0.0 collective-permute-done.3.high_ref
  112.6 0.1 shard_map.69
  112.7 24.1 %all_to_all.17 = bf16[8,128,128]{2,1,0:T(8,128)(2,1)S(1)} all-to-all(bf16[8,128,128]{2,1,0:T(8,128)(2,1)S(1)} %shard_map.69), channel_id=1, replica_groups=mesh['groups'=2,'expert'=4,'z_0'=8,'z_1'=2,'core'=2] {'z_0'}, dimensions={0} | all-to-all | bytes 524288 | tf_op jit(solution)/shard_map/all_to_all | solution.py:228
  136.8 0.7 reduce_sum.12
  (1 shorter events, 0.0 us)
Async XLA Ops:
  0.0 0.8 copy-start.2
  0.8 0.7 copy-start.3
  12.0 59.0 %copy-start.1 = (bf16[1,4096,448]{1,2,0:T(8,128)(2,1)S(1)}, bf16[1,4096,448]{1,2,0:T(8,128)(2,1)}, u32[]{:S(2)}) copy-start(bf16[1,4096,448]{1,2,0:T(8,128)(2,1)} %param.9) | copy-start | bytes 11010052
  70.6 0.7 copy-start.4
  70.6 0.7 copy-start.5
  70.9 4.2 %collective-permute-start = (bf16[16,4,104,128]{3,2,1,0:T(8,128)(2,1)S(1)}, bf16[16,4,104,128]{3,2,1,0:T(8,128)(2,1)S(1)}, u32[]{:S(2)}, u32[]{:S(2)}) collective-permute-start(bf16[16,4,104,128]{3,2,1,0:T(8,128)(2,1)S(1)} %bitcast.16), channel_id=1, source_target_pairs={{0,1},{1,0},{2,3},{3,2},{4,5},{5,4},{6,7},{7,6},{8,9},{9,8},{10,11... | collective-permute-start | bytes 5111816 | tf_op jit(solution)/shard_map/ppermute | solution.py:188
  71.3 3.8 %copy-start = (bf16[1,448,4096]{2,1,0:T(8,128)(2,1)S(1)}, bf16[1,448,4096]{2,1,0:T(8,128)(2,1)}, u32[]{:S(2)}) copy-start(bf16[1,448,4096]{2,1,0:T(8,128)(2,1)} %param.11) | copy-start | bytes 11010052
  78.0 3.5 %collective-permute-start.1 = (bf16[4,16,96,128]{3,2,1,0:T(8,128)(2,1)S(1)}, bf16[4,16,96,128]{3,2,1,0:T(8,128)(2,1)S(1)}, u32[]{:S(2)}, u32[]{:S(2)}) collective-permute-start(bf16[4,16,96,128]{3,2,1,0:T(8,128)(2,1)S(1)} %get-tuple-element.25), channel_id=1, source_target_pairs={{0,1},{1,0},{2,3},{3,2},{4,5},{5,4},{6,7},{7,6},{8,9},{9,8},{10,11... | collective-permute-start | bytes 4718600 | tf_op jit(solution)/shard_map/ppermute | solution.py:207
  106.3 6.3 %collective-permute-start.2 = (bf16[4,128,128]{2,1,0:T(8,128)(2,1)S(1)}, bf16[4,128,128]{2,1,0:T(8,128)(2,1)S(1)}, u32[]{:S(2)}, u32[]{:S(2)}) collective-permute-start(bf16[4,128,128]{2,1,0:T(8,128)(2,1)S(1)} %get-tuple-element.27), channel_id=1, source_target_pairs={{0,2},{2,4},{4,6},{6,8},{8,10},{10,12},{12,14},{14,16},{16,18},{18... | collective-permute-start | bytes 393224 | tf_op jit(solution)/shard_map/ppermute | solution.py:225
  106.5 6.2 %collective-permute-start.3 = (bf16[4,128,128]{2,1,0:T(8,128)(2,1)S(1)}, bf16[4,128,128]{2,1,0:T(8,128)(2,1)S(1)}, u32[]{:S(2)}, u32[]{:S(2)}) collective-permute-start(bf16[4,128,128]{2,1,0:T(8,128)(2,1)S(1)} %get-tuple-element.28), channel_id=1, source_target_pairs={{0,30},{2,0},{4,2},{6,4},{8,6},{10,8},{12,10},{14,12},{16,14},{18,... | collective-permute-start | bytes 393224 | tf_op jit(solution)/shard_map/ppermute | solution.py:226

commit v7 on v6

--- a/solution.py
+++ b/solution.py
@@ -73,10 +73,8 @@
     return [pltpu.make_async_copy(w_ref.at[:, span], buf.at[:, span], sems.at[i]) for i, span in enumerate(spans)]
 
 
-def core_columns(ref, core, start, count):
-    return side_by_side(
-        [ref[:, pl.ds(pl.multiple_of((z * CORES + core) * LANES, LANES), LANES)] for z in range(start, start + count)]
-    )
+def core_columns(ref, core, chips):
+    return side_by_side([ref[:, pl.ds(pl.multiple_of((z * CORES + core) * LANES, LANES), LANES)] for z in chips])
 
 
 def up_partial(core, x_ref, w_ref, copies=None):
@@ -87,23 +85,24 @@
         if copies is not None:
             copies[k].wait()
         part = lax.dot_general(
-            x, core_columns(w_ref, core, k * step, step), (((1,), (1,)), ((), ())), preferred_element_type=jnp.float32
+            x, core_columns(w_ref, core, range(k * step, (k + 1) * step)), (((1,), (1,)), ((), ())), preferred_element_type=jnp.float32
         )
         total = part if k == 0 else total + part
     return total
 
 
-def down_into(hidden, core, wd_ref, out_ref):
-    blocks, chips, cap, lanes = out_ref.shape
-    step = chips // CHUNKS
-    for k in range(CHUNKS):
-        part = dot32(hidden, core_columns(wd_ref, core, k * step, step)).astype(out_ref.dtype)
+def down_into(hidden, core, parity, wd_ref, out_ref):
+    blocks, count, cap, lanes = out_ref.shape
+    step = 4
+    for k in range(0, count, step):
+        chips = [PARITIES * z + parity for z in range(k, k + step)]
+        part = dot32(hidden, core_columns(wd_ref, core, chips)).astype(out_ref.dtype)
         for z in range(step):
-            out_ref[:, k * step + z] = part[:, z * lanes : (z + 1) * lanes].reshape(blocks, cap, lanes)
+            out_ref[:, k + z] = part[:, z * lanes : (z + 1) * lanes].reshape(blocks, cap, lanes)
 
 
 def first_half_body(
-    core_ref, x_ref, routes_ref, weights_ref, wg_ref, wu_ref, gate_ref, up_ref, u_here, table_ref, sems
+    place_ref, x_ref, routes_ref, weights_ref, wg_ref, wu_ref, gate_ref, up_ref, u_here, table_ref, sems
 ):
     copies = column_copies(wu_ref, u_here, sems)
     for copy in copies:
@@ -113,43 +112,48 @@
         return sum(jnp.where(routes_ref[k : k + 1, :] == e, weights_ref[k : k + 1, :], 0.0) for k in range(2))
 
     table_ref[...] = slot_table(routes_ref, CAP, x_ref.shape[1], weight_of).T
-    gate_ref[...] = up_partial(core_ref[0], x_ref, wg_ref)
-    up_ref[...] = up_partial(core_ref[0], x_ref, u_here, copies)
-
-
-def second_half_body(core_ref, x_ref, gate_ref, up_ref, wg_ref, wu_ref, wd_ref, hidden_ref, out_ref):
-    other = 1 - core_ref[0]
-    gate = up_partial(other, x_ref, wg_ref) + gate_ref[...]
-    up = up_partial(other, x_ref, wu_ref) + up_ref[...]
+    gate_ref[...] = up_partial(place_ref[0], x_ref, wg_ref)
+    up_ref[...] = up_partial(place_ref[0], x_ref, u_here, copies)
+
+
+def second_half_body(place_ref, x_ref, gate_ref, up_ref, wg_ref, wu_ref, wd_ref, hidden_ref, out_ref):
+    core, parity = place_ref[0], place_ref[1]
+    gate = up_partial(1 - core, x_ref, wg_ref) + gate_ref[...]
+    up = up_partial(1 - core, x_ref, wu_ref) + up_ref[...]
     hidden = (gate / (1.0 + jnp.exp(-gate)) * up).astype(hidden_ref.dtype)
     hidden_ref[...] = hidden
-    down_into(hidden, other, wd_ref, out_ref)
-
-
-def own_down_body(core_ref, hidden_ref, d_here, out_ref):
-    down_into(hidden_ref[...], core_ref[0], d_here, out_ref)
-
-
-def combine_body(parity_ref, table_ref, results_ref, own_ref, right_ref, left_ref):
-    parity = parity_ref[0]
+    down_into(hidden, 1 - core, 1 - parity, wd_ref, out_ref)
+
+
+def down_body(place_ref, hidden_ref, wd_ref, out_ref, *, own_core, own_parity):
+    core, parity = place_ref[0], place_ref[1]
+    down_into(
+        hidden_ref[...], core if own_core else 1 - core, parity if own_parity else 1 - parity, wd_ref, out_ref
+    )
+
+
+def outgoing_body(mine_ref, arrived_ref, right_ref, left_ref):
+    half = right_ref.shape[1]
+    for part, ref in enumerate((right_ref, left_ref)):
+        chips = pl.ds(part * half, half)
+        ref[...] = (mine_ref[:, chips] + arrived_ref[:, chips].astype(jnp.float32)).astype(ref.dtype)
+
+
+def pair_body(mine_ref, arrived_ref, low_ref, high_ref, out_ref):
+    half = low_ref.shape[1]
+    for part, ref in enumerate((low_ref, high_ref)):
+        chips = pl.ds(part * half, half)
+        total = mine_ref[:, chips] + arrived_ref[:, chips].astype(jnp.float32) + ref[...].astype(jnp.float32)
+        out_ref[:, chips] = total.astype(out_ref.dtype)
+
+
+def combine_body(table_ref, results_ref, out_ref):
+    chips, _, lanes = out_ref.shape
     table = table_ref[...]
-    half = right_ref.shape[0]
-
-    def rows_of(chip):
-        return results_ref[:, chip].reshape(-1, LANES)
-
-    for k in range(2 * half):
-        mine, other = rows_of(PARITIES * k + parity), rows_of(PARITIES * k + 1 - parity)
-        rows = dot32(table, jnp.concatenate([mine, other], axis=1)).astype(own_ref.dtype)
-        own_ref[k] = rows[:, :LANES]
-        (right_ref if k < half else left_ref)[k % half] = rows[:, LANES:]
-
-
-def chip_pair_body(own_ref, low_ref, high_ref, out_ref):
-    half = low_ref.shape[0]
-    for part, ref in enumerate((low_ref, high_ref)):
-        rows = pl.ds(part * half, half)
-        out_ref[rows] = (own_ref[rows].astype(jnp.float32) + ref[...].astype(jnp.float32)).astype(out_ref.dtype)
+    for z in range(0, chips, 2):
+        rows = dot32(table, side_by_side([results_ref[:, z], results_ref[:, z + 1]])).astype(out_ref.dtype)
+        for k in range(2):
+            out_ref[z + k] = rows[:, k * lanes : (k + 1) * lanes]
 
 
 def call(body, out_shape, in_specs, scratch=(), flops=0):
@@ -175,9 +179,8 @@
     shape = jax.ShapeDtypeStruct
 
     routes, weights = route_ids.T, gate_weights.T
-    core = lax.axis_index("core").astype(jnp.int32).reshape(1)
-    parity = lax.axis_index("z_1").astype(jnp.int32).reshape(1)
-    tokens, core, parity = lax.optimization_barrier((tokens, core, parity))
+    place = jnp.stack([lax.axis_index("core"), lax.axis_index("z_1")]).astype(jnp.int32)
+    tokens, place = lax.optimization_barrier((tokens, place))
 
     swap = functools.partial(lax.ppermute, axis_name="core", perm=[(0, 1), (1, 0)])
     exchange = functools.partial(lax.all_to_all, split_axis=0, concat_axis=0, tiled=True)
@@ -197,35 +200,34 @@
         (SMEM, VMEM, VMEM, VMEM, VMEM, HBM),
         [pltpu.SemaphoreType.DMA((CHUNKS,))],
         flops=up_flops,
-    )(core, own, routes, weights, gate_rows, up_rows)
-    hidden, theirs = call(
+    )(place, own, routes, weights, gate_rows, up_rows)
+    of_parity = chips // PARITIES
+    half = shape((experts, of_parity, CAP, lanes), bf16)
+    quarter = shape((experts, of_parity // 2, CAP, lanes), bf16)
+    wide = shape(half.shape, f32)
+
+    def down(out, **which):
+        body = functools.partial(down_body, **which)
+        return call(body, out, (SMEM, VMEM, VMEM), flops=up_flops // 4)(place, hidden, down_rows)
+
+    hidden, theirs_away = call(
         second_half_body,
-        (shape((slots, width), bf16), shape((experts, chips, CAP, lanes), bf16)),
+        (shape((slots, width), bf16), half),
         (SMEM, VMEM, VMEM, VMEM, VMEM, VMEM, VMEM),
-        flops=up_flops * 3 // 2,
-    )(core, other, gate_half, up_half, gate_rows, up_here, down_rows)
-    arrived = swap(theirs)
-    mine = call(own_down_body, shape((experts, chips, CAP, lanes), f32), (SMEM, VMEM, VMEM), flops=up_flops // 2)(
-        core, hidden, down_rows
-    )
-    chip_sum = (mine + arrived.astype(f32)).astype(bf16)
-    results = exchange(chip_sum, "expert")
-
-    of_parity = chips // PARITIES
-
-    def block(count):
-        return shape((count, token_count, lanes), bf16)
-
-    blended, right, left = call(
-        combine_body,
-        (block(of_parity), block(of_parity // 2), block(of_parity // 2)),
-        (SMEM, VMEM, VMEM),
-        flops=2 * slots * token_count * chips * lanes,
-    )(parity, combine_table, results)
+        flops=up_flops * 5 // 4,
+    )(place, other, gate_half, up_half, gate_rows, up_here, down_rows)
+    arrived_away = swap(theirs_away)
+    mine_away = down(wide, own_core=True, own_parity=False)
+    right, left = call(outgoing_body, (quarter, quarter), (VMEM, VMEM))(mine_away, arrived_away)
     low = lax.ppermute(right, Z, [(z, (z + 1) % chips) for z in range(chips)])
     high = lax.ppermute(left, Z, [(z, (z - 1) % chips) for z in range(chips)])
-    paired = call(chip_pair_body, block(of_parity), (VMEM, VMEM, VMEM))(blended, low, high)
-    pieces = exchange(paired, "z_0")
+    arrived = swap(down(half, own_core=False, own_parity=True))
+    mine = down(wide, own_core=True, own_parity=True)
+    paired = call(pair_body, half, (VMEM,) * 4)(mine, arrived, low, high)
+
+    results = exchange(paired, "expert")
+    blended = call(combine_body, shape((of_parity, token_count, lanes), bf16), (VMEM, VMEM))(combine_table, results)
+    pieces = exchange(blended, "z_0")
     return pieces.astype(f32).sum(axis=0).astype(bf16)
 
 

time: 138 us -> 134 us (0.971)
  blocking collectives: 117 us -> 107 us
  Pallas kernels: 8.55 us -> 11.6 us
  waiting for transfers between devices: 5.02 us -> 8.05 us
    all_to_all x2, blocking collectives: 48.1 us -> 38.2 us  [the longest x1 23.7 us: shards(): pieces = exchange(blended, 'z_0')]
    ppermute x1, waiting for transfers between devices: 2.94 us -> 8.04 us  [shards(): low = lax.ppermute(right, Z, [(z, (z + 1) % chips) for z in range(chips)])]
    pallas_call x4 -> x7, Pallas kernels: 4.44 us -> 7.25 us  [the longest x3 3.55 us: down(): call(body, out, (SMEM, VMEM, VMEM), flops=up_flops // 4)]
    ppermute x1 -> x2, waiting for transfers between devices: 2.07 us -> 0.01 us  [the longest x1 0.01 us: shards(): arrived_away = swap(theirs_away)]
  transfers between devices with their start and end apart: 4 -> 5, of which waited for: 2 -> 1; matrix products, arithmetic and copies ran while one was open for 0% -> 0% of each run, Pallas kernels for 4% -> 6%
where the time goes in v7:
time: 134 us
  blocking collectives  107 us (80%)
  Pallas kernels  11.6 us (9%)
  waiting for transfers between devices  8.05 us (6%)
  starting transfers between devices  4.24 us (3%)
  local copies, waits for them, and re-layouts  1.68 us (1%)
    all_gather x1, blocking collectives, shards(): own = lax.all_gather(slices, Z, axis=0, tiled=False).astype(bf16)  58.6 us
    all_to_all x1, blocking collectives, shards(): pieces = exchange(blended, 'z_0')  23.7 us
    all_to_all x1, blocking collectives, shards(): results = exchange(paired, 'expert')  14.6 us
    all_to_all x1, blocking collectives, shards(): slices = exchange(picked.astype(jnp.float16), 'expert')  10.2 us
    ppermute x1, waiting for transfers between devices, shards(): low = lax.ppermute(right, Z, [(z, (z + 1) % chips) for z in range(chips)])  8.04 us
    pallas_call x1, Pallas kernels, shards(): call(first_half_body, (acc, acc, shape((width, width_in), bf16), shape((t...  4.07 us
    pallas_call x3, Pallas kernels, down(): call(body, out, (SMEM, VMEM, VMEM), flops=up_flops // 4)  3.55 us
    ppermute x1, starting transfers between devices, shards(): high = lax.ppermute(left, Z, [(z, (z - 1) % chips) for z in range(chips)])  3.21 us
  transfers between devices with their start and end apart: 5, of which 1 were waited for; matrix products, arithmetic and copies ran while one was open for 0% of the time, Pallas kernels for 6%

profile of v7, /device:TPU:40, one launch (start us, length us, event | category | flops | bytes accessed | tf_op | source)
XLA Modules:
  0.0 133.8 jit_solution(23646096608163449)
XLA Ops:
  0.0 0.1 pad_add_fusion.place_ref
  0.1 0.0 copy-start.2
  0.1 0.8 copy-done.2
  0.8 0.0 copy-start.3
  0.8 0.7 copy-done.3
  1.5 0.3 shard_map.64
  1.8 10.2 %all_to_all.15 = f16[4,104,128]{2,1,0:T(8,128)(2,1)S(1)} all-to-all(f16[4,104,128]{2,1,0:T(8,128)(2,1)S(1)} %convert_element_type.8), channel_id=1, replica_groups=mesh['groups'=2,'expert'=4,'z_0'=8,'z_1'=2,'core'=2] {'expert'}, dimensions={0} | all-to-all | bytes 212992 | tf_op jit(solution)/shard_map/all_to_all | solution.py:189
  12.1 0.0 copy-start.1
  12.1 58.6 %all-gather.2 = f16[64,104,128]{2,1,0:T(8,128)(2,1)S(1)} all-gather(f16[4,104,128]{2,1,0:T(8,128)(2,1)S(1)} %all_to_all.15), channel_id=2, replica_groups=mesh['groups'=2,'expert'=4,'z_0'=8,'z_1'=2,'core'=2] {'z_0','z_1'}, dimensions={0}, use_global_device_ids=true | all-gather | bytes 1810432 | tf_op jit(solution)/shard_map/all_gather | solution.py:190
  70.6 0.0 copy-start.4
  70.6 0.0 copy-start.5
  70.6 0.3 convert_element_type.10
  70.9 0.1 collective-permute-start
  71.1 0.0 copy-done.1
  71.1 0.2 copy-done.4
  71.3 0.0 copy-done.5
  71.3 0.0 copy-start
  71.3 4.1 %shard_map.65 = (f32[384,448]{1,0:T(8,128)S(1)}, f32[384,448]{1,0:T(8,128)S(1)}, bf16[448,4096]{1,0:T(8,128)(2,1)S(1)}, bf16[128,384]{1,0:T(8,128)(2,1)S(1)}) custom-call(s32[2]{0:T(128)S(1)} %pad_add_fusion.place_ref, bf16[16,4,104,128]{3,2,1,0:T(8,128)(2,1)S(1)} %bitcast.19, s32[2,128]{1,0:T(2,128)S(1)} %bitcast.21, f32[2,128]{1,0:T(2,128)S(1)} %bitcast.22, ...), custom_call_target="tpu_custom_call" | custom-call | flops 1409286144 | bytes 3523215 | tf_op jit(solution)/shard_map/pallas_call | solution.py:197
  75.4 0.0 collective-permute-done.x_ref
  75.4 0.0 copy-done
  75.4 3.0 %shard_map.66 = (bf16[384,448]{1,0:T(8,128)(2,1)S(1)}, bf16[4,8,96,128]{3,2,1,0:T(8,128)(2,1)S(1)}) custom-call(s32[2]{0:T(128)S(1)} %pad_add_fusion.place_ref, bf16[16,4,104,128]{3,2,1,0:T(8,128)(2,1)S(1)} %collective-permute-done.x_ref, f32[384,448]{1,0:T(8,128)S(1)} %get-tuple-element.18.gate_ref, f32[384,448]{1,0:T(8,128)S(1)} %get-tuple-element.19.up_ref, ...), custom_call_target="tpu_custom_call" | custom-call | flops 1761607680 | bytes 4404019 | tf_op jit(solution)/shard_map/pallas_call | solution.py:213
  78.5 0.4 collective-permute-start.2
  78.8 1.2 shard_map.68
  80.0 0.4 collective-permute-start.1
  80.4 1.2 shard_map.69.mine_ref
  81.6 0.0 collective-permute-done.2.arrived_ref
  81.6 0.1 shard_map.70
  81.7 0.1 collective-permute-start.3
  81.9 3.2 %collective-permute-start.4 = (bf16[4,4,96,128]{3,2,1,0:T(8,128)(2,1)S(1)}, bf16[4,4,96,128]{3,2,1,0:T(8,128)(2,1)S(1)}, u32[]{:S(2)}, u32[]{:S(2)}) collective-permute-start(bf16[4,4,96,128]{3,2,1,0:T(8,128)(2,1)S(1)} %get-tuple-element.24), channel_id=1, source_target_pairs={{0,30},{2,0},{4,2},{6,4},{8,6},{10,8},{12,10},{14,12},{16,14},{18,... | collective-permute-start | bytes 1179656 | tf_op jit(solution)/shard_map/ppermute | solution.py:223
  85.1 1.2 shard_map.67.mine_ref
  86.3 0.0 collective-permute-done.1.arrived_ref
  86.3 8.0 %collective-permute-done.3.low_ref = bf16[4,4,96,128]{3,2,1,0:T(8,128)(2,1)S(1)} collective-permute-done((bf16[4,4,96,128]{3,2,1,0:T(8,128)(2,1)S(1)}, bf16[4,4,96,128]{3,2,1,0:T(8,128)(2,1)S(1)}, u32[]{:S(2)}, u32[]{:S(2)}) %collective-permute-start.3) | collective-permute-done | bytes 393248 | tf_op jit(solution)/shard_map/ppermute | solution.py:222
  94.3 0.0 collective-permute-done.4.high_ref
  94.4 0.2 shard_map.71
  94.6 14.6 %all_to_all.16.results_ref = bf16[4,8,96,128]{3,2,1,0:T(8,128)(2,1)S(1)} all-to-all(bf16[4,8,96,128]{3,2,1,0:T(8,128)(2,1)S(1)} %shard_map.71), channel_id=1, replica_groups=mesh['groups'=2,'expert'=4,'z_0'=8,'z_1'=2,'core'=2] {'expert'}, dimensions={0} | all-to-all | bytes 1572864 | tf_op jit(solution)/shard_map/all_to_all | solution.py:228
  109.2 0.3 shard_map.72
  109.5 23.7 %all_to_all.17 = bf16[8,128,128]{2,1,0:T(8,128)(2,1)S(1)} all-to-all(bf16[8,128,128]{2,1,0:T(8,128)(2,1)S(1)} %shard_map.72), channel_id=1, replica_groups=mesh['groups'=2,'expert'=4,'z_0'=8,'z_1'=2,'core'=2] {'z_0'}, dimensions={0} | all-to-all | bytes 524288 | tf_op jit(solution)/shard_map/all_to_all | solution.py:230
  133.1 0.7 reduce_sum.12
  (1 shorter events, 0.0 us)
Async XLA Ops:
  0.1 0.8 copy-start.2
  0.8 0.7 copy-start.3
  12.1 59.0 %copy-start.1 = (bf16[1,4096,448]{1,2,0:T(8,128)(2,1)S(1)}, bf16[1,4096,448]{1,2,0:T(8,128)(2,1)}, u32[]{:S(2)}) copy-start(bf16[1,4096,448]{1,2,0:T(8,128)(2,1)} %param.9) | copy-start | bytes 11010052
  70.6 0.7 copy-start.4
  70.6 0.7 copy-start.5
  70.9 4.5 %collective-permute-start = (bf16[16,4,104,128]{3,2,1,0:T(8,128)(2,1)S(1)}, bf16[16,4,104,128]{3,2,1,0:T(8,128)(2,1)S(1)}, u32[]{:S(2)}, u32[]{:S(2)}) collective-permute-start(bf16[16,4,104,128]{3,2,1,0:T(8,128)(2,1)S(1)} %bitcast.18), channel_id=1, source_target_pairs={{0,1},{1,0},{2,3},{3,2},{4,5},{5,4},{6,7},{7,6},{8,9},{9,8},{10,11... | collective-permute-start | bytes 5111816 | tf_op jit(solution)/shard_map/ppermute | solution.py:191
  71.3 4.1 %copy-start = (bf16[1,448,4096]{2,1,0:T(8,128)(2,1)S(1)}, bf16[1,448,4096]{2,1,0:T(8,128)(2,1)}, u32[]{:S(2)}) copy-start(bf16[1,448,4096]{2,1,0:T(8,128)(2,1)} %param.11) | copy-start | bytes 11010052
  78.5 3.1 %collective-permute-start.2 = (bf16[4,8,96,128]{3,2,1,0:T(8,128)(2,1)S(1)}, bf16[4,8,96,128]{3,2,1,0:T(8,128)(2,1)S(1)}, u32[]{:S(2)}, u32[]{:S(2)}) collective-permute-start(bf16[4,8,96,128]{3,2,1,0:T(8,128)(2,1)S(1)} %get-tuple-element.22), channel_id=1, source_target_pairs={{0,1},{1,0},{2,3},{3,2},{4,5},{5,4},{6,7},{7,6},{8,9},{9,8},{10,11... | collective-permute-start | bytes 2359304 | tf_op jit(solution)/shard_map/ppermute | solution.py:219
  80.0 6.3 %collective-permute-start.1 = (bf16[4,8,96,128]{3,2,1,0:T(8,128)(2,1)S(1)}, bf16[4,8,96,128]{3,2,1,0:T(8,128)(2,1)S(1)}, u32[]{:S(2)}, u32[]{:S(2)}) collective-permute-start(bf16[4,8,96,128]{3,2,1,0:T(8,128)(2,1)S(1)} %shard_map.68), channel_id=1, source_target_pairs={{0,1},{1,0},{2,3},{3,2},{4,5},{5,4},{6,7},{7,6},{8,9},{9,8},{10,11... | collective-permute-start | bytes 2359304 | tf_op jit(solution)/shard_map/ppermute | solution.py:224
  81.7 12.6 %collective-permute-start.3 = (bf16[4,4,96,128]{3,2,1,0:T(8,128)(2,1)S(1)}, bf16[4,4,96,128]{3,2,1,0:T(8,128)(2,1)S(1)}, u32[]{:S(2)}, u32[]{:S(2)}) collective-permute-start(bf16[4,4,96,128]{3,2,1,0:T(8,128)(2,1)S(1)} %get-tuple-element.23), channel_id=1, source_target_pairs={{0,2},{2,4},{4,6},{6,8},{8,10},{10,12},{12,14},{14,16},{16,18},{18... | collective-permute-start | bytes 1179656 | tf_op jit(solution)/shard_map/ppermute | solution.py:222
  81.9 12.5 %collective-permute-start.4 = (bf16[4,4,96,128]{3,2,1,0:T(8,128)(2,1)S(1)}, bf16[4,4,96,128]{3,2,1,0:T(8,128)(2,1)S(1)}, u32[]{:S(2)}, u32[]{:S(2)}) collective-permute-start(bf16[4,4,96,128]{3,2,1,0:T(8,128)(2,1)S(1)} %get-tuple-element.24), channel_id=1, source_target_pairs={{0,30},{2,0},{4,2},{6,4},{8,6},{10,8},{12,10},{14,12},{16,14},{18,... | collective-permute-start | bytes 1179656 | tf_op jit(solution)/shard_map/ppermute | solution.py:223

commit v8 on v7

--- a/solution.py
+++ b/solution.py
@@ -7,6 +7,7 @@
 from jax.experimental.pallas import tpu as pltpu
 from jax.sharding import Mesh
 from jax.sharding import PartitionSpec as P
+
 
 CAP = 96
 CORES = 2
@@ -46,8 +47,14 @@
     return jnp.concatenate(parts, axis=0).astype(jnp.bfloat16)
 
 
-def dispatch_body(routes_ref, tokens_ref, out_ref):
+def dispatch_body(routes_in, tokens_in, out_ref, routes_ref, tokens_ref, sems):
     experts, rows, lanes = out_ref.shape
+    pairs = ((routes_in, routes_ref), (tokens_in, tokens_ref))
+    copies = [pltpu.make_async_copy(source, target, sems.at[i]) for i, (source, target) in enumerate(pairs)]
+    for copy in copies:
+        copy.start()
+    for copy in copies:
+        copy.wait()
     tokens = tokens_ref[...]
     largest = jnp.max(jnp.abs(tokens.astype(jnp.float32)))
     scale, mark = jnp.float32(2.0**TOP), jnp.float32(1.0)
@@ -77,20 +84,6 @@
     return side_by_side([ref[:, pl.ds(pl.multiple_of((z * CORES + core) * LANES, LANES), LANES)] for z in chips])
 
 
-def up_partial(core, x_ref, w_ref, copies=None):
-    step = x_ref.shape[0] // CHUNKS
-    total = None
-    for k in range(CHUNKS):
-        x = side_by_side([unscaled(x_ref, z) for z in range(k * step, (k + 1) * step)])
-        if copies is not None:
-            copies[k].wait()
-        part = lax.dot_general(
-            x, core_columns(w_ref, core, range(k * step, (k + 1) * step)), (((1,), (1,)), ((), ())), preferred_element_type=jnp.float32
-        )
-        total = part if k == 0 else total + part
-    return total
-
-
 def down_into(hidden, core, parity, wd_ref, out_ref):
     blocks, count, cap, lanes = out_ref.shape
     step = 4
@@ -101,28 +94,32 @@
             out_ref[:, k + z] = part[:, z * lanes : (z + 1) * lanes].reshape(blocks, cap, lanes)
 
 
-def first_half_body(
-    place_ref, x_ref, routes_ref, weights_ref, wg_ref, wu_ref, gate_ref, up_ref, u_here, table_ref, sems
-):
-    copies = column_copies(wu_ref, u_here, sems)
-    for copy in copies:
+def up_body(place_ref, x_ref, wg_ref, wu_ref, wd_ref, hidden_ref, out_ref, d_here, u_buf, x_buf, sems):
+    core, parity = place_ref[0], place_ref[1]
+    ups = column_copies(wu_ref, u_buf, sems.at[0])
+    downs = column_copies(wd_ref, d_here, sems.at[1])
+    for copy in ups + downs:
         copy.start()
-
-    def weight_of(e):
-        return sum(jnp.where(routes_ref[k : k + 1, :] == e, weights_ref[k : k + 1, :], 0.0) for k in range(2))
-
-    table_ref[...] = slot_table(routes_ref, CAP, x_ref.shape[1], weight_of).T
-    gate_ref[...] = up_partial(place_ref[0], x_ref, wg_ref)
-    up_ref[...] = up_partial(place_ref[0], x_ref, u_here, copies)
-
-
-def second_half_body(place_ref, x_ref, gate_ref, up_ref, wg_ref, wu_ref, wd_ref, hidden_ref, out_ref):
-    core, parity = place_ref[0], place_ref[1]
-    gate = up_partial(1 - core, x_ref, wg_ref) + gate_ref[...]
-    up = up_partial(1 - core, x_ref, wu_ref) + up_ref[...]
+    step = x_ref.shape[0] // CHUNKS
+    spans = [slice(k * step * LANES, (k + 1) * step * LANES) for k in range(CHUNKS)]
+
+    def part(x, w):
+        return lax.dot_general(x, w, (((1,), (1,)), ((), ())), preferred_element_type=jnp.float32)
+
+    gate = up = None
+    for k, span in enumerate(spans):
+        x = side_by_side([unscaled(x_ref, z) for z in range(k * step, (k + 1) * step)])
+        x_buf[:, span] = x
+        gate = part(x, wg_ref[:, span]) if k == 0 else gate + part(x, wg_ref[:, span])
+    for k, span in enumerate(spans):
+        ups[k].wait()
+        more = part(x_buf[:, span], u_buf[:, span])
+        up = more if k == 0 else up + more
     hidden = (gate / (1.0 + jnp.exp(-gate)) * up).astype(hidden_ref.dtype)
     hidden_ref[...] = hidden
-    down_into(hidden, 1 - core, 1 - parity, wd_ref, out_ref)
+    for copy in downs:
+        copy.wait()
+    down_into(hidden, 1 - core, 1 - parity, d_here, out_ref)
 
 
 def down_body(place_ref, hidden_ref, wd_ref, out_ref, *, own_core, own_parity):
@@ -130,6 +127,14 @@
     down_into(
         hidden_ref[...], core if own_core else 1 - core, parity if own_parity else 1 - parity, wd_ref, out_ref
     )
+
+
+def last_down_body(place_ref, hidden_ref, wd_ref, routes_ref, weights_ref, out_ref, table_ref):
+    def weight_of(e):
+        return sum(jnp.where(routes_ref[k : k + 1, :] == e, weights_ref[k : k + 1, :], 0.0) for k in range(2))
+
+    table_ref[...] = slot_table(routes_ref, out_ref.shape[2], out_ref.shape[0], weight_of).T
+    down_into(hidden_ref[...], place_ref[0], place_ref[1], wd_ref, out_ref)
 
 
 def outgoing_body(mine_ref, arrived_ref, right_ref, left_ref):
@@ -169,7 +174,7 @@
     )
 
 
-def shards(tokens, route_ids, gate_weights, w_gate, w_up, w_down):
+def layer(tokens, route_ids, gate_weights, w_gate, w_up, w_down):
     experts = lax.axis_size("expert")
     chips = lax.axis_size(Z)
     token_count, lanes = tokens.shape
@@ -185,44 +190,46 @@
     swap = functools.partial(lax.ppermute, axis_name="core", perm=[(0, 1), (1, 0)])
     exchange = functools.partial(lax.all_to_all, split_axis=0, concat_axis=0, tiled=True)
 
-    picked = call(dispatch_body, shape((experts, CAP + MARK_ROWS, lanes), bf16), (VMEM, VMEM))(routes, tokens)
+    first_routes, first_tokens, up_rows, down_rows = (
+        pltpu.with_memory_space_constraint(v, pltpu.HBM) for v in (routes, tokens, w_up[0].T, w_down[0])
+    )
+    picked = call(
+        dispatch_body,
+        shape((experts, CAP + MARK_ROWS, lanes), bf16),
+        (HBM, HBM),
+        [pltpu.VMEM(routes.shape, routes.dtype), pltpu.VMEM(tokens.shape, tokens.dtype), pltpu.SemaphoreType.DMA((2,))],
+    )(first_routes, first_tokens)
     slices = exchange(picked.astype(jnp.float16), "expert")
-    own = lax.all_gather(slices, Z, axis=0, tiled=False).astype(bf16)
-    other = swap(own)
-
-    gate_rows, up_rows, down_rows = w_gate[0].T, w_up[0].T, w_down[0]
-    up_rows = pltpu.with_memory_space_constraint(up_rows, pltpu.HBM)
-    up_flops = 2 * slots * width * width_in
-    acc = shape((slots, width), f32)
-    gate_half, up_half, up_here, combine_table = call(
-        first_half_body,
-        (acc, acc, shape((width, width_in), bf16), shape((token_count, slots), bf16)),
-        (SMEM, VMEM, VMEM, VMEM, VMEM, HBM),
-        [pltpu.SemaphoreType.DMA((CHUNKS,))],
-        flops=up_flops,
-    )(place, own, routes, weights, gate_rows, up_rows)
+    rows = lax.all_gather(slices, ETP, axis=0, tiled=False).astype(bf16)
+
     of_parity = chips // PARITIES
     half = shape((experts, of_parity, CAP, lanes), bf16)
     quarter = shape((experts, of_parity // 2, CAP, lanes), bf16)
     wide = shape(half.shape, f32)
-
-    def down(out, **which):
-        body = functools.partial(down_body, **which)
-        return call(body, out, (SMEM, VMEM, VMEM), flops=up_flops // 4)(place, hidden, down_rows)
-
-    hidden, theirs_away = call(
-        second_half_body,
-        (shape((slots, width), bf16), half),
-        (SMEM, VMEM, VMEM, VMEM, VMEM, VMEM, VMEM),
-        flops=up_flops * 5 // 4,
-    )(place, other, gate_half, up_half, gate_rows, up_here, down_rows)
+    held = shape((width, width_in), bf16)
+    down_flops = slots * width * width_in // 2
+
+    hidden, theirs_away, down_here = call(
+        up_body,
+        (shape((slots, width), bf16), half, held),
+        (SMEM, VMEM, VMEM, HBM, HBM),
+        [pltpu.VMEM(held.shape, bf16), pltpu.VMEM((slots, width_in), bf16), pltpu.SemaphoreType.DMA((2, CHUNKS))],
+        flops=9 * down_flops,
+    )(place, rows, w_gate[0].T, up_rows, down_rows)
     arrived_away = swap(theirs_away)
-    mine_away = down(wide, own_core=True, own_parity=False)
+    mine_away = call(
+        functools.partial(down_body, own_core=True, own_parity=False), wide, (SMEM, VMEM, VMEM), flops=down_flops
+    )(place, hidden, down_here)
     right, left = call(outgoing_body, (quarter, quarter), (VMEM, VMEM))(mine_away, arrived_away)
     low = lax.ppermute(right, Z, [(z, (z + 1) % chips) for z in range(chips)])
     high = lax.ppermute(left, Z, [(z, (z - 1) % chips) for z in range(chips)])
-    arrived = swap(down(half, own_core=False, own_parity=True))
-    mine = down(wide, own_core=True, own_parity=True)
+    theirs = call(
+        functools.partial(down_body, own_core=False, own_parity=True), half, (SMEM, VMEM, VMEM), flops=down_flops
+    )(place, hidden, down_here)
+    arrived = swap(theirs)
+    mine, combine_table = call(
+        last_down_body, (wide, shape((token_count, slots), bf16)), (SMEM,) + (VMEM,) * 4, flops=down_flops
+    )(place, hidden, down_here, routes, weights)
     paired = call(pair_body, half, (VMEM,) * 4)(mine, arrived, low, high)
 
     results = exchange(paired, "expert")
@@ -245,6 +252,4 @@
         P("expert", None, ETP),
         P("expert", ETP, None),
     )
-    return jax.shard_map(
-        shards, mesh=finer, in_specs=placed, out_specs=P(("groups", "expert"), ETP), check_vma=False
-    )
+    return jax.shard_map(layer, mesh=finer, in_specs=placed, out_specs=P(("groups", "expert"), ETP), check_vma=False)

time: 134 us -> 134 us (level)
    pallas_call x9 -> x8, Pallas kernels: 11.6 us -> 10.7 us  [the longest x1 5.4 us: layer(): call(up_body, (shape((slots, width), bf16), half, held), (SMEM, VMEM, VME...]
    ppermute x5 -> x4, starting transfers between devices: 4.24 us -> 4.11 us  [the longest x1 1.81 us: layer(): high = lax.ppermute(left, Z, [(z, (z - 1) % chips) for z in range(chips)])]
    ppermute x5 -> x4, waiting for transfers between devices: 8.05 us -> 8.18 us  [the longest x1 8.17 us: layer(): low = lax.ppermute(right, Z, [(z, (z + 1) % chips) for z in range(chips)])]
  transfers between devices with their start and end apart: 5 -> 4, of which waited for: 1 -> 1; matrix products, arithmetic and copies ran while one was open for 0% -> 0% of each run, Pallas kernels for 6% -> 3%
where the time goes in v8:
time: 134 us
  blocking collectives  108 us (81%)
  Pallas kernels  10.7 us (8%)
  waiting for transfers between devices  8.18 us (6%)
  starting transfers between devices  4.11 us (3%)
  local copies, waits for them, and re-layouts  1.46 us (1%)
  other arithmetic  1.34 us (1%)
    all_gather x1, blocking collectives, layer(): rows = lax.all_gather(slices, ETP, axis=0, tiled=False).astype(bf16)  59.5 us
    all_to_all x1, blocking collectives, layer(): pieces = exchange(blended, 'z_0')  23.6 us
    all_to_all x1, blocking collectives, layer(): results = exchange(paired, 'expert')  14.7 us
    all_to_all x1, blocking collectives, layer(): slices = exchange(picked.astype(jnp.float16), 'expert')  10.2 us
    ppermute x1, waiting for transfers between devices, layer(): low = lax.ppermute(right, Z, [(z, (z + 1) % chips) for z in range(chips)])  8.17 us
    pallas_call x1, Pallas kernels, layer(): call(up_body, (shape((slots, width), bf16), half, held), (SMEM, VMEM, VME...  5.4 us
  transfers between devices with their start and end apart: 4, of which 1 were waited for; matrix products, arithmetic and copies ran while one was open for 0% of the time, Pallas kernels for 3%

profile of v8, /device:TPU:40, one launch (start us, length us, event | category | flops | bytes accessed | tf_op | source)
XLA Modules:
  0.0 133.9 jit_solution(16702673073395165367)
XLA Ops:
  0.0 0.1 pad_add_fusion.place_ref
  0.1 1.1 shard_map.64
  1.2 10.2 %all_to_all.15 = f16[4,104,128]{2,1,0:T(8,128)(2,1)S(1)} all-to-all(f16[4,104,128]{2,1,0:T(8,128)(2,1)S(1)} %convert_element_type.8), channel_id=1, replica_groups=mesh['groups'=2,'expert'=4,'z_0'=8,'z_1'=2,'core'=2] {'expert'}, dimensions={0} | all-to-all | bytes 212992 | tf_op jit(solution)/shard_map/all_to_all | solution.py:202
  11.4 59.5 %all-gather.2 = f16[128,104,128]{2,1,0:T(8,128)(2,1)S(1)} all-gather(f16[4,104,128]{2,1,0:T(8,128)(2,1)S(1)} %all_to_all.15), channel_id=2, replica_groups=mesh['groups'=2,'expert'=4,'z_0'=8,'z_1'=2,'core'=2] {'z_0','z_1','core'}, dimensions={0}, use_global_device_ids=true | all-gather | bytes 3514368 | tf_op jit(solution)/shard_map/all_gather | solution.py:203
  70.9 0.0 copy-start
  70.9 0.6 convert_element_type.10
  71.5 1.4 %copy-done = bf16[1,4096,448]{1,2,0:T(8,128)(2,1)S(1)} copy-done((bf16[1,4096,448]{1,2,0:T(8,128)(2,1)S(1)}, bf16[1,4096,448]{1,2,0:T(8,128)(2,1)}, u32[]{:S(2)}) %copy-start) | copy-done | bytes 3670040
  73.0 5.4 %shard_map.65 = (bf16[384,448]{1,0:T(8,128)(2,1)S(1)}, bf16[4,8,96,128]{3,2,1,0:T(8,128)(2,1)S(1)}, bf16[448,4096]{1,0:T(8,128)(2,1)S(1)}) custom-call(s32[2]{0:T(128)S(1)} %pad_add_fusion.place_ref, bf16[32,4,104,128]{3,2,1,0:T(8,128)(2,1)S(1)} %bitcast.12, bf16[448,4096]{1,0:T(8,128)(2,1)S(1)} %bitcast.13, bf16[448,4096]{1,0:T(8,128)(2,1)} %bitcast.17, ...), custom_call_target="tpu_custom_call" | custom-call | flops 3170893824 | bytes 7927234 | tf_op jit(solution)/shard_map/pallas_call | solution.py:212
  78.4 0.5 collective-permute-start.1
  78.9 1.2 shard_map.67
  80.0 0.0 copy-start.1
  80.1 0.0 copy-start.2
  80.1 0.3 collective-permute-start
  80.4 1.2 shard_map.68.mine_ref
  81.5 0.0 collective-permute-done.1.arrived_ref
  81.5 0.1 shard_map.69
  81.7 1.5 %collective-permute-start.2 = (bf16[4,4,96,128]{3,2,1,0:T(8,128)(2,1)S(1)}, bf16[4,4,96,128]{3,2,1,0:T(8,128)(2,1)S(1)}, u32[]{:S(2)}, u32[]{:S(2)}) collective-permute-start(bf16[4,4,96,128]{3,2,1,0:T(8,128)(2,1)S(1)} %get-tuple-element.21), channel_id=1, source_target_pairs={{0,2},{2,4},{4,6},{6,8},{8,10},{10,12},{12,14},{14,16},{16,18},{18... | collective-permute-start | bytes 1179656 | tf_op jit(solution)/shard_map/ppermute | solution.py:224
  83.2 1.8 %collective-permute-start.3 = (bf16[4,4,96,128]{3,2,1,0:T(8,128)(2,1)S(1)}, bf16[4,4,96,128]{3,2,1,0:T(8,128)(2,1)S(1)}, u32[]{:S(2)}, u32[]{:S(2)}) collective-permute-start(bf16[4,4,96,128]{3,2,1,0:T(8,128)(2,1)S(1)} %get-tuple-element.22), channel_id=1, source_target_pairs={{0,30},{2,0},{4,2},{6,4},{8,6},{10,8},{12,10},{14,12},{16,14},{18,... | collective-permute-start | bytes 1179656 | tf_op jit(solution)/shard_map/ppermute | solution.py:225
  85.0 0.0 copy-done.1
  85.0 0.0 copy-done.2
  85.0 1.2 shard_map.66
  86.2 0.0 collective-permute-done.arrived_ref
  86.2 8.2 %collective-permute-done.2.low_ref = bf16[4,4,96,128]{3,2,1,0:T(8,128)(2,1)S(1)} collective-permute-done((bf16[4,4,96,128]{3,2,1,0:T(8,128)(2,1)S(1)}, bf16[4,4,96,128]{3,2,1,0:T(8,128)(2,1)S(1)}, u32[]{:S(2)}, u32[]{:S(2)}) %collective-permute-start.2) | collective-permute-done | bytes 393248 | tf_op jit(solution)/shard_map/ppermute | solution.py:224
  94.4 0.0 collective-permute-done.3.high_ref
  94.4 0.2 shard_map.70
  94.7 14.7 %all_to_all.16.results_ref = bf16[4,8,96,128]{3,2,1,0:T(8,128)(2,1)S(1)} all-to-all(bf16[4,8,96,128]{3,2,1,0:T(8,128)(2,1)S(1)} %shard_map.70), channel_id=1, replica_groups=mesh['groups'=2,'expert'=4,'z_0'=8,'z_1'=2,'core'=2] {'expert'}, dimensions={0} | all-to-all | bytes 1572864 | tf_op jit(solution)/shard_map/all_to_all | solution.py:235
  109.3 0.3 shard_map.71
  109.7 23.6 %all_to_all.17 = bf16[8,128,128]{2,1,0:T(8,128)(2,1)S(1)} all-to-all(bf16[8,128,128]{2,1,0:T(8,128)(2,1)S(1)} %shard_map.71), channel_id=1, replica_groups=mesh['groups'=2,'expert'=4,'z_0'=8,'z_1'=2,'core'=2] {'z_0'}, dimensions={0} | all-to-all | bytes 524288 | tf_op jit(solution)/shard_map/all_to_all | solution.py:237
  133.3 0.7 reduce_sum.12
  (1 shorter events, 0.0 us)
Async XLA Ops:
  70.9 2.0 %copy-start = (bf16[1,4096,448]{1,2,0:T(8,128)(2,1)S(1)}, bf16[1,4096,448]{1,2,0:T(8,128)(2,1)}, u32[]{:S(2)}) copy-start(bf16[1,4096,448]{1,2,0:T(8,128)(2,1)} %param.9) | copy-start | bytes 11010052
  78.4 3.2 %collective-permute-start.1 = (bf16[4,8,96,128]{3,2,1,0:T(8,128)(2,1)S(1)}, bf16[4,8,96,128]{3,2,1,0:T(8,128)(2,1)S(1)}, u32[]{:S(2)}, u32[]{:S(2)}) collective-permute-start(bf16[4,8,96,128]{3,2,1,0:T(8,128)(2,1)S(1)} %get-tuple-element.20), channel_id=1, source_target_pairs={{0,1},{1,0},{2,3},{3,2},{4,5},{5,4},{6,7},{7,6},{8,9},{9,8},{10,11... | collective-permute-start | bytes 2359304 | tf_op jit(solution)/shard_map/ppermute | solution.py:219
  80.0 5.0 %copy-start.1 = (s32[128,2]{0,1:T(2,128)S(1)}, s32[128,2]{0,1:T(2,128)}, u32[]{:S(2)}) copy-start(s32[128,2]{0,1:T(2,128)} %param.7) | copy-start | bytes 3076
  80.1 5.0 %copy-start.2 = (f32[128,2]{0,1:T(2,128)S(1)}, f32[128,2]{0,1:T(2,128)}, u32[]{:S(2)}) copy-start(f32[128,2]{0,1:T(2,128)} %param.8) | copy-start | bytes 3076
  80.1 6.1 %collective-permute-start = (bf16[4,8,96,128]{3,2,1,0:T(8,128)(2,1)S(1)}, bf16[4,8,96,128]{3,2,1,0:T(8,128)(2,1)S(1)}, u32[]{:S(2)}, u32[]{:S(2)}) collective-permute-start(bf16[4,8,96,128]{3,2,1,0:T(8,128)(2,1)S(1)} %shard_map.67), channel_id=1, source_target_pairs={{0,1},{1,0},{2,3},{3,2},{4,5},{5,4},{6,7},{7,6},{8,9},{9,8},{10,11... | collective-permute-start | bytes 2359304 | tf_op jit(solution)/shard_map/ppermute | solution.py:229
  81.7 12.7 %collective-permute-start.2 = (bf16[4,4,96,128]{3,2,1,0:T(8,128)(2,1)S(1)}, bf16[4,4,96,128]{3,2,1,0:T(8,128)(2,1)S(1)}, u32[]{:S(2)}, u32[]{:S(2)}) collective-permute-start(bf16[4,4,96,128]{3,2,1,0:T(8,128)(2,1)S(1)} %get-tuple-element.21), channel_id=1, source_target_pairs={{0,2},{2,4},{4,6},{6,8},{8,10},{10,12},{12,14},{14,16},{16,18},{18... | collective-permute-start | bytes 1179656 | tf_op jit(solution)/shard_map/ppermute | solution.py:224
  83.2 11.2 %collective-permute-start.3 = (bf16[4,4,96,128]{3,2,1,0:T(8,128)(2,1)S(1)}, bf16[4,4,96,128]{3,2,1,0:T(8,128)(2,1)S(1)}, u32[]{:S(2)}, u32[]{:S(2)}) collective-permute-start(bf16[4,4,96,128]{3,2,1,0:T(8,128)(2,1)S(1)} %get-tuple-element.22), channel_id=1, source_target_pairs={{0,30},{2,0},{4,2},{6,4},{8,6},{10,8},{12,10},{14,12},{16,14},{18,... | collective-permute-start | bytes 1179656 | tf_op jit(solution)/shard_map/ppermute | solution.py:225

commit v9 on v8

--- a/solution.py
+++ b/solution.py
@@ -15,9 +15,6 @@
 ETP = (*Z, "core")
 LANES = 128
 CHUNKS = 4
-TOP = 12
-LEVELS = 14
-MARK_ROWS = 8
 PARITIES = 2
 
 HBM = pl.BlockSpec(memory_space=pltpu.HBM)
@@ -47,31 +44,13 @@
     return jnp.concatenate(parts, axis=0).astype(jnp.bfloat16)
 
 
-def dispatch_body(routes_in, tokens_in, out_ref, routes_ref, tokens_ref, sems):
-    experts, rows, lanes = out_ref.shape
-    pairs = ((routes_in, routes_ref), (tokens_in, tokens_ref))
-    copies = [pltpu.make_async_copy(source, target, sems.at[i]) for i, (source, target) in enumerate(pairs)]
-    for copy in copies:
-        copy.start()
-    for copy in copies:
-        copy.wait()
-    tokens = tokens_ref[...]
-    largest = jnp.max(jnp.abs(tokens.astype(jnp.float32)))
-    scale, mark = jnp.float32(2.0**TOP), jnp.float32(1.0)
-    for level in range(1, LEVELS):
-        lower = largest < 2.0 ** (15 - TOP - 8 * level)
-        scale = jnp.where(lower, 2.0 ** (TOP + 8 * level), scale)
-        mark = jnp.where(lower, 2.0**-level, mark)
-    picked = dot32(slot_table(routes_ref, CAP, experts, lambda e: 1.0), tokens) * scale
-    out_ref[:, :CAP] = picked.astype(out_ref.dtype).reshape(experts, CAP, lanes)
-    out_ref[:, CAP:] = jnp.full((experts, rows - CAP, lanes), mark, jnp.float32).astype(out_ref.dtype)
-
-
-def unscaled(tile_ref, z):
-    mark = tile_ref[z, :, CAP : CAP + 1].astype(jnp.float32)
-    for _ in range(3):
-        mark = mark * mark
-    return tile_ref[z, :, :CAP] * (mark * 2.0**-TOP).astype(tile_ref.dtype)
+def dispatch_body(routes_ref, tokens_ref, out_ref):
+    experts, chips, cap, lanes = out_ref.shape
+    table = slot_table(routes_ref, cap, experts, lambda e: 1.0)
+    for z in range(0, chips, 2):
+        rows = dot32(table, side_by_side([tokens_ref[z], tokens_ref[z + 1]])).astype(out_ref.dtype)
+        for k in range(2):
+            out_ref[:, z + k] = rows[:, k * lanes : (k + 1) * lanes].reshape(experts, cap, lanes)
 
 
 def column_copies(w_ref, buf, sems):
@@ -94,32 +73,38 @@
             out_ref[:, k + z] = part[:, z * lanes : (z + 1) * lanes].reshape(blocks, cap, lanes)
 
 
-def up_body(place_ref, x_ref, wg_ref, wu_ref, wd_ref, hidden_ref, out_ref, d_here, u_buf, x_buf, sems):
+def up_partial(core, x_ref, w_ref, copies=None):
+    step = x_ref.shape[1] // CHUNKS
+    total = None
+    for k in range(CHUNKS):
+        chips = range(k * step, (k + 1) * step)
+        if copies is not None:
+            copies[k].wait()
+        part = lax.dot_general(
+            side_by_side([x_ref[:, z] for z in chips]),
+            core_columns(w_ref, core, chips),
+            (((1,), (1,)), ((), ())),
+            preferred_element_type=jnp.float32,
+        )
+        total = part if k == 0 else total + part
+    return total
+
+
+def first_half_body(place_ref, x_ref, wg_ref, wu_ref, gate_ref, up_ref, u_here, sems):
+    copies = column_copies(wu_ref, u_here, sems)
+    for copy in copies:
+        copy.start()
+    gate_ref[...] = up_partial(place_ref[0], x_ref, wg_ref)
+    up_ref[...] = up_partial(place_ref[0], x_ref, u_here, copies)
+
+
+def second_half_body(place_ref, x_ref, gate_ref, up_ref, wg_ref, wu_ref, wd_ref, hidden_ref, out_ref):
     core, parity = place_ref[0], place_ref[1]
-    ups = column_copies(wu_ref, u_buf, sems.at[0])
-    downs = column_copies(wd_ref, d_here, sems.at[1])
-    for copy in ups + downs:
-        copy.start()
-    step = x_ref.shape[0] // CHUNKS
-    spans = [slice(k * step * LANES, (k + 1) * step * LANES) for k in range(CHUNKS)]
-
-    def part(x, w):
-        return lax.dot_general(x, w, (((1,), (1,)), ((), ())), preferred_element_type=jnp.float32)
-
-    gate = up = None
-    for k, span in enumerate(spans):
-        x = side_by_side([unscaled(x_ref, z) for z in range(k * step, (k + 1) * step)])
-        x_buf[:, span] = x
-        gate = part(x, wg_ref[:, span]) if k == 0 else gate + part(x, wg_ref[:, span])
-    for k, span in enumerate(spans):
-        ups[k].wait()
-        more = part(x_buf[:, span], u_buf[:, span])
-        up = more if k == 0 else up + more
+    gate = up_partial(1 - core, x_ref, wg_ref) + gate_ref[...]
+    up = up_partial(1 - core, x_ref, wu_ref) + up_ref[...]
     hidden = (gate / (1.0 + jnp.exp(-gate)) * up).astype(hidden_ref.dtype)
     hidden_ref[...] = hidden
-    for copy in downs:
-        copy.wait()
-    down_into(hidden, 1 - core, 1 - parity, d_here, out_ref)
+    down_into(hidden, 1 - core, 1 - parity, wd_ref, out_ref)
 
 
 def down_body(place_ref, hidden_ref, wd_ref, out_ref, *, own_core, own_parity):
@@ -190,46 +175,47 @@
     swap = functools.partial(lax.ppermute, axis_name="core", perm=[(0, 1), (1, 0)])
     exchange = functools.partial(lax.all_to_all, split_axis=0, concat_axis=0, tiled=True)
 
-    first_routes, first_tokens, up_rows, down_rows = (
-        pltpu.with_memory_space_constraint(v, pltpu.HBM) for v in (routes, tokens, w_up[0].T, w_down[0])
-    )
+    gathered = lax.all_gather(tokens, Z, axis=0, tiled=False)
     picked = call(
-        dispatch_body,
-        shape((experts, CAP + MARK_ROWS, lanes), bf16),
-        (HBM, HBM),
-        [pltpu.VMEM(routes.shape, routes.dtype), pltpu.VMEM(tokens.shape, tokens.dtype), pltpu.SemaphoreType.DMA((2,))],
-    )(first_routes, first_tokens)
-    slices = exchange(picked.astype(jnp.float16), "expert")
-    rows = lax.all_gather(slices, ETP, axis=0, tiled=False).astype(bf16)
+        dispatch_body, shape((experts, chips, CAP, lanes), bf16), (VMEM, VMEM), flops=2 * slots * token_count * chips * lanes
+    )(routes, gathered)
+    own = exchange(picked, "expert")
+    other = swap(own)
 
     of_parity = chips // PARITIES
     half = shape((experts, of_parity, CAP, lanes), bf16)
     quarter = shape((experts, of_parity // 2, CAP, lanes), bf16)
     wide = shape(half.shape, f32)
+    acc = shape((slots, width), f32)
     held = shape((width, width_in), bf16)
     down_flops = slots * width * width_in // 2
-
-    hidden, theirs_away, down_here = call(
-        up_body,
-        (shape((slots, width), bf16), half, held),
-        (SMEM, VMEM, VMEM, HBM, HBM),
-        [pltpu.VMEM(held.shape, bf16), pltpu.VMEM((slots, width_in), bf16), pltpu.SemaphoreType.DMA((2, CHUNKS))],
-        flops=9 * down_flops,
-    )(place, rows, w_gate[0].T, up_rows, down_rows)
+    gate_rows, up_rows, down_rows = w_gate[0].T, w_up[0].T, w_down[0]
+    up_rows = pltpu.with_memory_space_constraint(up_rows, pltpu.HBM)
+
+    gate_half, up_half, up_here = call(
+        first_half_body,
+        (acc, acc, held),
+        (SMEM, VMEM, VMEM, HBM),
+        [pltpu.SemaphoreType.DMA((CHUNKS,))],
+        flops=4 * down_flops,
+    )(place, own, gate_rows, up_rows)
+    hidden, theirs_away = call(
+        second_half_body, (shape((slots, width), bf16), half), (SMEM,) + (VMEM,) * 6, flops=5 * down_flops
+    )(place, other, gate_half, up_half, gate_rows, up_here, down_rows)
     arrived_away = swap(theirs_away)
     mine_away = call(
         functools.partial(down_body, own_core=True, own_parity=False), wide, (SMEM, VMEM, VMEM), flops=down_flops
-    )(place, hidden, down_here)
+    )(place, hidden, down_rows)
     right, left = call(outgoing_body, (quarter, quarter), (VMEM, VMEM))(mine_away, arrived_away)
     low = lax.ppermute(right, Z, [(z, (z + 1) % chips) for z in range(chips)])
     high = lax.ppermute(left, Z, [(z, (z - 1) % chips) for z in range(chips)])
     theirs = call(
         functools.partial(down_body, own_core=False, own_parity=True), half, (SMEM, VMEM, VMEM), flops=down_flops
-    )(place, hidden, down_here)
+    )(place, hidden, down_rows)
     arrived = swap(theirs)
     mine, combine_table = call(
         last_down_body, (wide, shape((token_count, slots), bf16)), (SMEM,) + (VMEM,) * 4, flops=down_flops
-    )(place, hidden, down_here, routes, weights)
+    )(place, hidden, down_rows, routes, weights)
     paired = call(pair_body, half, (VMEM,) * 4)(mine, arrived, low, high)
 
     results = exchange(paired, "expert")

time: 134 us -> 135 us (level)
    all_to_all x1, blocking collectives: 10.2 us -> 18.3 us  [layer(): own = exchange(picked, 'expert')]
    all_gather x1, blocking collectives: 59.5 us -> 51.5 us  [layer(): gathered = lax.all_gather(tokens, Z, axis=0, tiled=False)]
    ppermute x1, starting transfers between devices: 1.54 us -> 0.13 us  [layer(): low = lax.ppermute(right, Z, [(z, (z + 1) % chips) for z in range(chips)])]
    ppermute x1, starting transfers between devices: 1.81 us -> 3.21 us  [layer(): high = lax.ppermute(left, Z, [(z, (z - 1) % chips) for z in range(chips)])]
    pallas_call x2 -> x3, Pallas kernels: 6.49 us -> 7.65 us  [the longest x1 3.92 us: layer(): call(first_half_body, (acc, acc, held), (SMEM, VMEM, VMEM, HBM), [pltpu.S...]
  transfers between devices with their start and end apart: 4 -> 5, of which waited for: 1 -> 1; matrix products, arithmetic and copies ran while one was open for 0% -> 0% of each run, Pallas kernels for 3% -> 6%
where the time goes in v9:
time: 135 us
  blocking collectives  109 us (81%)
  Pallas kernels  11.9 us (9%)
  waiting for transfers between devices  8.31 us (6%)
  starting transfers between devices  4.11 us (3%)
    all_gather x1, blocking collectives, layer(): gathered = lax.all_gather(tokens, Z, axis=0, tiled=False)  51.5 us
    all_to_all x1, blocking collectives, layer(): pieces = exchange(blended, 'z_0')  24 us
    all_to_all x1, blocking collectives, layer(): own = exchange(picked, 'expert')  18.3 us
    all_to_all x1, blocking collectives, layer(): results = exchange(paired, 'expert')  14.8 us
    ppermute x1, waiting for transfers between devices, layer(): low = lax.ppermute(right, Z, [(z, (z + 1) % chips) for z in range(chips)])  8.3 us
    pallas_call x1, Pallas kernels, layer(): call(first_half_body, (acc, acc, held), (SMEM, VMEM, VMEM, HBM), [pltpu.S...  3.92 us
    ppermute x1, starting transfers between devices, layer(): high = lax.ppermute(left, Z, [(z, (z - 1) % chips) for z in range(chips)])  3.21 us
    pallas_call x1, Pallas kernels, layer(): call(second_half_body, (shape((slots, width), bf16), half), (SMEM,) + (VM...  3.05 us
  transfers between devices with their start and end apart: 5, of which 1 were waited for; matrix products, arithmetic and copies ran while one was open for 0% of the time, Pallas kernels for 6%

profile of v9, /device:TPU:40, one launch (start us, length us, event | category | flops | bytes accessed | tf_op | source)
XLA Modules:
  0.0 134.5 jit_solution(8747061669674229804)
XLA Ops:
  0.0 0.1 pad_add_fusion.place_ref
  0.1 51.5 %all-gather = bf16[2048,128]{1,0:T(8,128)(2,1)S(1)} all-gather(bf16[128,128]{1,0:T(8,128)(2,1)} %param.6), channel_id=2, replica_groups=mesh['groups'=2,'expert'=4,'z_0'=8,'z_1'=2,'core'=2] {'z_0','z_1'}, dimensions={0}, use_global_device_ids=true | all-gather | bytes 557056 | tf_op jit(solution)/shard_map/all_gather | solution.py:178
  51.6 0.0 copy-start.2
  51.6 0.7 copy-done.2
  52.3 0.0 copy-start.1
  52.3 0.7 shard_map.64
  53.0 18.3 %all_to_all.15.x_ref = bf16[4,16,96,128]{3,2,1,0:T(8,128)(2,1)S(1)} all-to-all(bf16[4,16,96,128]{3,2,1,0:T(8,128)(2,1)S(1)} %shard_map.64), channel_id=1, replica_groups=mesh['groups'=2,'expert'=4,'z_0'=8,'z_1'=2,'core'=2] {'expert'}, dimensions={0} | all-to-all | bytes 3145728 | tf_op jit(solution)/shard_map/all_to_all | solution.py:182
  71.3 0.0 collective-permute-start
  71.3 0.0 copy-done.1
  71.3 0.0 copy-start
  71.3 3.9 %shard_map.65 = (f32[384,448]{1,0:T(8,128)S(1)}, f32[384,448]{1,0:T(8,128)S(1)}, bf16[448,4096]{1,0:T(8,128)(2,1)S(1)}) custom-call(s32[2]{0:T(128)S(1)} %pad_add_fusion.place_ref, bf16[4,16,96,128]{3,2,1,0:T(8,128)(2,1)S(1)} %all_to_all.15.x_ref, bf16[448,4096]{1,0:T(8,128)(2,1)S(1)} %bitcast.16, bf16[448,4096]{1,0:T(8,128)(2,1)} %bitcast.22), custom_call_target="tpu_custom_call" | custom-call | flops 1409286144 | bytes 3523215 | tf_op jit(solution)/shard_map/pallas_call | solution.py:195
  75.2 0.0 collective-permute-done.x_ref
  75.2 0.0 copy-done
  75.2 3.1 %shard_map.66 = (bf16[384,448]{1,0:T(8,128)(2,1)S(1)}, bf16[4,8,96,128]{3,2,1,0:T(8,128)(2,1)S(1)}) custom-call(s32[2]{0:T(128)S(1)} %pad_add_fusion.place_ref, bf16[4,16,96,128]{3,2,1,0:T(8,128)(2,1)S(1)} %collective-permute-done.x_ref, f32[384,448]{1,0:T(8,128)S(1)} %get-tuple-element.18.gate_ref, f32[384,448]{1,0:T(8,128)S(1)} %get-tuple-element.19.up_ref, ...), custom_call_target="tpu_custom_call" | custom-call | flops 1761607680 | bytes 4404019 | tf_op jit(solution)/shard_map/pallas_call | solution.py:202
  78.3 0.6 collective-permute-start.2
  78.9 1.2 shard_map.68
  80.1 0.1 collective-permute-start.1
  80.3 1.2 shard_map.69.mine_ref
  81.5 0.0 copy-start.3
  81.5 0.0 collective-permute-done.2.arrived_ref
  81.5 0.1 shard_map.70
  81.6 0.1 collective-permute-start.3
  81.8 3.2 %collective-permute-start.4 = (bf16[4,4,96,128]{3,2,1,0:T(8,128)(2,1)S(1)}, bf16[4,4,96,128]{3,2,1,0:T(8,128)(2,1)S(1)}, u32[]{:S(2)}, u32[]{:S(2)}) collective-permute-start(bf16[4,4,96,128]{3,2,1,0:T(8,128)(2,1)S(1)} %get-tuple-element.26), channel_id=1, source_target_pairs={{0,30},{2,0},{4,2},{6,4},{8,6},{10,8},{12,10},{14,12},{16,14},{18,... | collective-permute-start | bytes 1179656 | tf_op jit(solution)/shard_map/ppermute | solution.py:211
  85.0 0.0 copy-done.3
  85.0 1.2 shard_map.67
  86.2 0.0 collective-permute-done.1.arrived_ref
  86.2 8.3 %collective-permute-done.3.low_ref = bf16[4,4,96,128]{3,2,1,0:T(8,128)(2,1)S(1)} collective-permute-done((bf16[4,4,96,128]{3,2,1,0:T(8,128)(2,1)S(1)}, bf16[4,4,96,128]{3,2,1,0:T(8,128)(2,1)S(1)}, u32[]{:S(2)}, u32[]{:S(2)}) %collective-permute-start.3) | collective-permute-done | bytes 393248 | tf_op jit(solution)/shard_map/ppermute | solution.py:210
  94.5 0.0 collective-permute-done.4.high_ref
  94.5 0.3 shard_map.71
  94.7 14.8 %all_to_all.16.results_ref = bf16[4,8,96,128]{3,2,1,0:T(8,128)(2,1)S(1)} all-to-all(bf16[4,8,96,128]{3,2,1,0:T(8,128)(2,1)S(1)} %shard_map.71), channel_id=1, replica_groups=mesh['groups'=2,'expert'=4,'z_0'=8,'z_1'=2,'core'=2] {'expert'}, dimensions={0} | all-to-all | bytes 1572864 | tf_op jit(solution)/shard_map/all_to_all | solution.py:221
  109.5 0.3 shard_map.72
  109.9 24.0 %all_to_all.17 = bf16[8,128,128]{2,1,0:T(8,128)(2,1)S(1)} all-to-all(bf16[8,128,128]{2,1,0:T(8,128)(2,1)S(1)} %shard_map.72), channel_id=1, replica_groups=mesh['groups'=2,'expert'=4,'z_0'=8,'z_1'=2,'core'=2] {'z_0'}, dimensions={0} | all-to-all | bytes 524288 | tf_op jit(solution)/shard_map/all_to_all | solution.py:223
  133.9 0.7 reduce_sum.12
Async XLA Ops:
  51.6 0.7 copy-start.2
  52.3 19.0 %copy-start.1 = (bf16[1,4096,448]{1,2,0:T(8,128)(2,1)S(1)}, bf16[1,4096,448]{1,2,0:T(8,128)(2,1)}, u32[]{:S(2)}) copy-start(bf16[1,4096,448]{1,2,0:T(8,128)(2,1)} %param.9) | copy-start | bytes 11010052
  71.3 3.9 %collective-permute-start = (bf16[4,16,96,128]{3,2,1,0:T(8,128)(2,1)S(1)}, bf16[4,16,96,128]{3,2,1,0:T(8,128)(2,1)S(1)}, u32[]{:S(2)}, u32[]{:S(2)}) collective-permute-start(bf16[4,16,96,128]{3,2,1,0:T(8,128)(2,1)S(1)} %all_to_all.15.x_ref), channel_id=1, source_target_pairs={{0,1},{1,0},{2,3},{3,2},{4,5},{5,4},{6,7},{7,6},{8,9},{9,8},{10,11... | collective-permute-start | bytes 4718600 | tf_op jit(solution)/shard_map/ppermute | solution.py:183
  71.3 3.9 %copy-start = (bf16[1,448,4096]{2,1,0:T(8,128)(2,1)S(1)}, bf16[1,448,4096]{2,1,0:T(8,128)(2,1)}, u32[]{:S(2)}) copy-start(bf16[1,448,4096]{2,1,0:T(8,128)(2,1)} %param.11) | copy-start | bytes 11010052
  78.3 3.2 %collective-permute-start.2 = (bf16[4,8,96,128]{3,2,1,0:T(8,128)(2,1)S(1)}, bf16[4,8,96,128]{3,2,1,0:T(8,128)(2,1)S(1)}, u32[]{:S(2)}, u32[]{:S(2)}) collective-permute-start(bf16[4,8,96,128]{3,2,1,0:T(8,128)(2,1)S(1)} %get-tuple-element.24), channel_id=1, source_target_pairs={{0,1},{1,0},{2,3},{3,2},{4,5},{5,4},{6,7},{7,6},{8,9},{9,8},{10,11... | collective-permute-start | bytes 2359304 | tf_op jit(solution)/shard_map/ppermute | solution.py:205
  80.1 6.0 %collective-permute-start.1 = (bf16[4,8,96,128]{3,2,1,0:T(8,128)(2,1)S(1)}, bf16[4,8,96,128]{3,2,1,0:T(8,128)(2,1)S(1)}, u32[]{:S(2)}, u32[]{:S(2)}) collective-permute-start(bf16[4,8,96,128]{3,2,1,0:T(8,128)(2,1)S(1)} %shard_map.68), channel_id=1, source_target_pairs={{0,1},{1,0},{2,3},{3,2},{4,5},{5,4},{6,7},{7,6},{8,9},{9,8},{10,11... | collective-permute-start | bytes 2359304 | tf_op jit(solution)/shard_map/ppermute | solution.py:215
  81.5 3.5 %copy-start.3 = (f32[128,2]{0,1:T(2,128)S(1)}, f32[128,2]{0,1:T(2,128)}, u32[]{:S(2)}) copy-start(f32[128,2]{0,1:T(2,128)} %param.8) | copy-start | bytes 3076
  81.6 12.8 %collective-permute-start.3 = (bf16[4,4,96,128]{3,2,1,0:T(8,128)(2,1)S(1)}, bf16[4,4,96,128]{3,2,1,0:T(8,128)(2,1)S(1)}, u32[]{:S(2)}, u32[]{:S(2)}) collective-permute-start(bf16[4,4,96,128]{3,2,1,0:T(8,128)(2,1)S(1)} %get-tuple-element.25), channel_id=1, source_target_pairs={{0,2},{2,4},{4,6},{6,8},{8,10},{10,12},{12,14},{14,16},{16,18},{18... | collective-permute-start | bytes 1179656 | tf_op jit(solution)/shard_map/ppermute | solution.py:210
  81.8 12.7 %collective-permute-start.4 = (bf16[4,4,96,128]{3,2,1,0:T(8,128)(2,1)S(1)}, bf16[4,4,96,128]{3,2,1,0:T(8,128)(2,1)S(1)}, u32[]{:S(2)}, u32[]{:S(2)}) collective-permute-start(bf16[4,4,96,128]{3,2,1,0:T(8,128)(2,1)S(1)} %get-tuple-element.26), channel_id=1, source_target_pairs={{0,30},{2,0},{4,2},{6,4},{8,6},{10,8},{12,10},{14,12},{16,14},{18,... | collective-permute-start | bytes 1179656 | tf_op jit(solution)/shard_map/ppermute | solution.py:211
